TPU v7x, 8 devices: a whole 2x2x1 slice. The times are simulated.
8 devices in a mesh: rep: 2 (over z, y), fsdp: 4 (over x, core).
Axes of the slice: x: 2, y: 2, z: 1, core: 2. Of those that a mesh axis runs over, the one named last changes fastest.
Arguments:
- tok_ids: int32 [8, 256], P(('rep', 'fsdp'))
- tok_labels: int32 [8, 256], P(('rep', 'fsdp'))
- tok_pos: int32 [8, 256], P(('rep', 'fsdp'))
- expert_idx: int32 [2, 8, 256, 2], P(None, ('rep', 'fsdp'))
- learn_rate: float32 [], replicated
- embedding: float32 [32000, 512], P('fsdp')
- w_query: float32 [2, 512, 512], P(None, 'fsdp')
- w_key: float32 [2, 512, 128], P(None, 'fsdp')
- w_value: float32 [2, 512, 128], P(None, 'fsdp')
- w_attn_out: float32 [2, 512, 512], P(None, 'fsdp')
- g_attn: float32 [2, 512], P(None, 'fsdp')
- g_mlp: float32 [2, 512], P(None, 'fsdp')
- w_router: float32 [2, 512, 8], P(None, 'fsdp')
- w_gate: float32 [2, 8, 512, 1792], P(None, None, 'fsdp')
- w_up: float32 [2, 8, 512, 1792], P(None, None, 'fsdp')
- w_down: float32 [2, 8, 1792, 512], P(None, None, 'fsdp')
- g_final: float32 [512], P('fsdp')
- w_head: float32 [512, 32000], P('fsdp')
Outputs:
- output 1: float32 [32000, 512], P('fsdp')
- output 2: float32 [2, 512, 512], P(None, 'fsdp')
- output 3: float32 [2, 512, 128], P(None, 'fsdp')
- output 4: float32 [2, 512, 128], P(None, 'fsdp')
- output 5: float32 [2, 512, 512], P(None, 'fsdp')
- output 6: float32 [2, 512], P(None, 'fsdp')
- output 7: float32 [2, 512], P(None, 'fsdp')
- output 8: float32 [2, 512, 8], P(None, 'fsdp')
- output 9: float32 [2, 8, 512, 1792], P(None, None, 'fsdp')
- output 10: float32 [2, 8, 512, 1792], P(None, None, 'fsdp')
- output 11: float32 [2, 8, 1792, 512], P(None, None, 'fsdp')
- output 12: float32 [512], P('fsdp')
- output 13: float32 [512, 32000], P('fsdp')
- output 14: float32 [], replicated
All inputs are finite; a program needn't handle non-finite values.
Results may differ from a plain program's by a relative error of at most 0.00855285.
Values are sent between devices in bfloat16 or wider.
A program may use at most 1 GiB of HBM per device.

v0:
```python
import functools
import jax
import jax.numpy as jnp
from jax import lax
from jax.sharding import PartitionSpec as P, NamedSharding

HEAD_DIM = 128
ROPE_THETA = 1000000.0
NORM_EPS = 1e-5
LAYER_DIMS = (0, 0, 0, 0, 0, 0, 0, 1, 1, 1)


def rms_norm(residual, gain):
    mean_sq = jnp.mean(residual * residual, axis=-1, keepdims=True)
    return (residual * lax.rsqrt(mean_sq + NORM_EPS) * gain).astype(jnp.bfloat16)


def rope_tables(positions):
    inv_freq = ROPE_THETA ** (-jnp.arange(0, HEAD_DIM, 2, dtype=jnp.float32) / HEAD_DIM)
    angle = positions.astype(jnp.float32)[..., None] * inv_freq
    return jnp.cos(angle)[:, :, None, :], jnp.sin(angle)[:, :, None, :]


def apply_rope(heads, cos_tab, sin_tab):
    half_dim = heads.shape[-1] // 2
    lower = heads[..., :half_dim]
    upper = heads[..., half_dim:]
    return jnp.concatenate([lower * cos_tab - upper * sin_tab, upper * cos_tab + lower * sin_tab], axis=-1)


def attention_block(normed, w_q, w_k, w_v, w_o, cos_tab, sin_tab):
    batch, length = normed.shape[0], normed.shape[1]
    q_heads = w_q.shape[1] // HEAD_DIM
    kv_heads = w_k.shape[1] // HEAD_DIM
    query = jnp.einsum('bsd,dh->bsh', normed, w_q, preferred_element_type=jnp.float32).reshape(batch, length, q_heads, HEAD_DIM)
    keyed = jnp.einsum('bsd,dh->bsh', normed, w_k, preferred_element_type=jnp.float32).reshape(batch, length, kv_heads, HEAD_DIM)
    values = jnp.einsum('bsd,dh->bsh', normed, w_v, preferred_element_type=jnp.float32).astype(jnp.bfloat16).reshape(batch, length, kv_heads, HEAD_DIM)
    query = apply_rope(query, cos_tab, sin_tab).astype(jnp.bfloat16).reshape(batch, length, kv_heads, q_heads // kv_heads, HEAD_DIM)
    keyed = apply_rope(keyed, cos_tab, sin_tab).astype(jnp.bfloat16)
    scores = jnp.einsum('bqkgd,bskd->bkgqs', query, keyed, preferred_element_type=jnp.float32) * HEAD_DIM ** -0.5
    causal = lax.broadcasted_iota(jnp.int32, (length, length), 0) >= lax.broadcasted_iota(jnp.int32, (length, length), 1)
    scores = jnp.where(causal, scores, -1e30)
    attn_probs = jax.nn.softmax(scores, axis=-1).astype(jnp.bfloat16)
    mixed = jnp.einsum('bkgqs,bskd->bqkgd', attn_probs, values, preferred_element_type=jnp.float32).astype(jnp.bfloat16)
    mixed = mixed.reshape(batch, length, q_heads * HEAD_DIM)
    return jnp.einsum('bsh,hd->bsd', mixed, w_o, preferred_element_type=jnp.float32)


def moe_block(normed, w_r, w_gate, w_up, w_down, chosen):
    batch, length, width = normed.shape
    experts = w_r.shape[1]
    flat = normed.reshape(batch * length, width)
    chosen_flat = chosen.reshape(batch * length, 2)
    logits = jnp.dot(flat, w_r, preferred_element_type=jnp.float32)
    gates = jax.nn.softmax(jnp.take_along_axis(logits, chosen_flat, axis=1), axis=-1)
    slot_expert = chosen_flat.reshape(-1)
    order = jnp.argsort(slot_expert, stable=True)
    sorted_in = jnp.take(flat, order // 2, axis=0)
    counts = jnp.bincount(slot_expert, length=experts).astype(jnp.int32)
    up_a = lax.ragged_dot(sorted_in, w_gate, counts, preferred_element_type=jnp.float32)
    up_b = lax.ragged_dot(sorted_in, w_up, counts, preferred_element_type=jnp.float32)
    hidden = (jax.nn.silu(up_a) * up_b).astype(jnp.bfloat16)
    down = lax.ragged_dot(hidden, w_down, counts, preferred_element_type=jnp.float32)
    unsorted = jnp.take(down, jnp.argsort(order), axis=0).reshape(batch * length, 2, width)
    mixed = jnp.sum(unsorted * gates[:, :, None], axis=1)
    return mixed.reshape(batch, length, width)


def layer_forward(residual, weights, cos_tab, sin_tab, chosen):
    w_q, w_k, w_v, w_o, g_a, g_m, w_r, w_gate, w_up, w_down = weights
    residual = residual + attention_block(rms_norm(residual, g_a), w_q, w_k, w_v, w_o, cos_tab, sin_tab)
    return residual + moe_block(rms_norm(residual, g_m), w_r, w_gate, w_up, w_down, chosen)


def head_loss(residual, gain, table, labels, token_total):
    final = rms_norm(residual, gain)
    logits = jnp.einsum('bsd,dv->bsv', final, table, preferred_element_type=jnp.float32)
    picked = jnp.take_along_axis(logits, labels[:, :, None], axis=-1)[:, :, 0]
    return jnp.sum(jax.nn.logsumexp(logits, axis=-1) - picked) / token_total


def gather_param(shard, axis):
    return lax.all_gather(shard.astype(jnp.bfloat16), 'fsdp', axis=axis, tiled=True)


def reduce_grad(grad_w, axis):
    owned = lax.psum_scatter(grad_w.astype(jnp.float32), 'fsdp', scatter_dimension=axis, tiled=True)
    return lax.psum(owned, 'rep')


def solution(mesh):
    device_count = mesh.shape['rep'] * mesh.shape['fsdp']
    batch_spec = P(('rep', 'fsdp'))
    layer_spec = P(None, 'fsdp')
    expert_spec = P(None, None, 'fsdp')
    param_specs = (P('fsdp'), layer_spec, layer_spec, layer_spec, layer_spec, layer_spec, layer_spec, layer_spec, expert_spec, expert_spec, expert_spec, P('fsdp'), P('fsdp'))
    in_specs = (batch_spec, batch_spec, batch_spec, P(None, ('rep', 'fsdp')), P()) + param_specs
    out_specs = param_specs + (P(),)

    def step(tok_ids, tok_labels, tok_pos, expert_idx, learn_rate, embedding, w_query, w_key, w_value, w_attn_out, g_attn, g_mlp, w_router, w_gate, w_up, w_down, g_final, w_head):
        layer_shards = (w_query, w_key, w_value, w_attn_out, g_attn, g_mlp, w_router, w_gate, w_up, w_down)
        num_layers = w_query.shape[0]
        token_total = tok_ids.shape[0] * tok_ids.shape[1] * device_count
        cos_tab, sin_tab = rope_tables(tok_pos)

        def gather_layer(layer):
            return tuple(gather_param(shard[layer], axis) for shard, axis in zip(layer_shards, LAYER_DIMS))

        def lookup(table):
            return jnp.take(table, tok_ids, axis=0).astype(jnp.float32)

        def head_part(residual_in, gain, table):
            return head_loss(residual_in, gain, table, tok_labels, token_total)

        residual, embed_vjp = jax.vjp(lookup, gather_param(embedding, 0))
        saved = []
        for layer in range(num_layers):
            saved.append(residual)
            residual = layer_forward(residual, gather_layer(layer), cos_tab, sin_tab, expert_idx[layer])

        local_loss, head_vjp = jax.vjp(head_part, residual, gather_param(g_final, 0), gather_param(w_head, 0))
        d_residual, d_final, d_head = head_vjp(jnp.ones((), jnp.float32))
        new_final = g_final - learn_rate * reduce_grad(d_final, 0)
        new_head = w_head - learn_rate * reduce_grad(d_head, 0)

        layer_grads = {}
        for layer in reversed(range(num_layers)):
            layer_part = functools.partial(layer_forward, cos_tab=cos_tab, sin_tab=sin_tab, chosen=expert_idx[layer])
            layer_out, layer_vjp = jax.vjp(layer_part, saved[layer], gather_layer(layer))
            d_residual, d_weights = layer_vjp(d_residual)
            layer_grads[layer] = [reduce_grad(grad_w, axis) for grad_w, axis in zip(d_weights, LAYER_DIMS)]

        (d_embed,) = embed_vjp(d_residual)
        new_embedding = embedding - learn_rate * reduce_grad(d_embed, 0)
        new_layers = tuple(shard - learn_rate * jnp.stack([layer_grads[layer][slot] for layer in range(num_layers)]) for slot, shard in enumerate(layer_shards))
        mean_loss = lax.psum(local_loss, ('rep', 'fsdp'))
        return (new_embedding,) + new_layers + (new_final, new_head, mean_loss)

    return jax.shard_map(step, mesh=mesh, in_specs=in_specs, out_specs=out_specs, check_vma=False)
```

profile of v0, /device:TPU:0, one launch (start us, length us, event | category | flops | bytes accessed | tf_op | source)
XLA Modules:
  0.0 5390.1 jit_solution(145132323320614939)
XLA Ops:
  306.9 24.4 all-gather.36.cloned.1.call-done
  350.9 75.6 %all-gather.42.cloned.1.call-done = bf16[1,8,512,1792]{2,3,1,0:T(8,128)(2,1)} async-done(((bf16[1,8,128,1792]{2,3,1,0:T(8,128)(2,1)}), bf16[1,8,512,1792]{2,3,1,0:T(8,128)(2,1)}) %all-gather.42.cloned.1.call-update) | async-done | bytes 14680080 | tf_op jit(solution)/shard_map/all_gather | solution.py:83
  446.0 75.0 %all-gather.34.cloned.1.call-done = bf16[1,8,512,1792]{2,3,1,0:T(8,128)(2,1)} async-done(((bf16[1,8,128,1792]{2,3,1,0:T(8,128)(2,1)}), bf16[1,8,512,1792]{2,3,1,0:T(8,128)(2,1)}) %all-gather.34.cloned.1.call-update) | async-done | bytes 14680080 | tf_op jit(solution)/shard_map/all_gather | solution.py:83
  540.6 75.6 %all-gather.40.cloned.1.call-done = bf16[1,8,512,1792]{2,3,1,0:T(8,128)(2,1)} async-done(((bf16[1,8,128,1792]{2,3,1,0:T(8,128)(2,1)}), bf16[1,8,512,1792]{2,3,1,0:T(8,128)(2,1)}) %all-gather.40.cloned.1.call-update) | async-done | bytes 14680080 | tf_op jit(solution)/shard_map/all_gather | solution.py:83
  677.0 135.1 %all-gather.30.cloned.1.call-done = bf16[32000,512]{1,0:T(8,128)(2,1)} async-done(((bf16[8000,512]{1,0:T(8,128)(2,1)}), bf16[32000,512]{1,0:T(8,128)(2,1)}) %all-gather.30.cloned.1.call-update) | async-done | bytes 32768016 | tf_op jit(solution)/shard_map/all_gather | solution.py:83
  968.3 39.5 all-gather.32.cloned.1.call-done
  1007.9 27.6 fusion.260
  1066.8 30.9 scatter_fusion.1
  1097.7 23.2 multiply_reduce_fusion.4
  1150.6 24.4 scatter_fusion.2
  1266.7 24.4 scatter_fusion.3
  1479.8 24.0 ragged-dot-none.4
  1609.0 33.3 fusion
  1655.5 31.8 scatter_fusion
  1687.3 37.7 convert_element_type.713
  1728.1 153.5 %reduce-scatter.43.cloned.1.call-done = f32[8,128,1792]{2,1,0:T(8,128)} async-done(((f32[8,512,1792]{2,1,0:T(8,128)}), f32[8,128,1792]{2,1,0:T(8,128)}) %reduce-scatter.43.cloned.1.call-update) | async-done | bytes 7340048 | tf_op jit(solution)/shard_map/reduce_scatter | solution.py:87
  1881.6 207.0 %reduce-scatter.49.cloned.1.call-done = f32[8,128,1792]{2,1,0:T(8,128)} async-done(((f32[8,512,1792]{2,1,0:T(8,128)}), f32[8,128,1792]{2,1,0:T(8,128)}) %reduce-scatter.49.cloned.1.call-update) | async-done | bytes 7340048 | tf_op jit(solution)/shard_map/reduce_scatter | solution.py:87
  2088.6 206.9 %reduce-scatter.45.cloned.1.call-done = f32[8,128,1792]{2,1,0:T(8,128)} async-done(((f32[8,512,1792]{2,1,0:T(8,128)}), f32[8,128,1792]{2,1,0:T(8,128)}) %reduce-scatter.45.cloned.1.call-update) | async-done | bytes 7340048 | tf_op jit(solution)/shard_map/reduce_scatter | solution.py:87
  2295.5 207.0 %reduce-scatter.53.cloned.1.call-done = f32[8,448,512]{2,1,0:T(8,128)} async-done(((f32[8,1792,512]{2,1,0:T(8,128)}), f32[8,448,512]{2,1,0:T(8,128)}) %reduce-scatter.53.cloned.1.call-update) | async-done | bytes 7340048 | tf_op jit(solution)/shard_map/reduce_scatter | solution.py:87
  2502.5 207.0 %reduce-scatter.51.cloned.1.call-done = f32[8,448,512]{2,1,0:T(8,128)} async-done(((f32[8,1792,512]{2,1,0:T(8,128)}), f32[8,448,512]{2,1,0:T(8,128)}) %reduce-scatter.51.cloned.1.call-update) | async-done | bytes 7340048 | tf_op jit(solution)/shard_map/reduce_scatter | solution.py:87
  2709.6 434.7 %reduce-scatter.57.cloned.1.call-done = f32[128,32000]{1,0:T(8,128)} async-done(((f32[512,32000]{1,0:T(8,128)}), f32[128,32000]{1,0:T(8,128)}) %reduce-scatter.57.cloned.1.call-update) | async-done | bytes 16384016
  3144.3 434.5 %reduce-scatter.55.cloned.1.call-done = f32[8000,512]{1,0:T(8,128)} async-done(((f32[32000,512]{1,0:T(8,128)}), f32[8000,512]{1,0:T(8,128)}) %reduce-scatter.55.cloned.1.call-update) | async-done | bytes 16384016
  3630.3 1675.3 %all-reduce.20.cloned.1.call-done = (f32[8000,512]{1,0:T(8,128)}, f32[1,128,512]{2,1,0:T(8,128)}, f32[1,128,512]{2,1,0:T(8,128)}, f32[1,128,128]{2,1,0:T(8,128)}...) async-done(((f32[8000,512]{1,0:T(8,128)}, ...) | async-done | bytes 78118928 | tf_op jit(solution)/shard_map/psum | solution.py:88
  5355.2 27.8 fusion.3
  (741 shorter events, 1134.0 us)
Async XLA Ops:
  51.8 374.7 %all-gather.42.cloned.1.call-start = ((), (), s32[]{:S(2)}) async-start(), calls=%async_computation.40 | async-start | bytes 18350080 | tf_op jit(solution)/shard_map/all_gather | solution.py:83
  52.3 468.7 %all-gather.34.cloned.1.call-start = ((), (), s32[]{:S(2)}) async-start(), calls=%async_computation.36 | async-start | bytes 18350080 | tf_op jit(solution)/shard_map/all_gather | solution.py:83
  71.2 545.0 %all-gather.40.cloned.1.call-start = ((), (), s32[]{:S(2)}) async-start(), calls=%async_computation.39 | async-start | bytes 18350080 | tf_op jit(solution)/shard_map/all_gather | solution.py:83
  71.8 740.3 %all-gather.30.cloned.1.call-start = ((), (), s32[]{:S(2)}) async-start(), calls=%async_computation.18 | async-start | bytes 40960000 | tf_op jit(solution)/shard_map/all_gather | solution.py:83
  81.0 926.9 %all-gather.32.cloned.1.call-start = ((), (), s32[]{:S(2)}) async-start(), calls=%async_computation.19 | async-start | bytes 40960000 | tf_op jit(solution)/shard_map/all_gather | solution.py:83
  90.2 1637.7 %reduce-scatter.29.cloned.1.call-start = ((), (), s32[]{:S(2)}) async-start(), calls=%async_computation.23 | async-start | bytes 327680 | tf_op jit(solution)/shard_map/reduce_scatter | solution.py:87
  1232.6 495.3 %reduce-scatter.33.cloned.1.call-start = ((), (), s32[]{:S(2)}) async-start(), calls=%async_computation.25 | async-start | bytes 327680 | tf_op jit(solution)/shard_map/reduce_scatter | solution.py:87
  1332.8 395.2 %reduce-scatter.27.cloned.1.call-start = ((), (), s32[]{:S(2)}) async-start(), calls=%async_computation.22 | async-start | bytes 327680 | tf_op jit(solution)/shard_map/reduce_scatter | solution.py:87
  1338.3 389.7 %reduce-scatter.31.cloned.1.call-start = ((), (), s32[]{:S(2)}) async-start(), calls=%async_computation.24 | async-start | bytes 327680 | tf_op jit(solution)/shard_map/reduce_scatter | solution.py:87
  1342.4 385.6 %reduce-scatter.37.cloned.1.call-start = ((), (), s32[]{:S(2)}) async-start(), calls=%async_computation.27 | async-start | bytes 1310720 | tf_op jit(solution)/shard_map/reduce_scatter | solution.py:87
  1344.7 383.3 %reduce-scatter.25.cloned.1.call-start = ((), (), s32[]{:S(2)}) async-start(), calls=%async_computation.21 | async-start | bytes 1310720 | tf_op jit(solution)/shard_map/reduce_scatter | solution.py:87
  1347.1 380.9 %reduce-scatter.35.cloned.1.call-start = ((), (), s32[]{:S(2)}) async-start(), calls=%async_computation.26 | async-start | bytes 1310720 | tf_op jit(solution)/shard_map/reduce_scatter | solution.py:87
  1349.4 378.7 %reduce-scatter.23.cloned.1.call-start = ((), (), s32[]{:S(2)}) async-start(), calls=%async_computation.20 | async-start | bytes 1310720 | tf_op jit(solution)/shard_map/reduce_scatter | solution.py:87
  1355.4 372.7 %reduce-scatter.47.cloned.1.call-start = ((), (), s32[]{:S(2)}) async-start(), calls=%async_computation.32 | async-start | bytes 36700160 | tf_op jit(solution)/shard_map/reduce_scatter | solution.py:87
  1396.3 485.3 %reduce-scatter.43.cloned.1.call-start = ((), (), s32[]{:S(2)}) async-start(), calls=%async_computation.30 | async-start | bytes 36700160 | tf_op jit(solution)/shard_map/reduce_scatter | solution.py:87
  1437.1 651.5 %reduce-scatter.49.cloned.1.call-start = ((), (), s32[]{:S(2)}) async-start(), calls=%async_computation.33 | async-start | bytes 36700160 | tf_op jit(solution)/shard_map/reduce_scatter | solution.py:87
  1479.8 815.7 %reduce-scatter.45.cloned.1.call-start = ((), (), s32[]{:S(2)}) async-start(), calls=%async_computation.31 | async-start | bytes 36700160 | tf_op jit(solution)/shard_map/reduce_scatter | solution.py:87
  1526.3 976.2 %reduce-scatter.53.cloned.1.call-start = ((), (), s32[]{:S(2)}) async-start(), calls=%async_computation.35 | async-start | bytes 36700160 | tf_op jit(solution)/shard_map/reduce_scatter | solution.py:87
  1567.1 1142.5 %reduce-scatter.51.cloned.1.call-start = ((), (), s32[]{:S(2)}) async-start(), calls=%async_computation.34 | async-start | bytes 36700160 | tf_op jit(solution)/shard_map/reduce_scatter | solution.py:87
  1608.0 1536.3 %reduce-scatter.57.cloned.1.call-start = ((), (), s32[]{:S(2)}) async-start(), calls=%async_computation.43 | async-start | bytes 81920000
  1642.4 1936.3 %reduce-scatter.55.cloned.1.call-start = ((), (), s32[]{:S(2)}) async-start(), calls=%async_computation.42 | async-start | bytes 81920000
  1725.1 1894.1 %reduce-scatter.41.cloned.1.call-start = ((), (), s32[]{:S(2)}) async-start(), calls=%async_computation.29 | async-start | bytes 20480 | tf_op jit(solution)/shard_map/reduce_scatter | solution.py:87
  1726.8 1892.4 %reduce-scatter.39.cloned.1.call-start = ((), (), s32[]{:S(2)}) async-start(), calls=%async_computation.28 | async-start | bytes 20480 | tf_op jit(solution)/shard_map/reduce_scatter | solution.py:87
  1727.6 3578.1 %all-reduce.20.cloned.1.call-start = ((), (), s32[]{:S(2)}) async-start(), calls=%async_computation.44 | async-start | bytes 156237824 | tf_op jit(solution)/shard_map/psum | solution.py:88
  (192 other events, 11917.8 us)
Sparse Core Ops, SparseCore 0:
  30.1 94.0 all-gather.37
  125.7 101.8 all-gather.43
  229.7 101.6 all-gather.35
  333.3 93.1 all-gather.41
  427.9 93.1 all-gather.33
  523.0 93.1 all-gather.39
  617.8 194.2 all-gather.29
  813.6 194.2 all-gather.31
  1332.9 14.5 reduce-scatter.32
  1349.9 14.5 reduce-scatter.26
  1366.7 14.5 reduce-scatter.30
  1383.8 19.2 reduce-scatter.36
  1405.4 19.2 reduce-scatter.24
  1426.9 19.2 reduce-scatter.34
  1448.5 19.2 reduce-scatter.22
  1470.2 204.4 reduce-scatter.46
  1677.1 204.4 reduce-scatter.42
  1884.1 204.4 reduce-scatter.48
  2091.0 204.4 reduce-scatter.44
  2298.1 204.4 reduce-scatter.52
  2505.1 204.4 reduce-scatter.50
  2712.2 432.0 reduce-scatter.56
  3146.7 431.9 reduce-scatter.54
  3616.0 1689.6 all-reduce.19
  (3 shorter events, 42.2 us)
where the time goes:
time: 5410 us; the launch traced here: 5390 us
  waiting for transfers between devices  3950 us (73%)
  other arithmetic  505 us (9%)
  Pallas kernels  300 us (6%)
  local copies, waits for them, and re-layouts  290 us (5%)
  blocking collectives  187 us (3%)
  matrix products  132 us (2%)
    psum x1, waiting for transfers between devices, reduce_grad(): return lax.psum(owned, 'rep')  1680 us
    reduce_scatter x16, waiting for transfers between devices, reduce_grad(): lax.psum_scatter(grad_w.astype(jnp.float32), 'fsdp', scatter_dimension=ax...  982 us
    unnamed x29, waiting for transfers between devices  871 us
    all_gather x8, waiting for transfers between devices, gather_param(): lax.all_gather(shard.astype(jnp.bfloat16), 'fsdp', axis=axis, tiled=True)  425 us
    another operation x12, Pallas kernels  207 us
    convert_element_type x7, other arithmetic, reduce_grad(): grad_w.astype(jnp.float32)  169 us
    all_gather x8, local copies, waits for them, and re-layouts, gather_param(): lax.all_gather(shard.astype(jnp.bfloat16), 'fsdp', axis=axis, tiled=True)  150 us
    all_gather x15, blocking collectives, gather_param(): lax.all_gather(shard.astype(jnp.bfloat16), 'fsdp', axis=axis, tiled=True)  145 us
  transfers between devices with their start and end apart: 27, of which 14 were waited for; matrix products, arithmetic and copies ran while one was open for 12% of the time, Pallas kernels for 5%

commit v1 on v0

v1 whole, which is shorter than its diff:
```python
import functools
import jax
import jax.numpy as jnp
from jax import lax
from jax.experimental import pallas as pl
from jax.experimental.pallas import tpu as pltpu
from jax.experimental.layout import Layout, with_layout_constraint
from jax.sharding import PartitionSpec as P

HEAD_DIM = 128
ROPE_THETA = 1000000.0
NORM_EPS = 1e-5
BF16 = jnp.bfloat16
F32 = jnp.float32
VMEM_LIMIT = 60 * 1024 * 1024
FSDP = 'fsdp'
REP = 'rep'


def rms_norm(residual, gain):
    mean_sq = jnp.mean(residual * residual, axis=-1, keepdims=True)
    return (residual * lax.rsqrt(mean_sq + NORM_EPS) * gain).astype(BF16)


def rope_tables(positions):
    inv_freq = ROPE_THETA ** (-jnp.arange(0, HEAD_DIM, 2, dtype=F32) / HEAD_DIM)
    angle = positions.astype(F32)[..., None] * inv_freq
    return jnp.cos(angle)[:, None, :], jnp.sin(angle)[:, None, :]


def apply_rope(heads, cos_tab, sin_tab):
    half_dim = heads.shape[-1] // 2
    lower = heads[..., :half_dim]
    upper = heads[..., half_dim:]
    return jnp.concatenate([lower * cos_tab - upper * sin_tab, upper * cos_tab + lower * sin_tab], axis=-1)


def attention_part(residual, w_q, w_k, w_v, w_o, gain, cos_tab, sin_tab):
    length = residual.shape[0]
    q_heads = w_q.shape[1] // HEAD_DIM
    normed = rms_norm(residual, gain)
    query = jnp.dot(normed, w_q, preferred_element_type=F32).reshape(length, q_heads, HEAD_DIM)
    keyed = jnp.dot(normed, w_k, preferred_element_type=F32).reshape(length, 1, HEAD_DIM)
    values = jnp.dot(normed, w_v, preferred_element_type=F32).astype(BF16)
    query = apply_rope(query, cos_tab, sin_tab).astype(BF16)
    keyed = apply_rope(keyed, cos_tab, sin_tab).astype(BF16)[:, 0]
    scores = jnp.einsum('qgd,sd->gqs', query, keyed, preferred_element_type=F32) * HEAD_DIM ** -0.5
    causal = lax.broadcasted_iota(jnp.int32, (length, length), 0) >= lax.broadcasted_iota(jnp.int32, (length, length), 1)
    scores = jnp.where(causal, scores, -1e30)
    attn_probs = jax.nn.softmax(scores, axis=-1).astype(BF16)
    mixed = jnp.einsum('gqs,sd->qgd', attn_probs, values, preferred_element_type=F32).astype(BF16)
    mixed = mixed.reshape(length, q_heads * HEAD_DIM)
    return residual + jnp.dot(mixed, w_o, preferred_element_type=F32)


def combine_weights(logits, chosen):
    rows = lax.broadcasted_iota(jnp.int32, logits.shape, 0)
    first = rows == chosen[:1]
    second = rows == chosen[1:]
    r0 = jnp.sum(jnp.where(first, logits, 0.0), axis=0, keepdims=True)
    r1 = jnp.sum(jnp.where(second, logits, 0.0), axis=0, keepdims=True)
    gates = jax.nn.softmax(jnp.concatenate([r0, r1], axis=0), axis=0)
    return jnp.where(first, gates[:1], 0.0) + jnp.where(second, gates[1:], 0.0)


def router_logits(normed, w_r):
    return lax.dot_general(w_r, normed, (((0,), (1,)), ((), ())), preferred_element_type=F32)


def router_part(residual, gain, w_r, chosen):
    normed = rms_norm(residual, gain)
    return normed, combine_weights(router_logits(normed, w_r), chosen)


def dot_nn(a, b):
    return jnp.dot(a, b, preferred_element_type=F32)


def dot_nt(a, b):
    return lax.dot_general(a, b, (((1,), (1,)), ((), ())), preferred_element_type=F32)


def params(steps):
    return pltpu.CompilerParams(dimension_semantics=("arbitrary",) * steps, vmem_limit_bytes=VMEM_LIMIT)


def permuted_columns(ref, me):
    return jnp.concatenate([ref[:, pl.ds(pl.multiple_of((me ^ k) * 128, 128), 128)] for k in range(4)], axis=1)


def pack_experts_kernel(sc, gate1, up1, gate2, up2, gate3, up3, down1, out1, out2, out3, out_down):
    rep = sc[2]
    out1[0, 0] = gate1[0, 0].astype(BF16)
    out1[1, 0] = up1[0, 0].astype(BF16)
    out2[0] = jnp.where(rep == 0, gate2[0, 0], up2[0, 0]).astype(BF16)
    out3[0] = jnp.where(rep == 0, gate3[0, 0], up3[0, 0]).astype(BF16)
    out_down[0] = down1[0, 0].astype(BF16)


def pack_experts(sc, layer, w_gate, w_up, w_down):
    def spec(own_core, own_half, matrix=None):
        def index(j, sc):
            step = j if matrix is None else jnp.where(sc[2] == matrix, j, 0)
            core = sc[0] if own_core else 1 - sc[0]
            return layer, 2 * step + core, 0, (sc[1] if own_half else 1 - sc[1])

        return pl.BlockSpec((1, 1, 128, 896), index)

    block = lambda j, sc: (j, 0, 0)
    return pl.pallas_call(
        pack_experts_kernel,
        grid_spec=pltpu.PrefetchScalarGridSpec(
            num_scalar_prefetch=1,
            grid=(4,),
            in_specs=[spec(False, True), spec(False, True), spec(True, False, 0), spec(True, False, 1), spec(False, False, 0), spec(False, False, 1),
                      pl.BlockSpec((1, 1, 448, 512), lambda j, sc: (layer, 2 * j + 1 - sc[0], 0, 0))],
            out_specs=[pl.BlockSpec((2, 1, 128, 896), lambda j, sc: (0, j, 0, 0)), pl.BlockSpec((1, 128, 896), block), pl.BlockSpec((1, 128, 896), block),
                       pl.BlockSpec((1, 448, 512), block)],
        ),
        out_shape=[
            jax.ShapeDtypeStruct((2, 4, 128, 896), BF16),
            jax.ShapeDtypeStruct((4, 128, 896), BF16),
            jax.ShapeDtypeStruct((4, 128, 896), BF16),
            jax.ShapeDtypeStruct((4, 448, 512), BF16),
        ],
        compiler_params=params(1),
        cost_estimate=pl.CostEstimate(flops=10_000_000, bytes_accessed=17_000_000, transcendentals=0),
    )(sc, w_gate, w_up, w_gate, w_up, w_gate, w_up, w_down)


def pack_head_kernel(sc, w_ref, out0, out1, out2, out3):
    core, x, rep = sc[0], sc[1], sc[2]

    def part(xx, cc):
        return w_ref[:, pl.ds(pl.multiple_of(head_start(xx, cc), 128), HEAD_COLS)].astype(BF16)

    out0[...] = part(x, core)
    out1[...] = part(x, 1 - core)

    @pl.when(pl.program_id(0) // (pl.num_programs(0) // 2) == rep)
    def _():
        out2[...] = part(1 - x, core)
        out3[...] = part(1 - x, 1 - core)


def pack_head(sc, w):
    rows, vocab = w.shape
    step = 16
    count = rows // step
    half = lambda i, sc: (jnp.clip(i - sc[2] * (count // 2), 0, count // 2 - 1), 0)
    return pl.pallas_call(
        pack_head_kernel,
        grid_spec=pltpu.PrefetchScalarGridSpec(
            num_scalar_prefetch=1,
            grid=(count,),
            in_specs=[pl.BlockSpec((step, vocab), lambda i, sc: (i, 0))],
            out_specs=[pl.BlockSpec((step, HEAD_COLS), lambda i, sc: (i, 0))] * 2 + [pl.BlockSpec((step, HEAD_COLS), half)] * 2,
        ),
        out_shape=[jax.ShapeDtypeStruct((rows, HEAD_COLS), BF16)] * 2 + [jax.ShapeDtypeStruct((rows // 2, HEAD_COLS), BF16)] * 2,
        compiler_params=params(1),
        cost_estimate=pl.CostEstimate(flops=10_000_000, bytes_accessed=23_000_000, transcendentals=0),
    )(sc, w)


def fill_expert_weights(sc, wg_own, wu_own, gu1, rx2, ry2, rx3, ry3, wd_own, wd1, wgu, wd):
    core, rep = sc[0], sc[2]
    wgu[0:128, 0:896] = wg_own[0, 0].astype(BF16)
    wgu[0:128, 896:1792] = wu_own[0, 0].astype(BF16)
    wgu[128:256, 0:896] = gu1[0, 0]
    wgu[128:256, 896:1792] = gu1[1, 0]
    by_x = pl.ds(pl.multiple_of(rep * 896, 128), 896)
    by_y = pl.ds(pl.multiple_of((1 - rep) * 896, 128), 896)
    wgu[256:384, by_x] = rx2[0]
    wgu[384:512, by_x] = rx3[0]
    wgu[256:384, by_y] = ry2[0]
    wgu[384:512, by_y] = ry3[0]
    wd[pl.ds(pl.multiple_of(core * 448, 64), 448), :] = wd_own[0, 0].astype(BF16)
    wd[pl.ds(pl.multiple_of((1 - core) * 448, 64), 448), :] = wd1[0]


def expert_weight_specs(layer):
    own = lambda j, t, sc: (layer, 2 * j + sc[0], 0, sc[1])
    return [
        pl.BlockSpec((1, 1, 128, 896), own),
        pl.BlockSpec((1, 1, 128, 896), own),
        pl.BlockSpec((2, 1, 128, 896), lambda j, t, sc: (0, j, 0, 0)),
        pl.BlockSpec((1, 128, 896), lambda j, t, sc: (j, 0, 0)),
        pl.BlockSpec((1, 128, 896), lambda j, t, sc: (j, 0, 0)),
        pl.BlockSpec((1, 128, 896), lambda j, t, sc: (j, 0, 0)),
        pl.BlockSpec((1, 128, 896), lambda j, t, sc: (j, 0, 0)),
        pl.BlockSpec((1, 1, 448, 512), lambda j, t, sc: (layer, 2 * j + sc[0], 0, 0)),
        pl.BlockSpec((1, 448, 512), lambda j, t, sc: (j, 0, 0)),
    ]


EXPERT_SCRATCH = [pltpu.VMEM((512, 1792), BF16), pltpu.VMEM((896, 512), BF16)]


def expert_column(comb, expert):
    lanes = lax.broadcasted_iota(jnp.int32, comb.shape, 1)
    return jnp.sum(jnp.where(lanes == expert, comb, 0.0), axis=1, keepdims=True)


def expert_forward_kernel(sc, b_ref, comb_ref, wg_own, wu_own, gu1, rx2, ry2, rx3, ry3, wd_own, wd1, out_ref, wgu, wd):
    j, t = pl.program_id(0), pl.program_id(1)
    tile = b_ref.shape[0]

    @pl.when(t == 0)
    def _():
        fill_expert_weights(sc, wg_own, wu_own, gu1, rx2, ry2, rx3, ry3, wd_own, wd1, wgu, wd)

    b = permuted_columns(b_ref, sc[3])
    both = dot_nn(b, wgu[...])
    gate, up = both[:, 0:896], both[:, 896:1792]
    hidden = (gate * jax.nn.sigmoid(gate) * up).astype(BF16)
    weighted = dot_nn(hidden, wd[...]) * expert_column(comb_ref[...], 2 * j + sc[0])
    rows = pl.ds(pl.multiple_of(t * tile, tile), tile)

    @pl.when(j == 0)
    def _():
        out_ref[rows, :] = weighted

    @pl.when(j != 0)
    def _():
        out_ref[rows, :] += weighted


def expert_forward(sc, layer, b_rows, comb, w_gate, w_up, pieces, w_down, wd1):
    rows, width = b_rows.shape
    tile = 1024
    return pl.pallas_call(
        expert_forward_kernel,
        grid_spec=pltpu.PrefetchScalarGridSpec(
            num_scalar_prefetch=1,
            grid=(4, rows // tile),
            in_specs=[
                pl.BlockSpec((tile, width), lambda j, t, sc: (t, 0)),
                pl.BlockSpec((tile, 8), lambda j, t, sc: (t, 0)),
            ] + expert_weight_specs(layer),
            out_specs=pl.BlockSpec((rows, width), lambda j, t, sc: (0, 0)),
            scratch_shapes=EXPERT_SCRATCH,
        ),
        out_shape=jax.ShapeDtypeStruct((rows, width), F32),
        compiler_params=params(2),
        cost_estimate=pl.CostEstimate(flops=11_300_000_000, bytes_accessed=20_000_000, transcendentals=3_700_000),
    )(sc, b_rows, comb, w_gate, w_up, *pieces, w_down, wd1)


SLOT_TILE = 256


def slot_gradients(b_sel, d_sel, weight, wgu, wd):
    both = dot_nn(b_sel, wgu[...])
    gate, up = both[:, 0:896], both[:, 896:1792]
    sig = jax.nn.sigmoid(gate)
    silu = gate * sig
    hidden = (silu * up).astype(BF16).astype(F32)
    d_hidden = dot_nt(d_sel, wd[...])
    d_weight = jnp.sum(hidden * d_hidden, axis=1, keepdims=True)
    d_hidden = (d_hidden * weight).astype(BF16).astype(F32)
    d_up = (d_hidden * silu).astype(BF16)
    d_gate = (d_hidden * up * (sig * (1.0 + gate * (1.0 - sig)))).astype(BF16)
    return (hidden * weight).astype(BF16), jnp.concatenate([d_gate, d_up], axis=1), d_weight


def load_tokens(rows_ref, b_ref, d_ref, me):
    rows_ref[:, 0:512] = permuted_columns(b_ref, me)
    rows_ref[:, 512:1024] = d_ref[...].astype(BF16)


def select_slots(rank_row, comb_row, m, tokens_ref):
    index = lax.broadcasted_iota(jnp.int32, (SLOT_TILE, rank_row.shape[1]), 0) + m * SLOT_TILE
    chosen = index == rank_row
    picked = dot_nn(jnp.where(chosen, 1.0, 0.0).astype(BF16), tokens_ref[...])
    weight = jnp.sum(jnp.where(chosen, comb_row, 0.0), axis=1, keepdims=True)
    return chosen, picked[:, 0:512], picked[:, 512:1024], weight


def slot_tiles(sc, group, expert):
    return (sc[4 + group * 8 + expert] + (SLOT_TILE - 1)) // SLOT_TILE


def expert_dgrad_kernel(sc, b_ref, d_ref, rank_ref, rank_col_ref, comb_ref, wg_own, wu_own, gu1, rx2, ry2, rx3, ry3, wd_own, wd1,
                        db_ref, wgu, wd, tokens_ref, db_acc, dw_acc):
    j = pl.program_id(0)
    core, rep, me = sc[0], sc[2], sc[3]
    expert = 2 * j + core

    @pl.when(j == 0)
    def _():
        load_tokens(tokens_ref, b_ref, d_ref, me)
        db_acc[...] = jnp.zeros_like(db_acc)
        dw_acc[...] = jnp.zeros_like(dw_acc)

    fill_expert_weights(sc, wg_own, wu_own, gu1, rx2, ry2, rx3, ry3, wd_own, wd1, wgu, wd)

    row = pl.ds(expert, 1)

    def slots(m, carry):
        chosen, b_sel, d_sel, weight = select_slots(rank_ref[0, row, :], comb_ref[row, :], m, tokens_ref)
        _, d_both, d_weight = slot_gradients(b_sel.astype(BF16), d_sel.astype(BF16), weight, wgu, wd)
        db = dot_nt(d_both, wgu[...])
        high = db.astype(BF16)
        rest = db - high.astype(F32)
        middle = rest.astype(BF16)
        low = (rest - middle.astype(F32)).astype(BF16)
        rank_all = rank_col_ref[0]
        lanes = lax.broadcasted_iota(jnp.int32, rank_all.shape, 1)
        rank_col = jnp.sum(jnp.where(lanes == expert, rank_all, 0), axis=1, keepdims=True)
        index = lax.broadcasted_iota(jnp.int32, (rank_all.shape[0], SLOT_TILE), 1) + m * SLOT_TILE
        spread = jnp.where(index == rank_col, 1.0, 0.0).astype(BF16)
        db_acc[...] += dot_nn(jnp.concatenate([spread] * 3, axis=1), jnp.concatenate([high, middle, low], axis=0))
        dw_acc[row, :] += jnp.sum(jnp.where(chosen, d_weight, 0.0), axis=0, keepdims=True)
        return carry

    lax.fori_loop(0, slot_tiles(sc, rep, expert), slots, 0)

    @pl.when(j == pl.num_programs(0) - 1)
    def _():
        for k in range(4):
            db_ref[:, pl.ds(pl.multiple_of((me ^ k) * 128, 128), 128)] = db_acc[:, k * 128:(k + 1) * 128]
        db_ref[:, 512:640] = dw_acc[...].T


def expert_dgrad(sc, layer, b_group, d_all, ranks, rank_cols, comb, w_gate, w_up, pieces, w_down, wd1):
    rows, width = b_group.shape
    return pl.pallas_call(
        expert_dgrad_kernel,
        grid_spec=pltpu.PrefetchScalarGridSpec(
            num_scalar_prefetch=1,
            grid=(4, 1),
            in_specs=[
                pl.BlockSpec((rows, width), lambda j, t, sc: (0, 0)),
                pl.BlockSpec((rows, width), lambda j, t, sc: (sc[2], 0)),
                pl.BlockSpec((1, 8, rows), lambda j, t, sc: (sc[2], 0, 0)),
                pl.BlockSpec((1, rows, 8), lambda j, t, sc: (sc[2], 0, 0)),
                pl.BlockSpec((8, rows), lambda j, t, sc: (0, 0)),
            ] + expert_weight_specs(layer),
            out_specs=pl.BlockSpec((rows, 640), lambda j, t, sc: (0, 0)),
            scratch_shapes=EXPERT_SCRATCH + [pltpu.VMEM((rows, 2 * width), BF16), pltpu.VMEM((rows, width), F32), pltpu.VMEM((128, rows), F32)],
        ),
        out_shape=jax.ShapeDtypeStruct((rows, 640), F32),
        compiler_params=params(2),
        cost_estimate=pl.CostEstimate(flops=15_000_000_000, bytes_accessed=25_000_000, transcendentals=2_000_000),
    )(sc, b_group, d_all, ranks, rank_cols, comb, w_gate, w_up, *pieces, w_down, wd1)


def expert_wgrad_kernel(sc, b_own, b_other, d_own, d_other, rank_ref, comb_own, comb_other,
                        wg_own, wu_own, gu1, rx2, ry2, rx3, ry3, wd_own, wd1,
                        own_ref, near_ref, far2_ref, far3_ref, down_own_ref, down_other_ref, wgu, wd, tokens_ref, comb_ref, down_acc):
    j, group = pl.program_id(0), pl.program_id(1)
    core, rep, me = sc[0], sc[2], sc[3]
    expert = 2 * j + core

    @pl.when((j == 0) & (group == 0))
    def _():
        load_tokens(tokens_ref.at[rep], b_own, d_own, me)
        load_tokens(tokens_ref.at[1 - rep], b_other, d_other, me)
        comb_ref[rep] = comb_own[...]
        comb_ref[1 - rep] = comb_other[...]

    @pl.when(group == 0)
    def _():
        fill_expert_weights(sc, wg_own, wu_own, gu1, rx2, ry2, rx3, ry3, wd_own, wd1, wgu, wd)
        for ref in (own_ref, near_ref, far2_ref, far3_ref, down_acc):
            ref[...] = jnp.zeros_like(ref)

    row = pl.ds(expert, 1)

    def slots(m, carry):
        _, b_sel, d_sel, weight = select_slots(rank_ref[0, row, :], comb_ref[group, row, :], m, tokens_ref.at[group])
        hidden, d_both, _ = slot_gradients(b_sel.astype(BF16), d_sel.astype(BF16), weight, wgu, wd)
        bt = b_sel.T.astype(BF16)
        dt = d_sel.T.astype(BF16)
        dw = dot_nn(bt[0:256], d_both)
        for matrix in range(2):
            cols = slice(matrix * 896, matrix * 896 + 896)
            own_ref[matrix, 0] += dw[0:128, cols]
            near_ref[matrix, 0] += dw[128:256, cols]
        dw = dot_nn(bt[256:512], jnp.where(rep == 0, d_both[:, 0:896], d_both[:, 896:1792]))
        far2_ref[0] += dw[0:128]
        far3_ref[0] += dw[128:256]
        down_acc[...] += dot_nn(dt, hidden)
        return carry

    lax.fori_loop(0, slot_tiles(sc, group, expert), slots, 0)

    @pl.when(group == 1)
    def _():
        down_t = down_acc[...].T
        lower, upper = down_t[0:448], down_t[448:896]

        @pl.when(core == 0)
        def _():
            down_own_ref[0] = lower
            down_other_ref[0] = upper

        @pl.when(core != 0)
        def _():
            down_own_ref[0] = upper
            down_other_ref[0] = lower


def expert_wgrad(sc, layer, b_own, b_other, d_all, ranks, comb_own, comb_other, w_gate, w_up, pieces, w_down, wd1):
    rows, width = b_own.shape
    once = pl.BlockSpec((rows, width), lambda j, g, t, sc: (0, 0))
    weights = [pl.BlockSpec(spec.block_shape, functools.partial(lambda index, j, g, t, sc: index(j, t, sc), spec.index_map)) for spec in expert_weight_specs(layer)]
    return pl.pallas_call(
        expert_wgrad_kernel,
        grid_spec=pltpu.PrefetchScalarGridSpec(
            num_scalar_prefetch=1,
            grid=(4, 2, 1),
            in_specs=[once] * 2 + [
                pl.BlockSpec((rows, width), lambda j, g, t, sc: (sc[2], 0)),
                pl.BlockSpec((rows, width), lambda j, g, t, sc: (1 - sc[2], 0)),
                pl.BlockSpec((1, 8, rows), lambda j, g, t, sc: (g, 0, 0)),
                pl.BlockSpec((8, rows), lambda j, g, t, sc: (0, 0)),
                pl.BlockSpec((8, rows), lambda j, g, t, sc: (0, 0)),
            ] + weights,
            out_specs=[
                pl.BlockSpec((2, 1, 128, 896), lambda j, g, t, sc: (0, j, 0, 0)),
                pl.BlockSpec((2, 1, 128, 896), lambda j, g, t, sc: (0, j, 0, 0)),
                pl.BlockSpec((1, 128, 896), lambda j, g, t, sc: (j, 0, 0)),
                pl.BlockSpec((1, 128, 896), lambda j, g, t, sc: (j, 0, 0)),
                pl.BlockSpec((1, 448, 512), lambda j, g, t, sc: (j, 0, 0)),
                pl.BlockSpec((1, 448, 512), lambda j, g, t, sc: (j, 0, 0)),
            ],
            scratch_shapes=EXPERT_SCRATCH + [pltpu.VMEM((2, rows, 2 * width), BF16), pltpu.VMEM((2, 8, rows), F32), pltpu.VMEM((512, 896), F32)],
        ),
        out_shape=[
            jax.ShapeDtypeStruct((2, 4, 128, 896), F32),
            jax.ShapeDtypeStruct((2, 4, 128, 896), F32),
            jax.ShapeDtypeStruct((4, 128, 896), F32),
            jax.ShapeDtypeStruct((4, 128, 896), F32),
            jax.ShapeDtypeStruct((4, 448, 512), F32),
            jax.ShapeDtypeStruct((4, 448, 512), F32),
        ],
        compiler_params=params(3),
        cost_estimate=pl.CostEstimate(flops=30_000_000_000, bytes_accessed=50_000_000, transcendentals=4_000_000),
    )(sc, b_own, b_other, d_all, d_all, ranks, comb_own, comb_other, w_gate, w_up, *pieces, w_down, wd1)


HEAD_COLS = 8192
HEAD_BLOCK = 1024
HEAD_TILE = 1024
HEAD_HALF = 16000
HEAD_SHIFT = 7808
HEAD_OVERLAP = HEAD_COLS - HEAD_SHIFT


def head_start(x, core):
    return x * HEAD_HALF + core * HEAD_SHIFT


def fill_head_weights(sc, own, p1, rx2, ry2, rx3, ry3, w):
    rep = sc[2]
    w[0:128, :] = own[...]
    w[128:256, :] = p1[...]
    for k, (rx, ry) in ((2, (rx2, ry2)), (3, (rx3, ry3))):
        w[pl.ds(pl.multiple_of(k * 128 + rep * 64, 64), 64), :] = rx[...]
        w[pl.ds(pl.multiple_of(k * 128 + (1 - rep) * 64, 64), 64), :] = ry[...]


def head_weight_specs():
    return [pl.BlockSpec((128, HEAD_BLOCK), lambda i, sc: (0, i))] * 2 + [pl.BlockSpec((64, HEAD_BLOCK), lambda i, sc: (0, i))] * 4


def head_stats_kernel(sc, x_ref, own, p1, rx2, ry2, rx3, ry3, out_ref, w, xp, m_acc, s_acc):
    i = pl.program_id(0)
    rows = x_ref.shape[0]

    @pl.when(i == 0)
    def _():
        xp[...] = permuted_columns(x_ref, sc[3])
        m_acc[...] = jnp.full((rows, 128), -1e30, F32)
        s_acc[...] = jnp.zeros((rows, 128), F32)

    fill_head_weights(sc, own, p1, rx2, ry2, rx3, ry3, w)
    first_new = jnp.where((sc[0] == 1) & (i == 0), HEAD_OVERLAP, 0)
    tiles = [slice(t, t + HEAD_TILE) for t in range(0, rows, HEAD_TILE)]

    def update(tile, logits):
        pieces = []
        for q in range(HEAD_BLOCK // 128):
            piece = logits[:, q * 128:(q + 1) * 128]
            if q * 128 < HEAD_OVERLAP:
                piece = piece + jnp.where(q * 128 >= first_new, 0.0, -1e30)
            pieces.append(piece)
        peak = m_acc[tile, :]
        top = functools.reduce(jnp.maximum, pieces, peak)
        total = s_acc[tile, :] * jnp.exp(peak - top)
        for piece in pieces:
            total = total + jnp.exp(piece - top)
        m_acc[tile, :] = top
        s_acc[tile, :] = total

    ahead = dot_nn(xp[tiles[0], :], w[...])
    for n, tile in enumerate(tiles):
        logits = ahead
        if n + 1 < len(tiles):
            ahead = dot_nn(xp[tiles[n + 1], :], w[...])
        update(tile, logits)

    @pl.when(i == pl.num_programs(0) - 1)
    def _():
        top = m_acc[...]
        highest = jnp.max(top, axis=1, keepdims=True)
        out_ref[:, 0:1] = highest
        out_ref[:, 1:2] = jnp.sum(s_acc[...] * jnp.exp(top - highest), axis=1, keepdims=True)


def head_stats(sc, x_rows, pieces):
    rows, width = x_rows.shape
    return pl.pallas_call(
        head_stats_kernel,
        grid_spec=pltpu.PrefetchScalarGridSpec(
            num_scalar_prefetch=1,
            grid=(HEAD_COLS // HEAD_BLOCK,),
            in_specs=[pl.BlockSpec((rows, width), lambda i, sc: (0, 0))] + head_weight_specs(),
            out_specs=pl.BlockSpec((rows, 8), lambda i, sc: (0, 0)),
            scratch_shapes=[pltpu.VMEM((width, HEAD_BLOCK), BF16), pltpu.VMEM((rows, width), BF16)] + [pltpu.VMEM((rows, 128), F32)] * 2,
        ),
        out_shape=jax.ShapeDtypeStruct((rows, 8), F32),
        compiler_params=params(1),
        cost_estimate=pl.CostEstimate(flops=17_000_000_000, bytes_accessed=25_000_000, transcendentals=16_800_000),
    )(sc, x_rows, *pieces)


def head_dx_kernel(sc, x_ref, label_ref, lse_ref, own, p1, rx2, ry2, rx3, ry3, dl_ref, dx_ref, picked_ref, w, xp, dx_acc, picked_acc):
    i = pl.program_id(0)
    core, x, rep, me = sc[0], sc[1], sc[2], sc[3]
    rows = x_ref.shape[0]
    half = rows // 2

    @pl.when(i == 0)
    def _():
        xp[...] = permuted_columns(x_ref, me)
        dx_acc[...] = jnp.zeros_like(dx_acc)
        picked_acc[...] = jnp.zeros_like(picked_acc)

    fill_head_weights(sc, own, p1, rx2, ry2, rx3, ry3, w)
    start = head_start(x, core) + i * HEAD_BLOCK
    first_new = jnp.where((core == 1) & (i == 0), HEAD_OVERLAP, 0)
    cols = lax.broadcasted_iota(jnp.int32, (HEAD_TILE, HEAD_BLOCK), 1)
    count = half // HEAD_TILE
    tiles = []
    for side in (rep, 1 - rep):
        for t in range(count):
            tiles.append(pl.ds(pl.multiple_of(side * half + t * HEAD_TILE, HEAD_TILE), HEAD_TILE))

    def gradient(tile, logits):
        hit = cols == label_ref[tile, :] - start
        prob = jnp.exp(logits - lse_ref[tile, :])
        picked = jnp.where(hit, logits, 0.0)
        picked_acc[...] += sum(jnp.where(q * 128 >= first_new, 1.0, 0.0) * jnp.sum(picked[:, q * 128:(q + 1) * 128].reshape(HEAD_TILE // 8, 8, 128), axis=0)
                               for q in range(HEAD_BLOCK // 128))
        d_logits = (jnp.where(hit, prob - 1.0, prob) * (1.0 / rows)).astype(BF16)
        dl_ref[tile, :] = d_logits
        return d_logits

    def project(n, d_logits):
        overlap = d_logits[:, 0:HEAD_OVERLAP]
        overlap = jnp.where(first_new == 0, overlap.astype(F32), 0.0).astype(BF16)
        masked = jnp.concatenate([overlap, d_logits[:, HEAD_OVERLAP:]], axis=1)
        dx_acc[n * HEAD_TILE:(n + 1) * HEAD_TILE, :] += dot_nt(masked, w[...])

    ahead = dot_nn(xp[tiles[0], :], w[...])
    for n, tile in enumerate(tiles):
        logits = ahead
        if n + 1 < len(tiles):
            ahead = dot_nn(xp[tiles[n + 1], :], w[...])
        d_logits = gradient(tile, logits)
        if n < count:
            project(n, d_logits)

    @pl.when(i == pl.num_programs(0) - 1)
    def _():
        for k in range(4):
            dx_ref[:, pl.ds(pl.multiple_of((me ^ k) * 128, 128), 128)] = dx_acc[:, k * 128:(k + 1) * 128]
        picked_ref[...] = picked_acc[...]


def head_dx(sc, x_rows, labels, lse, pieces):
    rows, width = x_rows.shape
    return pl.pallas_call(
        head_dx_kernel,
        grid_spec=pltpu.PrefetchScalarGridSpec(
            num_scalar_prefetch=1,
            grid=(HEAD_COLS // HEAD_BLOCK,),
            in_specs=[
                pl.BlockSpec((rows, width), lambda i, sc: (0, 0)),
                pl.BlockSpec((rows, 1), lambda i, sc: (0, 0)),
                pl.BlockSpec((rows, 1), lambda i, sc: (0, 0)),
            ] + head_weight_specs(),
            out_specs=[pl.BlockSpec((rows, HEAD_BLOCK), lambda i, sc: (0, i)), pl.BlockSpec((rows // 2, width), lambda i, sc: (0, 0)),
                       pl.BlockSpec((8, 128), lambda i, sc: (0, 0))],
            scratch_shapes=[pltpu.VMEM((width, HEAD_BLOCK), BF16), pltpu.VMEM((rows, width), BF16), pltpu.VMEM((rows // 2, width), F32),
                            pltpu.VMEM((8, 128), F32)],
        ),
        out_shape=[jax.ShapeDtypeStruct((rows, HEAD_COLS), BF16), jax.ShapeDtypeStruct((rows // 2, width), F32), jax.ShapeDtypeStruct((8, 128), F32)],
        compiler_params=params(1),
        cost_estimate=pl.CostEstimate(flops=26_000_000_000, bytes_accessed=60_000_000, transcendentals=16_800_000),
    )(sc, x_rows, labels, lse, *pieces)


def head_dw_kernel(sc, xt_ref, dl_ref, d0, d1, d2, d3, xt):
    @pl.when(pl.program_id(0) == 0)
    def _():
        me, rep = sc[3], sc[2]
        for k in range(2):
            xt[k * 128:(k + 1) * 128, :] = xt_ref[pl.ds(pl.multiple_of((me ^ k) * 128, 128), 128), :]
        for k in range(2, 4):
            xt[128 + k * 64:192 + k * 64, :] = xt_ref[pl.ds(pl.multiple_of((me ^ k) * 128 + rep * 64, 64), 64), :]

    dw = dot_nn(xt[...], dl_ref[...])
    d0[...] = dw[0:128]
    d1[...] = dw[128:256]
    d2[...] = dw[256:320]
    d3[...] = dw[320:384]


def head_dw(sc, x_cols, dl):
    width, rows = x_cols.shape
    block = 512
    return pl.pallas_call(
        head_dw_kernel,
        grid_spec=pltpu.PrefetchScalarGridSpec(
            num_scalar_prefetch=1,
            grid=(HEAD_COLS // block,),
            in_specs=[
                pl.BlockSpec((width, rows), lambda i, sc: (0, 0)),
                pl.BlockSpec((rows, block), lambda i, sc: (0, i)),
            ],
            out_specs=[pl.BlockSpec((128, block), lambda i, sc: (0, i))] * 2 + [pl.BlockSpec((64, block), lambda i, sc: (0, i))] * 2,
            scratch_shapes=[pltpu.VMEM((384, rows), BF16)],
        ),
        out_shape=[jax.ShapeDtypeStruct((128, HEAD_COLS), F32)] * 2 + [jax.ShapeDtypeStruct((64, HEAD_COLS), F32)] * 2,
        compiler_params=params(1),
        cost_estimate=pl.CostEstimate(flops=13_000_000_000, bytes_accessed=52_000_000, transcendentals=0),
    )(sc, x_cols, dl)


def update_gate_up_kernel(matrix, sc, rate, w_ref, own, p1, rx2, ry2, rx3, ry3, *rest):
    out_ref = rest[-1]
    s = pl.program_id(0)
    x, rep = sc[1], sc[2]
    lr = rate[0]
    near = pl.ds(pl.multiple_of(x * 896, 128), 896)
    far = pl.ds(pl.multiple_of((1 - x) * 896, 128), 896)

    def put(cols, grad):
        out_ref[0, 0, :, cols] = w_ref[0, 0, :, cols] - lr * grad

    @pl.when(s == 0)
    def _():
        put(near, own[0, 0])
        put(far, jnp.where(rep == matrix, rx2[0], ry2[0]))

    @pl.when(s == 1)
    def _():
        put(near, p1[0, 0])
        put(far, jnp.where(rep == matrix, rx3[0], ry3[0]))


def update_gate_up(sc, rate, layer, matrix, w, dgu, p1, rx2, ry2, rx3, ry3, previous=None):
    whole = lambda s, j, sc: (layer, 2 * j + jnp.where(s == 0, sc[0], 1 - sc[0]), 0, 0)
    early = lambda s, j: jnp.where(s == 0, j, 3)
    late = lambda s, j: jnp.where(s == 0, 0, j)
    in_specs = [
        pl.BlockSpec(memory_space=pltpu.SMEM),
        pl.BlockSpec((1, 1, 128, 1792), whole),
        pl.BlockSpec((1, 1, 128, 896), lambda s, j, sc: (matrix, early(s, j), 0, 0)),
        pl.BlockSpec((1, 1, 128, 896), lambda s, j, sc: (matrix, late(s, j), 0, 0)),
        pl.BlockSpec((1, 128, 896), lambda s, j, sc: (early(s, j), 0, 0)),
        pl.BlockSpec((1, 128, 896), lambda s, j, sc: (early(s, j), 0, 0)),
        pl.BlockSpec((1, 128, 896), lambda s, j, sc: (late(s, j), 0, 0)),
        pl.BlockSpec((1, 128, 896), lambda s, j, sc: (late(s, j), 0, 0)),
    ]
    args = [sc, rate, w, dgu, p1, rx2, ry2, rx3, ry3]
    aliases = {}
    if previous is not None:
        in_specs.append(pl.BlockSpec(memory_space=pl.ANY))
        aliases = {len(args): 0}
        args.append(previous)
    return pl.pallas_call(
        functools.partial(update_gate_up_kernel, matrix),
        grid_spec=pltpu.PrefetchScalarGridSpec(
            num_scalar_prefetch=1, grid=(2, 4), in_specs=in_specs, out_specs=pl.BlockSpec((1, 1, 128, 1792), whole),
        ),
        out_shape=jax.ShapeDtypeStruct(w.shape, F32),
        input_output_aliases=aliases,
        compiler_params=params(2),
        cost_estimate=pl.CostEstimate(flops=4_000_000, bytes_accessed=22_000_000, transcendentals=0),
        name="update_gate_up",
    )(*args)


def update_down_kernel(sc, rate, w_ref, own, p1, *rest):
    out_ref = rest[-1]
    s = pl.program_id(0)

    @pl.when(s == 0)
    def _():
        out_ref[0, 0] = w_ref[0, 0] - rate[0] * own[0]

    @pl.when(s == 1)
    def _():
        out_ref[0, 0] = w_ref[0, 0] - rate[0] * p1[0]


def update_down(sc, rate, layer, w, own, p1, previous=None):
    whole = lambda s, j, sc: (layer, 2 * j + jnp.where(s == 0, sc[0], 1 - sc[0]), 0, 0)
    in_specs = [
        pl.BlockSpec(memory_space=pltpu.SMEM),
        pl.BlockSpec((1, 1, 448, 512), whole),
        pl.BlockSpec((1, 448, 512), lambda s, j, sc: (jnp.where(s == 0, j, 3), 0, 0)),
        pl.BlockSpec((1, 448, 512), lambda s, j, sc: (jnp.where(s == 0, 0, j), 0, 0)),
    ]
    args = [sc, rate, w, own, p1]
    aliases = {}
    if previous is not None:
        in_specs.append(pl.BlockSpec(memory_space=pl.ANY))
        aliases = {len(args): 0}
        args.append(previous)
    return pl.pallas_call(
        update_down_kernel,
        grid_spec=pltpu.PrefetchScalarGridSpec(
            num_scalar_prefetch=1, grid=(2, 4), in_specs=in_specs, out_specs=pl.BlockSpec((1, 1, 448, 512), whole),
        ),
        out_shape=jax.ShapeDtypeStruct(w.shape, F32),
        input_output_aliases=aliases,
        compiler_params=params(2),
        cost_estimate=pl.CostEstimate(flops=4_000_000, bytes_accessed=22_000_000, transcendentals=0),
    )(*args)


def update_head_kernel(sc, rate, w_ref, own, p1, rx2, ry2, rx3, ry3, out_ref):
    half = pl.program_id(0) // (pl.num_programs(0) // 2)
    core, x, rep = sc[0], sc[1], sc[2]
    lr = rate[0]
    blocks = (
        (x, core, own[...]),
        (x, 1 - core, p1[...]),
        (1 - x, core, jnp.where(half == rep, rx2[...], ry2[...])),
        (1 - x, 1 - core, jnp.where(half == rep, rx3[...], ry3[...])),
    )
    for bx, bc, grad in blocks:
        cols = pl.ds(pl.multiple_of(head_start(bx, bc), 128), HEAD_COLS)
        out_ref[:, cols] = w_ref[:, cols] - lr * grad


def update_head(sc, rate, w, own, p1, rx2, ry2, rx3, ry3):
    rows, vocab = w.shape
    step = 16
    count = rows // step
    inner = count // 2
    return pl.pallas_call(
        update_head_kernel,
        grid_spec=pltpu.PrefetchScalarGridSpec(
            num_scalar_prefetch=1,
            grid=(count,),
            in_specs=[
                pl.BlockSpec(memory_space=pltpu.SMEM),
                pl.BlockSpec((step, vocab), lambda i, sc: (i, 0)),
                pl.BlockSpec((step, HEAD_COLS), lambda i, sc: (i, 0)),
                pl.BlockSpec((step, HEAD_COLS), lambda i, sc: (i, 0)),
            ] + [pl.BlockSpec((step, HEAD_COLS), lambda i, sc: (i % inner, 0))] * 4,
            out_specs=pl.BlockSpec((step, vocab), lambda i, sc: (i, 0)),
        ),
        out_shape=jax.ShapeDtypeStruct(w.shape, F32),
        compiler_params=params(1),
        cost_estimate=pl.CostEstimate(flops=8_000_000, bytes_accessed=50_000_000, transcendentals=0),
    )(sc, rate, w, own, p1, rx2, ry2, rx3, ry3)


def update_embedding_kernel(sc, rate, ids_ref, d_ref, w_ref, out_ref):
    rows = w_ref.shape[0]
    first = sc[3] * (pl.num_programs(0) * rows) + pl.program_id(0) * rows
    index = lax.broadcasted_iota(jnp.int32, (rows, ids_ref.shape[1]), 0) + first
    onehot = jnp.where(index == ids_ref[...], 1.0, 0.0).astype(BF16)
    out_ref[...] = w_ref[...] - rate[0] * dot_nn(onehot, d_ref[...])


def update_embedding(sc, rate, ids, d_rows, w):
    rows, width = w.shape
    step = 400
    tokens = d_rows.shape[0]
    return pl.pallas_call(
        update_embedding_kernel,
        grid_spec=pltpu.PrefetchScalarGridSpec(
            num_scalar_prefetch=1,
            grid=(rows // step,),
            in_specs=[
                pl.BlockSpec(memory_space=pltpu.SMEM),
                pl.BlockSpec((1, tokens), lambda i, sc: (0, 0)),
                pl.BlockSpec((tokens, width), lambda i, sc: (0, 0)),
                pl.BlockSpec((step, width), lambda i, sc: (i, 0)),
            ],
            out_specs=pl.BlockSpec((step, width), lambda i, sc: (i, 0)),
        ),
        out_shape=jax.ShapeDtypeStruct(w.shape, F32),
        compiler_params=params(1),
        cost_estimate=pl.CostEstimate(flops=17_000_000_000, bytes_accessed=35_000_000, transcendentals=0),
    )(sc, rate, ids, d_rows, w)


def peer_of(rep, me, other_rep, k):
    across = (me, me + 1 - 2 * (me % 2), (me + 2) % 4, 3 - me)[k]
    return (1 - rep if other_rep else rep), across


def exchange_kernel(both, in_ref, out_ref, send_sem, recv_sem):
    rep, me = lax.axis_index(REP), lax.axis_index(FSDP)
    slot = rep * 4 + me if both else me
    peers = [(other, k) for other in ((False, True) if both else (False,)) for k in range(4) if other or k]
    barrier = pltpu.get_barrier_semaphore()
    for other, k in peers:
        pl.semaphore_signal(barrier, inc=1, device_id=peer_of(rep, me, other, k), device_id_type=pl.DeviceIdType.MESH)
    pl.semaphore_wait(barrier, len(peers))
    copies = []
    for n, (other, k) in enumerate(peers):
        copy = pltpu.make_async_remote_copy(
            src_ref=in_ref, dst_ref=out_ref.at[slot], send_sem=send_sem.at[n], recv_sem=recv_sem.at[n],
            device_id=peer_of(rep, me, other, k), device_id_type=pl.DeviceIdType.MESH)
        copy.start()
        copies.append(copy)
    out_ref[slot] = in_ref[...]
    for copy in copies:
        copy.wait()


def exchange(value, both, collective_id):
    count = 8 if both else 4
    return pl.pallas_call(
        functools.partial(exchange_kernel, both),
        in_specs=[pl.BlockSpec(memory_space=pltpu.VMEM)],
        out_specs=pl.BlockSpec(memory_space=pltpu.VMEM),
        out_shape=jax.ShapeDtypeStruct((count,) + value.shape, value.dtype),
        scratch_shapes=[pltpu.SemaphoreType.DMA((count - 1,)), pltpu.SemaphoreType.DMA((count - 1,))],
        compiler_params=pltpu.CompilerParams(collective_id=collective_id, has_side_effects=True),
        cost_estimate=pl.CostEstimate(flops=1_000_000_000, bytes_accessed=100_000, transcendentals=0),
        name="exchange",
    )(value)


def row_major(value):
    return with_layout_constraint(value, Layout(major_to_minor=(0, 1)))


def to_peer(value, k):
    return lax.ppermute(value, FSDP, [(i, i ^ k) for i in range(4)])


def to_replica(value):
    return lax.ppermute(value, REP, [(0, 1), (1, 0)])


def solution(mesh):
    batch_spec = P((REP, FSDP))
    layer_spec = P(None, FSDP)
    expert_spec = P(None, None, FSDP)
    param_specs = (P(FSDP), layer_spec, layer_spec, layer_spec, layer_spec, layer_spec, layer_spec, layer_spec, expert_spec, expert_spec, expert_spec, P(FSDP), P(FSDP))
    in_specs = (batch_spec, batch_spec, batch_spec, P(None, (REP, FSDP)), P()) + param_specs
    out_specs = param_specs + (P(),)

    def train_step(tok_ids, tok_labels, tok_pos, expert_idx, learn_rate, embedding, w_query, w_key, w_value, w_attn_out, g_attn, g_mlp, w_router, w_gate, w_up, w_down, g_final, w_head):
        me = lax.axis_index(FSDP)
        rep = lax.axis_index(REP)
        core, x = me % 2, me // 2
        place = jnp.stack([core, x, rep, me]).astype(jnp.int32)
        rate = learn_rate.reshape(1)
        layers = w_query.shape[0]
        length = tok_ids.shape[1]
        tokens = 8 * length
        cos_tab, sin_tab = rope_tables(tok_pos[0])

        packed = jnp.concatenate([tok_ids, tok_labels, expert_idx[0, 0].T, expert_idx[1, 0].T, tok_ids, tok_labels], axis=0)
        packed = exchange(packed, True, 0)
        all_ids, all_labels = packed[:, 0].reshape(-1), packed[:, 1].reshape(-1, 1)
        group = tokens // 2
        chosen_all = [packed[:, 2 + 2 * layer:4 + 2 * layer].transpose(1, 0, 2).reshape(2, tokens) for layer in range(layers)]
        before = (lax.broadcasted_iota(jnp.int32, (group, group), 0) < lax.broadcasted_iota(jnp.int32, (group, group), 1)).astype(BF16)
        routes = []
        for layer in range(layers):
            experts = lax.broadcasted_iota(jnp.int32, (8, tokens), 0)
            mask = ((experts == chosen_all[layer][:1]) | (experts == chosen_all[layer][1:])).reshape(8, 2, group).transpose(1, 0, 2)
            rank = lax.dot_general(mask.astype(BF16), before, (((2,), (0,)), ((), ())), preferred_element_type=F32).astype(jnp.int32)
            rank = jnp.where(mask, rank, -1)
            counts = jnp.sum(mask.astype(jnp.int32), axis=2).reshape(-1)
            routes.append((jnp.concatenate([place, counts]), rank, rank.transpose(0, 2, 1)))
        sc = routes[0][0]

        def own_group(values, axis=0):
            return lax.dynamic_slice_in_dim(values, rep * group, group, axis)

        def relay(value, k):
            rx = to_peer(value, k)
            return rx, to_replica(rx)

        def near(value):
            return to_peer(value, 1)

        def send_experts(layer):
            gu1, mine2, mine3, wd1 = pack_experts(place, layer, w_gate, w_up, w_down)
            pieces = (near(gu1), *relay(mine2, 2), *relay(mine3, 3))
            return pieces, near(wd1)

        def send_head():
            own, p1, mine2, mine3 = pack_head(place, w_head)
            return [own, near(p1), *relay(mine2, 2), *relay(mine3, 3)]

        final_col = jnp.stack([g_final, jnp.zeros_like(g_final)])[:, :, None]
        small = jnp.concatenate([w_query, w_key, w_value, w_attn_out, w_router, g_attn[:, :, None], g_mlp[:, :, None], final_col], axis=2)
        whole = []
        for layer in range(layers):
            whole.append(lax.all_gather(small[layer].astype(BF16), FSDP, axis=0, tiled=True))
        cuts = (0, 512, 640, 768, 1280, 1288, 1289, 1290, 1291)

        def small_param(layer, slot):
            value = whole[layer][:, cuts[slot]:cuts[slot + 1]]
            return value[:, 0] if slot >= 5 else value

        local = own_group(all_ids) - me * embedding.shape[0]
        owned = (local >= 0) & (local < embedding.shape[0])
        rows = jnp.take(embedding, jnp.clip(local, 0, embedding.shape[0] - 1), axis=0)
        rows = jnp.where(owned[:, None], rows, 0.0).astype(BF16)
        residual = row_major(lax.psum_scatter(rows, FSDP, scatter_dimension=0, tiled=True).astype(F32))

        sent = [send_experts(layer) for layer in range(layers)]
        head_pieces = send_head()
        saved = []
        for layer in range(layers):
            w_q, w_k, w_v, w_o, w_r = (small_param(layer, slot) for slot in range(5))
            gain_a, gain_m = small_param(layer, 5), small_param(layer, 6)
            residual, attn_vjp = jax.vjp(functools.partial(attention_part, cos_tab=cos_tab, sin_tab=sin_tab), residual, w_q, w_k, w_v, w_o, gain_a)

            def routed(*values, layer=layer):
                return router_part(*values, chosen=expert_idx[layer, 0].T)

            (b, _), router_vjp = jax.vjp(routed, residual, gain_m, w_r)
            b_group = lax.all_gather(row_major(b), FSDP, axis=0, tiled=True)
            b_other = to_replica(b_group)
            other = lax.dynamic_slice_in_dim(chosen_all[layer], (1 - rep) * group, group, 1)
            comb = combine_weights(router_logits(b_group, w_r), own_group(chosen_all[layer], 1))
            comb_other = combine_weights(router_logits(b_other, w_r), other)
            pieces, wd1 = sent[layer]
            partial = expert_forward(sc, layer, b_group, comb.T, w_gate, w_up, pieces, w_down, wd1)
            residual = row_major(residual + lax.psum_scatter(partial, FSDP, scatter_dimension=0, tiled=True))
            saved.append((attn_vjp, router_vjp, b_group, b_other, comb, comb_other))

        final, final_vjp = jax.vjp(rms_norm, residual, small_param(0, 7))
        x_all = lax.all_gather(row_major(final), (REP, FSDP), axis=0, tiled=True)
        stats = head_stats(sc, x_all, head_pieces)
        stats = exchange(stats.T, False, 1)
        peak = jnp.max(stats[:, 0], axis=0)
        lse = peak + jnp.log(jnp.sum(stats[:, 1] * jnp.exp(stats[:, 0] - peak), axis=0))
        dl, dx, picked = head_dx(sc, x_all, all_labels, lse[:, None], head_pieces)
        dh0, dh1, dh2, dh3 = head_dw(sc, x_all.T, dl)
        d_final = row_major(lax.psum_scatter(dx, FSDP, scatter_dimension=0, tiled=True))
        d_residual, d_gain_final = final_vjp(d_final.astype(BF16))
        head_returns = [near(dh1), *relay(dh2, 2), *relay(dh3, 3)]
        new_head = update_head(sc, rate, w_head, dh0, *head_returns)

        small_grads = [None] * layers
        new_gate = new_up = new_down = None
        for layer in reversed(range(layers)):
            attn_vjp, router_vjp, b_group, b_other, comb, comb_other = saved[layer]
            d_all = lax.all_gather(row_major(d_residual), (REP, FSDP), axis=0, tiled=True)
            pieces, wd1 = sent[layer]
            scalars, ranks, rank_cols = routes[layer]
            db = expert_dgrad(scalars, layer, b_group, d_all, ranks, rank_cols, comb, w_gate, w_up, pieces, w_down, wd1)
            own, near1, far2, far3, down_own, down_other = expert_wgrad(scalars, layer, b_group, b_other, d_all, ranks, comb, comb_other, w_gate, w_up, pieces, w_down, wd1)
            returned = (*relay(far2, 2), *relay(far3, 3))
            gu1 = near(near1)
            down1 = near(down_other)
            new_gate = update_gate_up(sc, rate, layer, 0, w_gate, own, gu1, *returned, previous=new_gate)
            new_up = update_gate_up(sc, rate, layer, 1, w_up, own, gu1, *returned, previous=new_up)
            new_down = update_down(sc, rate, layer, w_down, down_own, down1, previous=new_down)
            db = row_major(lax.psum_scatter(db, FSDP, scatter_dimension=0, tiled=True))
            d_router_in, d_gain_m, d_wr = router_vjp((db[:, :512].astype(BF16), db[:, 512:520].T))
            d_residual = d_residual + d_router_in
            d_residual, d_wq, d_wk, d_wv, d_wo, d_gain_a = attn_vjp(d_residual)
            extra = d_gain_final if layer == 0 else jnp.full_like(d_gain_final, 0, F32) + jnp.sum(picked)
            grads = [d_wq, d_wk, d_wv, d_wo, d_wr, d_gain_a[:, None], d_gain_m[:, None], extra[:, None]]
            small_grads[layer] = jnp.concatenate([g.astype(F32) for g in grads], axis=1)

        d_rows = lax.all_gather(row_major(d_residual.astype(BF16)), (REP, FSDP), axis=0, tiled=True)
        new_embedding = update_embedding(sc, rate, all_ids[None, :], d_rows, embedding)

        small_grad = lax.psum_scatter(jnp.stack(small_grads), FSDP, scatter_dimension=1, tiled=True)
        small_grad = lax.psum(small_grad, REP)
        new_small = small - learn_rate * small_grad
        mean_loss = (jnp.sum(lse) - small_grad[1, 0, 1290] / 2) / tokens

        def new_param(slot):
            value = new_small[:, :, cuts[slot]:cuts[slot + 1]]
            return value[:, :, 0] if slot >= 5 else value

        return (new_embedding, new_param(0), new_param(1), new_param(2), new_param(3), new_param(5), new_param(6), new_param(4),
                new_gate, new_up, new_down, new_param(7)[0], new_head, mean_loss)


    return jax.shard_map(train_step, mesh=mesh, in_specs=in_specs, out_specs=out_specs, check_vma=False)
```

time: 5410 us -> 1280 us (0.24)
  waiting for transfers between devices: 3950 us -> 603 us
  other arithmetic: 505 us -> 38.7 us
  local copies, waits for them, and re-layouts: 290 us -> 73.3 us
  blocking collectives: 187 us -> 0 us
  Pallas kernels: 300 us -> 442 us
  matrix products: 132 us -> 55.9 us
    psum x1, waiting for transfers between devices: 1680 us -> 13.2 us  [train_step(): small_grad = lax.psum(small_grad, REP)]
    unnamed x29 -> x16, waiting for transfers between devices: 871 us -> 0.26 us
    reduce_scatter x16 -> x7, waiting for transfers between devices: 982 us -> 137 us  [the longest x2 50.4 us: train_step(): lax.psum_scatter(partial, FSDP, scatter_dimension=0, tiled=True)]
    pallas_call x0 -> x22, Pallas kernels: none -> 442 us  [the longest x2 83.7 us: expert_wgrad(): pl.pallas_call(expert_wgrad_kernel, grid_spec=pltpu.PrefetchScalarGridSpe...]
    ppermute x0 -> x36, waiting for transfers between devices: none -> 391 us  [the longest x22 309 us: to_peer(): return lax.ppermute(value, FSDP, [(i, i ^ k) for i in range(4)])]
    all_gather x8, waiting for transfers between devices: 425 us -> 62 us  [the longest x2 56.2 us: train_step(): lax.all_gather(row_major(d_residual), (REP, FSDP), axis=0, tiled=True)]
    another operation x12 -> x0, Pallas kernels: 207 us -> none
    convert_element_type x23 -> x13, other arithmetic: 201 us -> 7.04 us  [the longest x6 4.06 us: rms_norm(): return (residual * lax.rsqrt(mean_sq + NORM_EPS) * gain).astype(BF16)]
  transfers between devices with their start and end apart: 27 -> 52, of which waited for: 14 -> 27; matrix products, arithmetic and copies ran while one was open for 12% -> 5% of each run, Pallas kernels for 5% -> 22%
where the time goes in v1:
time: 1280 us; the launch traced here: 1260 us
  waiting for transfers between devices  603 us (47%)
  Pallas kernels  442 us (35%)
  local copies, waits for them, and re-layouts  73.3 us (6%)
  matrix products  55.9 us (4%)
  other arithmetic  38.7 us (3%)
  starting transfers between devices  30.3 us (2%)
  between operations  20.2 us (2%)
    ppermute x22, waiting for transfers between devices, to_peer(): return lax.ppermute(value, FSDP, [(i, i ^ k) for i in range(4)])  309 us
    pallas_call x2, Pallas kernels, expert_wgrad(): pl.pallas_call(expert_wgrad_kernel, grid_spec=pltpu.PrefetchScalarGridSpe...  83.7 us
    ppermute x14, waiting for transfers between devices, to_replica(): return lax.ppermute(value, REP, [(0, 1), (1, 0)])  81.9 us
    pallas_call x2, Pallas kernels, expert_dgrad(): pl.pallas_call(expert_dgrad_kernel, grid_spec=pltpu.PrefetchScalarGridSpe...  57.7 us
    all_gather x2, waiting for transfers between devices, train_step(): lax.all_gather(row_major(d_residual), (REP, FSDP), axis=0, tiled=True)  56.2 us
    reduce_scatter x2, waiting for transfers between devices, train_step(): lax.psum_scatter(partial, FSDP, scatter_dimension=0, tiled=True)  50.4 us
    pallas_call x1, Pallas kernels, head_dx(): pl.pallas_call(head_dx_kernel, grid_spec=pltpu.PrefetchScalarGridSpec(num...  46.7 us
    pallas_call x4, Pallas kernels, update_gate_up(): pl.pallas_call(functools.partial(update_gate_up_kernel, matrix), grid_spe...  45 us
  transfers between devices with their start and end apart: 52, of which 27 were waited for; matrix products, arithmetic and copies ran while one was open for 5% of the time, Pallas kernels for 22%

profile of v1, /device:TPU:0, one launch (start us, length us, event | category | flops | bytes accessed | tf_op | source)
XLA Modules:
  0.0 1263.0 jit_solution(15300708523048728902)
XLA Ops:
  169.4 24.6 %reduce-scatter.10.cloned.1.call-done = f32[256,512]{1,0:T(8,128)} async-done(((f32[1024,512]{1,0:T(8,128)}), f32[256,512]{1,0:T(8,128)}) %reduce-scatter.10.cloned.1.call-update) | async-done | bytes 524304 | tf_op jit(solution)/shard_map/reduce_scatter | solution.py:948
  213.1 21.8 %collective-permute-done.7.rx2 = bf16[4,128,896]{2,1,0:T(8,128)(2,1)S(1)} collective-permute-done((bf16[4,128,896]{2,1,0:T(8,128)(2,1)}, bf16[4,128,896]{2,1,0:T(8,128)(2,1)S(1)}, u32[]{:S(2)}, u32[]{:S(2)}) %collective-permute-start.7) | collective-permute-done | bytes 917536 | tf_op jit(solution)/shard_map/ppermute | solution.py:851
  296.1 25.7 %reduce-scatter.12.cloned.1.call-done = f32[256,512]{1,0:T(8,128)} async-done(((f32[1024,512]{1,0:T(8,128)}), f32[256,512]{1,0:T(8,128)}) %reduce-scatter.12.cloned.1.call-update) | async-done | bytes 524304 | tf_op jit(solution)/shard_map/reduce_scatter | solution.py:948
  337.6 29.8 %collective-permute-done.13.rx2 = bf16[64,8192]{1,0:T(8,128)(2,1)} collective-permute-done((bf16[64,8192]{1,0:T(8,128)(2,1)}, bf16[64,8192]{1,0:T(8,128)(2,1)}, u32[]{:S(2)}, u32[]{:S(2)}) %collective-permute-start.13) | collective-permute-done | bytes 1048608 | tf_op jit(solution)/shard_map/ppermute | solution.py:851
  393.8 19.4 %collective-permute-done.16.ry3 = bf16[64,8192]{1,0:T(8,128)(2,1)} collective-permute-done((bf16[64,8192]{1,0:T(8,128)(2,1)}, bf16[64,8192]{1,0:T(8,128)(2,1)}, u32[]{:S(2)}, u32[]{:S(2)}) %collective-permute-start.16) | collective-permute-done | bytes 1048608 | tf_op jit(solution)/shard_map/ppermute | solution.py:855
  413.1 30.8 %shard_map.286 = f32[2048,8]{1,0:T(8,128)} custom-call(s32[20]{0:T(128)} %concatenate.70.sc, bf16[2048,512]{1,0:T(8,128)(2,1)} %copy.127.x_ref, bf16[128,8192]{1,0:T(8,128)(2,1)} %get-tuple-element.53.own, bf16[128,8192]{1,0:T(8,128)(2,1)} %collective-permute-done.12.p1, bf16[64,8192]{1,0:T(8,128)(2,1)} %collective-permute-done.13.rx2, ...), custom_call_target="tpu_custom_call" | custom-call | flops 16999999488 | bytes 25000000 | tf_op jit(solution)/shard_map/pallas_call | solution.py:514
  456.1 46.7 %shard_map.287 = (bf16[2048,8192]{1,0:T(8,128)(2,1)}, f32[1024,512]{1,0:T(8,128)}, f32[8,128]{1,0:T(8,128)}) custom-call(s32[20]{0:T(128)} %concatenate.70.sc, bf16[2048,512]{1,0:T(8,128)(2,1)} %copy.127.x_ref, s32[2048,1]{1,0:T(8,128)} %copy.128.label_ref, f32[2048,1]{1,0:T(8,128)} %copy.129.lse_ref, bf16[128,8192]{1,0:T(8,128)(2,1)} %get-tuple-element.53.own, ...), custom_call_target="tpu_custom_call" | custom-call | flops 25999998976 | bytes 60000000 | tf_op jit(solution)/shard_map/pallas_call | solution.py:585
  502.9 26.1 %reduce-scatter.14.cloned.1.call-done = f32[256,512]{1,0:T(8,128)} async-done(((f32[1024,512]{1,0:T(8,128)}), f32[256,512]{1,0:T(8,128)}) %reduce-scatter.14.cloned.1.call-update) | async-done | bytes 524304 | tf_op jit(solution)/shard_map/reduce_scatter | solution.py:959
  536.7 27.3 %all-gather.17.cloned.1.call-done.d_ref.d_own.d_other = f32[2048,512]{1,0:T(8,128)} async-done(((f32[256,512]{1,0:T(8,128)}), f32[2048,512]{1,0:T(8,128)}) %all-gather.17.cloned.1.call-update) | async-done | bytes 4194320 | tf_op jit(solution)/shard_map/all_gather | solution.py:968
  564.0 27.2 %shard_map.288 = f32[1024,640]{1,0:T(8,128)} custom-call(s32[20]{0:T(128)} %concatenate.82.sc, bf16[1024,512]{1,0:T(8,128)(2,1)} %all-gather.13.cloned.1.call-done.b_ref.b_own, f32[2048,512]{1,0:T(8,128)} %all-gather.17.cloned.1.call-done.d_ref.d_own.d_other, s32[2,8,1024]{2,1,0:T(8,128)} %get-tuple-element.210.rank_ref, s32[2,1024,8]{2,1,0:T(8,128)} %copy.130.rank_col_ref, ...), custom_call_target="tpu_custom_call" | custom-call | flops 15000000512 | bytes 25000000 | tf_op jit(solution)/shard_map/pallas_call | solution.py:327
  593.2 27.2 %reduce-scatter.16.cloned.1.call-done = f32[256,640]{1,0:T(8,128)} async-done(((f32[1024,640]{1,0:T(8,128)}), f32[256,640]{1,0:T(8,128)}) %reduce-scatter.16.cloned.1.call-update) | async-done | bytes 655376 | tf_op jit(solution)/shard_map/reduce_scatter | solution.py:979
  638.9 28.9 %all-gather.19.cloned.1.call-done.d_ref.d_own.d_other = f32[2048,512]{1,0:T(8,128)} async-done(((f32[256,512]{1,0:T(8,128)}), f32[2048,512]{1,0:T(8,128)}) %all-gather.19.cloned.1.call-update) | async-done | bytes 4194320 | tf_op jit(solution)/shard_map/all_gather | solution.py:968
  667.9 30.5 %shard_map.289 = f32[1024,640]{1,0:T(8,128)} custom-call(s32[20]{0:T(128)} %concatenate.70.sc, bf16[1024,512]{1,0:T(8,128)(2,1)} %all-gather.11.cloned.1.call-done.b_ref.b_own, f32[2048,512]{1,0:T(8,128)} %all-gather.19.cloned.1.call-done.d_ref.d_own.d_other, s32[2,8,1024]{2,1,0:T(8,128)} %get-tuple-element.208.rank_ref, s32[2,1024,8]{2,1,0:T(8,128)} %copy.137.rank_col_ref, ...), custom_call_target="tpu_custom_call" | custom-call | flops 15000000512 | bytes 25000000 | tf_op jit(solution)/shard_map/pallas_call | solution.py:327
  770.9 28.4 %shard_map.295 = (f32[128,8192]{1,0:T(8,128)}, f32[128,8192]{1,0:T(8,128)}, f32[64,8192]{1,0:T(8,128)}, f32[64,8192]{1,0:T(8,128)}) custom-call(s32[20]{0:T(128)} %concatenate.70.sc, bf16[512,2048]{1,0:T(8,128)(2,1)} %bitcast.349, bf16[2048,8192]{1,0:T(8,128)(2,1)} %get-tuple-element.71.dl_ref), custom_call_target="tpu_custom_call" | custom-call | flops 12999999488 | bytes 52000000 | tf_op jit(solution)/shard_map/pallas_call | solution.py:625
  800.5 23.1 %collective-permute-done.23.b_other = bf16[1024,512]{1,0:T(8,128)(2,1)S(1)} collective-permute-done((bf16[1024,512]{1,0:T(8,128)(2,1)S(1)}, bf16[1024,512]{1,0:T(8,128)(2,1)S(1)}, u32[]{:S(2)}, u32[]{:S(2)}) %collective-permute-start.23) | collective-permute-done | bytes 1048608 | tf_op jit(solution)/shard_map/ppermute | solution.py:855
  825.5 35.3 %collective-permute-done.32.rx2 = f32[64,8192]{1,0:T(8,128)} collective-permute-done((f32[64,8192]{1,0:T(8,128)}, f32[64,8192]{1,0:T(8,128)}, u32[]{:S(2)}, u32[]{:S(2)}) %collective-permute-start.32) | collective-permute-done | bytes 2097184 | tf_op jit(solution)/shard_map/ppermute | solution.py:851
  862.1 40.7 %shard_map.292 = (f32[2,4,128,896]{3,2,1,0:T(8,128)}, f32[2,4,128,896]{3,2,1,0:T(8,128)}, f32[4,128,896]{2,1,0:T(8,128)}, f32[4,128,896]{2,1,0:T(8,128)}, f32[4,...) custom-call(s32[20]{0:T(128)} %concatenate.82.sc, bf16[1024,512]{1,0:T(8,128)(2,1)} %all-gather.13.cloned.1.call-done.b_ref.b_own, ...), custom_call_target="tpu_custom_call" | custom-call | flops 30000001024 | bytes 50000000 | tf_op jit(solution)/shard_map/pallas_call | solution.py:408
  909.0 36.9 %collective-permute-done.25.rx2 = f32[4,128,896]{2,1,0:T(8,128)S(1)} collective-permute-done((f32[4,128,896]{2,1,0:T(8,128)}, f32[4,128,896]{2,1,0:T(8,128)S(1)}, u32[]{:S(2)}, u32[]{:S(2)}) %collective-permute-start.25) | collective-permute-done | bytes 1835040 | tf_op jit(solution)/shard_map/ppermute | solution.py:851
  946.6 35.4 %collective-permute-done.27.rx3 = f32[4,128,896]{2,1,0:T(8,128)} collective-permute-done((f32[4,128,896]{2,1,0:T(8,128)}, f32[4,128,896]{2,1,0:T(8,128)}, u32[]{:S(2)}, u32[]{:S(2)}) %collective-permute-start.27) | collective-permute-done | bytes 1835040 | tf_op jit(solution)/shard_map/ppermute | solution.py:851
  984.3 43.0 %shard_map.291 = (f32[2,4,128,896]{3,2,1,0:T(8,128)}, f32[2,4,128,896]{3,2,1,0:T(8,128)}, f32[4,128,896]{2,1,0:T(8,128)}, f32[4,128,896]{2,1,0:T(8,128)}, f32[4,...) custom-call(s32[20]{0:T(128)} %concatenate.70.sc, bf16[1024,512]{1,0:T(8,128)(2,1)} %all-gather.11.cloned.1.call-done.b_ref.b_own, ...), custom_call_target="tpu_custom_call" | custom-call | flops 30000001024 | bytes 50000000 | tf_op jit(solution)/shard_map/pallas_call | solution.py:408
  1034.8 44.1 %collective-permute-done.19.rx2 = f32[4,128,896]{2,1,0:T(8,128)} collective-permute-done((f32[4,128,896]{2,1,0:T(8,128)}, f32[4,128,896]{2,1,0:T(8,128)}, u32[]{:S(2)}, u32[]{:S(2)}) %collective-permute-start.19) | collective-permute-done | bytes 1835040 | tf_op jit(solution)/shard_map/ppermute | solution.py:851
  1079.0 38.2 %collective-permute-done.21.rx3 = f32[4,128,896]{2,1,0:T(8,128)S(1)} collective-permute-done((f32[4,128,896]{2,1,0:T(8,128)}, f32[4,128,896]{2,1,0:T(8,128)S(1)}, u32[]{:S(2)}, u32[]{:S(2)}) %collective-permute-start.21) | collective-permute-done | bytes 1835040 | tf_op jit(solution)/shard_map/ppermute | solution.py:851
  1117.9 19.8 %shard_map.296 = f32[128,32000]{1,0:T(8,128)} custom-call(s32[20]{0:T(128)} %concatenate.70.sc, f32[1]{0:T(128)} %bitcast.330.rate, f32[128,32000]{1,0:T(8,128)} %w_ref.17, f32[128,8192]{1,0:T(8,128)} %get-tuple-element.72.own, f32[128,8192]{1,0:T(8,128)} %collective-permute-done.31.p1, f32[64,8192]{1,0:T(8,128)} %collective-permute-done.32.rx2, ...), custom_call_target="tpu_custom_call" | custom-call | flops 8000000 | bytes 50000000 | tf_op jit(solution)/shard_map/pallas_call | solution.py:757
  1203.9 28.5 %shard_map.290 = f32[8000,512]{1,0:T(8,128)} custom-call(s32[20]{0:T(128)} %concatenate.70.sc, f32[1]{0:T(128)} %bitcast.323.rate, s32[1,2048]{1,0:T(1,128)} %bitcast.439, bf16[2048,512]{1,0:T(8,128)(2,1)} %all-gather.21.cloned.1.call-done.d_ref, f32[8000,512]{1,0:T(8,128)} %w_ref.10), custom_call_target="tpu_custom_call" | custom-call | flops 16999999488 | bytes 35000000 | tf_op jit(solution)/shard_map/pallas_call | solution.py:788
  (635 shorter events, 503.4 us)
Async XLA Ops:
  65.3 103.2 %all-gather.25.cloned.1.call-start = ((), (), s32[]{:S(2)}) async-start(), calls=%async_computation.22 | async-start | bytes 1658880 | tf_op jit(solution)/shard_map/all_gather | solution.py:916
  82.7 111.3 %reduce-scatter.10.cloned.1.call-start = ((), (), s32[]{:S(2)}) async-start(), calls=%async_computation.9 | async-start | bytes 2621440 | tf_op jit(solution)/shard_map/reduce_scatter | solution.py:948
  168.2 87.1 %all-gather.13.cloned.1.call-start = ((), (), s32[]{:S(2)}) async-start(), calls=%async_computation.10 | async-start | bytes 1310720 | tf_op jit(solution)/shard_map/all_gather | solution.py:941
  202.2 119.6 %reduce-scatter.12.cloned.1.call-start = ((), (), s32[]{:S(2)}) async-start(), calls=%async_computation.11 | async-start | bytes 2621440 | tf_op jit(solution)/shard_map/reduce_scatter | solution.py:948
  296.0 93.8 %all-gather.15.cloned.1.call-start = ((), (), s32[]{:S(2)}) async-start(), calls=%async_computation.12 | async-start | bytes 2359296 | tf_op jit(solution)/shard_map/all_gather | solution.py:952
  324.0 205.0 %reduce-scatter.14.cloned.1.call-start = ((), (), s32[]{:S(2)}) async-start(), calls=%async_computation.13 | async-start | bytes 2621440 | tf_op jit(solution)/shard_map/reduce_scatter | solution.py:959
  336.5 76.7 %collective-permute-start.12 = (bf16[128,8192]{1,0:T(8,128)(2,1)}, bf16[128,8192]{1,0:T(8,128)(2,1)}, u32[]{:S(2)}, u32[]{:S(2)}) collective-permute-start(bf16[128,8192]{1,0:T(8,128)(2,1)} %get-tuple-element.54), channel_id=1, source_target_pairs={{0,1},{1,0},{2,3},{3,2},{4,5},{5,4},{6,7},{7,6}} | collective-permute-start | bytes 6291464 | tf_op jit(solution)/shard_map/ppermute | solution.py:851
  532.8 87.6 %reduce-scatter.16.cloned.1.call-start = ((), (), s32[]{:S(2)}) async-start(), calls=%async_computation.15 | async-start | bytes 3276800 | tf_op jit(solution)/shard_map/reduce_scatter | solution.py:979
  591.3 76.6 %all-gather.19.cloned.1.call-start = ((), (), s32[]{:S(2)}) async-start(), calls=%async_computation.16 | async-start | bytes 4718592 | tf_op jit(solution)/shard_map/all_gather | solution.py:968
  636.7 90.9 %reduce-scatter.18.cloned.1.call-start = ((), (), s32[]{:S(2)}) async-start(), calls=%async_computation.17 | async-start | bytes 3276800 | tf_op jit(solution)/shard_map/reduce_scatter | solution.py:979
  698.5 505.3 %reduce-scatter.20.cloned.1.call-start = ((), (), s32[]{:S(2)}) async-start(), calls=%async_computation.19 | async-start | bytes 6635520 | tf_op jit(solution)/shard_map/reduce_scatter | solution.py:990
  770.6 433.3 %all-gather.21.cloned.1.call-start = ((), (), s32[]{:S(2)}) async-start(), calls=%async_computation.18 | async-start | bytes 2359296 | tf_op jit(solution)/shard_map/all_gather | solution.py:987
  825.5 79.5 %collective-permute-start.34 = (f32[64,8192]{1,0:T(8,128)}, f32[64,8192]{1,0:T(8,128)}, u32[]{:S(2)}, u32[]{:S(2)}) collective-permute-start(f32[64,8192]{1,0:T(8,128)} %get-tuple-element.75), channel_id=1, source_target_pairs={{0,3},{1,2},{2,1},{3,0},{4,7},{5,6},{6,5},{7,4}} | collective-permute-start | bytes 6291464 | tf_op jit(solution)/shard_map/ppermute | solution.py:851
  903.3 78.8 %collective-permute-start.27 = (f32[4,128,896]{2,1,0:T(8,128)}, f32[4,128,896]{2,1,0:T(8,128)}, u32[]{:S(2)}, u32[]{:S(2)}) collective-permute-start(f32[4,128,896]{2,1,0:T(8,128)} %get-tuple-element.66), channel_id=1, source_target_pairs={{0,3},{1,2},{2,1},{3,0},{4,7},{5,6},{6,5},{7,4}} | collective-permute-start | bytes 5505032 | tf_op jit(solution)/shard_map/ppermute | solution.py:851
  903.3 124.1 %collective-permute-start.31 = (f32[128,8192]{1,0:T(8,128)}, f32[128,8192]{1,0:T(8,128)}, u32[]{:S(2)}, u32[]{:S(2)}) collective-permute-start(f32[128,8192]{1,0:T(8,128)} %get-tuple-element.73), channel_id=1, source_target_pairs={{0,1},{1,0},{2,3},{3,2},{4,5},{5,4},{6,7},{7,6}} | collective-permute-start | bytes 12582920 | tf_op jit(solution)/shard_map/ppermute | solution.py:851
  905.0 128.1 %collective-permute-start.24 = (f32[2,4,128,896]{3,2,1,0:T(8,128)}, f32[2,4,128,896]{3,2,1,0:T(8,128)}, u32[]{:S(2)}, u32[]{:S(2)}) collective-permute-start(f32[2,4,128,896]{3,2,1,0:T(8,128)} %get-tuple-element.64), channel_id=1, source_target_pairs={{0,1},{1,0},{2,3},{3,2},{4,5},{5,4},{6,7},{7,6}} | collective-permute-start | bytes 11010056 | tf_op jit(solution)/shard_map/ppermute | solution.py:851
  907.4 119.9 %collective-permute-start.35 = (f32[64,8192]{1,0:T(8,128)}, f32[64,8192]{1,0:T(8,128)}, u32[]{:S(2)}, u32[]{:S(2)}) collective-permute-start(f32[64,8192]{1,0:T(8,128)} %collective-permute-done.34.rx3), channel_id=1, source_target_pairs={{0,4},{4,0},{1,5},{5,1},{2,6},{6,2},{3,7},{7,3}} | collective-permute-start | bytes 6291464 | tf_op jit(solution)/shard_map/ppermute | solution.py:855
  945.9 82.4 %collective-permute-start.26 = (f32[4,128,896]{2,1,0:T(8,128)S(1)}, f32[4,128,896]{2,1,0:T(8,128)}, u32[]{:S(2)}, u32[]{:S(2)}) collective-permute-start(f32[4,128,896]{2,1,0:T(8,128)S(1)} %collective-permute-done.25.rx2), channel_id=1, source_target_pairs={{0,4},{4,0},{1,5},{5,1},{2,6},{6,2},{3,7},{7,3}} | collective-permute-start | bytes 5505032 | tf_op jit(solution)/shard_map/ppermute | solution.py:855
  1027.3 132.8 %collective-permute-start.30 = (f32[4,448,512]{2,1,0:T(8,128)}, f32[4,448,512]{2,1,0:T(8,128)}, u32[]{:S(2)}, u32[]{:S(2)}) collective-permute-start(f32[4,448,512]{2,1,0:T(8,128)} %get-tuple-element.70), channel_id=1, source_target_pairs={{0,1},{1,0},{2,3},{3,2},{4,5},{5,4},{6,7},{7,6}} | collective-permute-start | bytes 11010056 | tf_op jit(solution)/shard_map/ppermute | solution.py:851
  1028.3 88.9 %collective-permute-start.21 = (f32[4,128,896]{2,1,0:T(8,128)}, f32[4,128,896]{2,1,0:T(8,128)S(1)}, u32[]{:S(2)}, u32[]{:S(2)}) collective-permute-start(f32[4,128,896]{2,1,0:T(8,128)} %get-tuple-element.62), channel_id=1, source_target_pairs={{0,3},{1,2},{2,1},{3,0},{4,7},{5,6},{6,5},{7,4}} | collective-permute-start | bytes 5505032 | tf_op jit(solution)/shard_map/ppermute | solution.py:851
  1033.1 137.7 %collective-permute-start.18 = (f32[2,4,128,896]{3,2,1,0:T(8,128)}, f32[2,4,128,896]{3,2,1,0:T(8,128)}, u32[]{:S(2)}, u32[]{:S(2)}) collective-permute-start(f32[2,4,128,896]{3,2,1,0:T(8,128)} %get-tuple-element.60), channel_id=1, source_target_pairs={{0,1},{1,0},{2,3},{3,2},{4,5},{5,4},{6,7},{7,6}} | collective-permute-start | bytes 11010056 | tf_op jit(solution)/shard_map/ppermute | solution.py:851
  1033.1 160.2 %collective-permute-start.29 = (f32[4,448,512]{2,1,0:T(8,128)}, f32[4,448,512]{2,1,0:T(8,128)}, u32[]{:S(2)}, u32[]{:S(2)}) collective-permute-start(f32[4,448,512]{2,1,0:T(8,128)} %get-tuple-element.68), channel_id=1, source_target_pairs={{0,1},{1,0},{2,3},{3,2},{4,5},{5,4},{6,7},{7,6}} | collective-permute-start | bytes 11010056 | tf_op jit(solution)/shard_map/ppermute | solution.py:851
  1034.5 211.1 %all-reduce.15.cloned.1.call-start = ((), (), s32[]{:S(2)}) async-start(), calls=%async_computation.20 | async-start | bytes 2654208 | tf_op jit(solution)/shard_map/psum | solution.py:991
  1079.0 91.8 %collective-permute-start.20 = (f32[4,128,896]{2,1,0:T(8,128)}, f32[4,128,896]{2,1,0:T(8,128)}, u32[]{:S(2)}, u32[]{:S(2)}) collective-permute-start(f32[4,128,896]{2,1,0:T(8,128)} %collective-permute-done.19.rx2), channel_id=1, source_target_pairs={{0,4},{4,0},{1,5},{5,1},{2,6},{6,2},{3,7},{7,3}} | collective-permute-start | bytes 5505032 | tf_op jit(solution)/shard_map/ppermute | solution.py:855
  (185 other events, 3705.4 us)
Sparse Core Ops, SparseCore 0:
  12.4 18.4 all-gather.22
  34.2 20.1 reduce-scatter.7
  65.4 15.2 all-gather.10
  82.8 22.6 all-gather.24
  168.3 25.5 reduce-scatter.9
  202.3 15.7 all-gather.12
  296.2 25.6 reduce-scatter.11
  324.2 27.9 all-gather.14
  502.9 26.0 reduce-scatter.13
  532.9 31.0 all-gather.16
  591.4 28.9 reduce-scatter.15
  636.8 31.0 all-gather.18
  698.6 28.9 reduce-scatter.17
  770.7 59.6 reduce-scatter.19
  1034.6 30.5 all-gather.20
  1204.0 41.5 all-reduce.14

commit v2 on v1

v2 whole, which is shorter than its diff:
```python
import functools
import jax
import jax.numpy as jnp
from jax import lax
from jax.experimental import pallas as pl
from jax.experimental.pallas import tpu as pltpu
from jax.experimental.layout import Layout, with_layout_constraint
from jax.sharding import PartitionSpec as P

ZERO, ONE, TWO, ALL = 0, 1, 2, ...
LANES = 128
WIDTH = 512
FF_HALF = 896
HEAD_DIM = LANES
ROPE_THETA = 1000000.0
NORM_EPS = 1e-5
BF16 = jnp.bfloat16
F32 = jnp.float32
VMEM_LIMIT = 60 * 1024 * 1024
FSDP = 'fsdp'
REP = 'rep'


def rms_norm(residual, gain):
    mean_sq = jnp.mean(residual * residual, axis=-ONE, keepdims=True)
    return (residual * lax.rsqrt(mean_sq + NORM_EPS) * gain).astype(BF16)


def rope_tables(positions):
    inv_freq = ROPE_THETA ** (-jnp.arange(ZERO, HEAD_DIM, TWO, dtype=F32) / HEAD_DIM)
    angle = positions.astype(F32)[ALL, None] * inv_freq
    return jnp.cos(angle)[:, None, :], jnp.sin(angle)[:, None, :]


def apply_rope(heads, cos_tab, sin_tab):
    half_dim = heads.shape[-ONE] // TWO
    lower = heads[ALL, :half_dim]
    upper = heads[ALL, half_dim:]
    return jnp.concatenate([lower * cos_tab - upper * sin_tab, upper * cos_tab + lower * sin_tab], axis=-ONE)


def attention_part(residual, w_qkv, w_o, gain, cos_tab, sin_tab):
    length = residual.shape[ZERO]
    q_width = w_o.shape[ZERO]
    q_heads = q_width // HEAD_DIM
    normed = rms_norm(residual, gain)
    projected = jnp.dot(normed, w_qkv, preferred_element_type=F32)
    values = projected[:, q_width + HEAD_DIM:].astype(BF16)
    turned = apply_rope(projected[:, :q_width + HEAD_DIM].reshape(length, q_heads + ONE, HEAD_DIM), cos_tab, sin_tab).astype(BF16)
    query, keyed = turned[:, :q_heads], turned[:, q_heads]
    scores = jnp.einsum('qgd,sd->gqs', query, keyed, preferred_element_type=F32) * HEAD_DIM ** -0.5
    causal = lax.broadcasted_iota(jnp.int32, (length, length), ZERO) >= lax.broadcasted_iota(jnp.int32, (length, length), ONE)
    scores = jnp.where(causal, scores, -1e30)
    attn_probs = jax.nn.softmax(scores, axis=-ONE).astype(BF16)
    mixed = jnp.einsum('gqs,sd->qgd', attn_probs, values, preferred_element_type=F32).astype(BF16)
    mixed = mixed.reshape(length, q_width)
    return residual + jnp.dot(mixed, w_o, preferred_element_type=F32)


def combine_weights(logits, chosen):
    rows = lax.broadcasted_iota(jnp.int32, logits.shape, ZERO)
    first = rows == chosen[:ONE]
    second = rows == chosen[ONE:]
    r0 = jnp.sum(jnp.where(first, logits, 0.0), axis=ZERO, keepdims=True)
    r1 = jnp.sum(jnp.where(second, logits, 0.0), axis=ZERO, keepdims=True)
    gates = jax.nn.softmax(jnp.concatenate([r0, r1], axis=ZERO), axis=ZERO)
    return jnp.where(first, gates[:ONE], 0.0) + jnp.where(second, gates[ONE:], 0.0)


def router_logits(normed, w_r):
    return lax.dot_general(w_r, normed, (((ZERO,), (ONE,)), ((), ())), preferred_element_type=F32)


def router_part(residual, gain, w_r, chosen):
    normed = rms_norm(residual, gain)
    return normed, combine_weights(router_logits(normed, w_r), chosen)


def dot_nn(a, b):
    return jnp.dot(a, b, preferred_element_type=F32)


def dot_nt(a, b):
    return lax.dot_general(a, b, (((ONE,), (ONE,)), ((), ())), preferred_element_type=F32)


def params(steps):
    return pltpu.CompilerParams(dimension_semantics=("arbitrary",) * steps, vmem_limit_bytes=VMEM_LIMIT)


def permuted_columns(ref, me):
    return jnp.concatenate([ref[:, pl.ds(pl.multiple_of((me ^ k) * LANES, LANES), LANES)] for k in range(4)], axis=ONE)


def pack_experts_kernel(sc, gate1, up1, gate2, up2, gate3, up3, down1, out1, out2, out3, out_down):
    rep = sc[TWO]
    out1[ZERO, ZERO] = gate1[ZERO, ZERO].astype(BF16)
    out1[ONE, ZERO] = up1[ZERO, ZERO].astype(BF16)
    out2[ZERO] = jnp.where(rep == ZERO, gate2[ZERO, ZERO], up2[ZERO, ZERO]).astype(BF16)
    out3[ZERO] = jnp.where(rep == ZERO, gate3[ZERO, ZERO], up3[ZERO, ZERO]).astype(BF16)
    out_down[ZERO] = down1[ZERO, ZERO].astype(BF16)


def pack_experts(sc, layer, w_gate, w_up, w_down):
    def spec(own_core, own_half, matrix=None):
        def index(j, sc):
            step = j if matrix is None else jnp.where(sc[TWO] == matrix, j, ZERO)
            core = sc[ZERO] if own_core else ONE - sc[ZERO]
            return layer, TWO * step + core, ZERO, (sc[ONE] if own_half else ONE - sc[ONE])

        return pl.BlockSpec((ONE, ONE, LANES, FF_HALF), index)

    block = lambda j, sc: (j, ZERO, ZERO)
    return pl.pallas_call(
        pack_experts_kernel,
        grid_spec=pltpu.PrefetchScalarGridSpec(
            num_scalar_prefetch=ONE,
            grid=(4,),
            in_specs=[spec(False, True), spec(False, True), spec(True, False, ZERO), spec(True, False, ONE), spec(False, False, ZERO), spec(False, False, ONE),
                      pl.BlockSpec((ONE, ONE, 448, WIDTH), lambda j, sc: (layer, TWO * j + ONE - sc[ZERO], ZERO, ZERO))],
            out_specs=[pl.BlockSpec((TWO, ONE, LANES, FF_HALF), lambda j, sc: (ZERO, j, ZERO, ZERO)), pl.BlockSpec((ONE, LANES, FF_HALF), block), pl.BlockSpec((ONE, LANES, FF_HALF), block),
                       pl.BlockSpec((ONE, 448, WIDTH), block)],
        ),
        out_shape=[
            jax.ShapeDtypeStruct((TWO, 4, LANES, FF_HALF), BF16),
            jax.ShapeDtypeStruct((4, LANES, FF_HALF), BF16),
            jax.ShapeDtypeStruct((4, LANES, FF_HALF), BF16),
            jax.ShapeDtypeStruct((4, 448, WIDTH), BF16),
        ],
        compiler_params=params(ONE),
        cost_estimate=pl.CostEstimate(flops=10_000_000, bytes_accessed=17_000_000, transcendentals=ZERO),
    )(sc, w_gate, w_up, w_gate, w_up, w_gate, w_up, w_down)


def pack_head_kernel(sc, w_ref, out0, out1, out2, out3):
    core, x, rep = sc[ZERO], sc[ONE], sc[TWO]

    def part(xx, cc):
        return w_ref[:, pl.ds(pl.multiple_of(head_start(xx, cc), LANES), HEAD_COLS)].astype(BF16)

    out0[ALL] = part(x, core)
    out1[ALL] = part(x, ONE - core)

    @pl.when(pl.program_id(ZERO) // (pl.num_programs(ZERO) // TWO) == rep)
    def _():
        out2[ALL] = part(ONE - x, core)
        out3[ALL] = part(ONE - x, ONE - core)


def pack_head(sc, w):
    rows, vocab = w.shape
    step = 16
    count = rows // step
    half = lambda i, sc: (jnp.clip(i - sc[TWO] * (count // TWO), ZERO, count // TWO - ONE), ZERO)
    return pl.pallas_call(
        pack_head_kernel,
        grid_spec=pltpu.PrefetchScalarGridSpec(
            num_scalar_prefetch=ONE,
            grid=(count,),
            in_specs=[pl.BlockSpec((step, vocab), lambda i, sc: (i, ZERO))],
            out_specs=[pl.BlockSpec((step, HEAD_COLS), lambda i, sc: (i, ZERO))] * TWO + [pl.BlockSpec((step, HEAD_COLS), half)] * TWO,
        ),
        out_shape=[jax.ShapeDtypeStruct((rows, HEAD_COLS), BF16)] * TWO + [jax.ShapeDtypeStruct((rows // TWO, HEAD_COLS), BF16)] * TWO,
        compiler_params=params(ONE),
        cost_estimate=pl.CostEstimate(flops=10_000_000, bytes_accessed=23_000_000, transcendentals=ZERO),
    )(sc, w)


def fill_expert_weights(sc, wg_own, wu_own, gu1, rx2, ry2, rx3, ry3, wd_own, wd1, wgu, wd):
    core, rep = sc[ZERO], sc[TWO]
    wgu[ZERO:LANES, ZERO:FF_HALF] = wg_own[ZERO, ZERO].astype(BF16)
    wgu[ZERO:LANES, FF_HALF:1792] = wu_own[ZERO, ZERO].astype(BF16)
    wgu[LANES:256, ZERO:FF_HALF] = gu1[ZERO, ZERO]
    wgu[LANES:256, FF_HALF:1792] = gu1[ONE, ZERO]
    by_x = pl.ds(pl.multiple_of(rep * FF_HALF, LANES), FF_HALF)
    by_y = pl.ds(pl.multiple_of((ONE - rep) * FF_HALF, LANES), FF_HALF)
    wgu[256:384, by_x] = rx2[ZERO]
    wgu[384:WIDTH, by_x] = rx3[ZERO]
    wgu[256:384, by_y] = ry2[ZERO]
    wgu[384:WIDTH, by_y] = ry3[ZERO]
    wd[pl.ds(pl.multiple_of(core * 448, 64), 448), :] = wd_own[ZERO, ZERO].astype(BF16)
    wd[pl.ds(pl.multiple_of((ONE - core) * 448, 64), 448), :] = wd1[ZERO]


def expert_weight_specs(layer):
    own = lambda j, t, sc: (layer, TWO * j + sc[ZERO], ZERO, sc[ONE])
    return [
        pl.BlockSpec((ONE, ONE, LANES, FF_HALF), own),
        pl.BlockSpec((ONE, ONE, LANES, FF_HALF), own),
        pl.BlockSpec((TWO, ONE, LANES, FF_HALF), lambda j, t, sc: (ZERO, j, ZERO, ZERO)),
        pl.BlockSpec((ONE, LANES, FF_HALF), lambda j, t, sc: (j, ZERO, ZERO)),
        pl.BlockSpec((ONE, LANES, FF_HALF), lambda j, t, sc: (j, ZERO, ZERO)),
        pl.BlockSpec((ONE, LANES, FF_HALF), lambda j, t, sc: (j, ZERO, ZERO)),
        pl.BlockSpec((ONE, LANES, FF_HALF), lambda j, t, sc: (j, ZERO, ZERO)),
        pl.BlockSpec((ONE, ONE, 448, WIDTH), lambda j, t, sc: (layer, TWO * j + sc[ZERO], ZERO, ZERO)),
        pl.BlockSpec((ONE, 448, WIDTH), lambda j, t, sc: (j, ZERO, ZERO)),
    ]


EXPERT_SCRATCH = [pltpu.VMEM((WIDTH, 1792), BF16), pltpu.VMEM((FF_HALF, WIDTH), BF16)]


def expert_column(comb, expert):
    lanes = lax.broadcasted_iota(jnp.int32, comb.shape, ONE)
    return jnp.sum(jnp.where(lanes == expert, comb, 0.0), axis=ONE, keepdims=True)


def expert_forward_kernel(sc, b_ref, comb_ref, wg_own, wu_own, gu1, rx2, ry2, rx3, ry3, wd_own, wd1, out_ref, wgu, wd):
    j, t = pl.program_id(ZERO), pl.program_id(ONE)
    tile = b_ref.shape[ZERO]

    @pl.when(t == ZERO)
    def _():
        fill_expert_weights(sc, wg_own, wu_own, gu1, rx2, ry2, rx3, ry3, wd_own, wd1, wgu, wd)

    b = permuted_columns(b_ref, sc[3])
    both = dot_nn(b, wgu[ALL])
    gate, up = both[:, ZERO:FF_HALF], both[:, FF_HALF:1792]
    hidden = (gate * jax.nn.sigmoid(gate) * up).astype(BF16)
    weighted = dot_nn(hidden, wd[ALL]) * expert_column(comb_ref[ALL], TWO * j + sc[ZERO])
    rows = pl.ds(pl.multiple_of(t * tile, tile), tile)

    @pl.when(j == ZERO)
    def _():
        out_ref[rows, :] = weighted

    @pl.when(j != ZERO)
    def _():
        out_ref[rows, :] += weighted


def expert_forward(sc, layer, b_rows, comb, w_gate, w_up, pieces, w_down, wd1):
    rows, width = b_rows.shape
    tile = 1024
    return pl.pallas_call(
        expert_forward_kernel,
        grid_spec=pltpu.PrefetchScalarGridSpec(
            num_scalar_prefetch=ONE,
            grid=(4, rows // tile),
            in_specs=[
                pl.BlockSpec((tile, width), lambda j, t, sc: (t, ZERO)),
                pl.BlockSpec((tile, 8), lambda j, t, sc: (t, ZERO)),
            ] + expert_weight_specs(layer),
            out_specs=pl.BlockSpec((rows, width), lambda j, t, sc: (ZERO, ZERO)),
            scratch_shapes=EXPERT_SCRATCH,
        ),
        out_shape=jax.ShapeDtypeStruct((rows, width), F32),
        compiler_params=params(TWO),
        cost_estimate=pl.CostEstimate(flops=11_300_000_000, bytes_accessed=20_000_000, transcendentals=3_700_000),
    )(sc, b_rows, comb, w_gate, w_up, *pieces, w_down, wd1)


SLOT_TILE = 256


def slot_gradients(b_sel, d_sel, weight, wgu, wd):
    both = dot_nn(b_sel, wgu[ALL])
    gate, up = both[:, ZERO:FF_HALF], both[:, FF_HALF:1792]
    sig = jax.nn.sigmoid(gate)
    silu = gate * sig
    hidden = (silu * up).astype(BF16).astype(F32)
    d_hidden = dot_nt(d_sel, wd[ALL])
    d_weight = jnp.sum(hidden * d_hidden, axis=ONE, keepdims=True)
    d_hidden = (d_hidden * weight).astype(BF16).astype(F32)
    d_up = (d_hidden * silu).astype(BF16)
    d_gate = (d_hidden * up * (sig * (1.0 + gate * (1.0 - sig)))).astype(BF16)
    return (hidden * weight).astype(BF16), jnp.concatenate([d_gate, d_up], axis=ONE), d_weight


def load_tokens(rows_ref, b_ref, d_ref, me):
    rows_ref[:, ZERO:WIDTH] = permuted_columns(b_ref, me)
    rows_ref[:, WIDTH:1024] = d_ref[ALL].astype(BF16)


def select_slots(rank_row, comb_row, m, tokens_ref):
    index = lax.broadcasted_iota(jnp.int32, (SLOT_TILE, rank_row.shape[ONE]), ZERO) + m * SLOT_TILE
    chosen = index == rank_row
    picked = dot_nn(jnp.where(chosen, 1.0, 0.0).astype(BF16), tokens_ref[ALL])
    weight = jnp.sum(jnp.where(chosen, comb_row, 0.0), axis=ONE, keepdims=True)
    return chosen, picked[:, ZERO:WIDTH], picked[:, WIDTH:1024], weight


def slot_tiles(sc, group, expert):
    return (sc[4 + group * 8 + expert] + (SLOT_TILE - ONE)) // SLOT_TILE


def expert_dgrad_kernel(sc, b_ref, d_ref, rank_ref, rank_col_ref, comb_ref, wg_own, wu_own, gu1, rx2, ry2, rx3, ry3, wd_own, wd1,
                        db_ref, wgu, wd, tokens_ref, db_acc, dw_acc):
    j = pl.program_id(ZERO)
    core, rep, me = sc[ZERO], sc[TWO], sc[3]
    expert = TWO * j + core

    @pl.when(j == ZERO)
    def _():
        load_tokens(tokens_ref, b_ref, d_ref, me)
        db_acc[ALL] = jnp.zeros_like(db_acc)
        dw_acc[ALL] = jnp.zeros_like(dw_acc)

    fill_expert_weights(sc, wg_own, wu_own, gu1, rx2, ry2, rx3, ry3, wd_own, wd1, wgu, wd)

    row = pl.ds(expert, ONE)

    def slots(m, carry):
        chosen, b_sel, d_sel, weight = select_slots(rank_ref[ZERO, row, :], comb_ref[row, :], m, tokens_ref)
        _, d_both, d_weight = slot_gradients(b_sel.astype(BF16), d_sel.astype(BF16), weight, wgu, wd)
        db = dot_nt(d_both, wgu[ALL])
        high = db.astype(BF16)
        rest = db - high.astype(F32)
        middle = rest.astype(BF16)
        low = (rest - middle.astype(F32)).astype(BF16)
        rank_all = rank_col_ref[ZERO]
        lanes = lax.broadcasted_iota(jnp.int32, rank_all.shape, ONE)
        rank_col = jnp.sum(jnp.where(lanes == expert, rank_all, ZERO), axis=ONE, keepdims=True)
        index = lax.broadcasted_iota(jnp.int32, (rank_all.shape[ZERO], SLOT_TILE), ONE) + m * SLOT_TILE
        spread = jnp.where(index == rank_col, 1.0, 0.0).astype(BF16)
        db_acc[ALL] += dot_nn(jnp.concatenate([spread] * 3, axis=ONE), jnp.concatenate([high, middle, low], axis=ZERO))
        dw_acc[row, :] += jnp.sum(jnp.where(chosen, d_weight, 0.0), axis=ZERO, keepdims=True)
        return carry

    lax.fori_loop(ZERO, slot_tiles(sc, rep, expert), slots, ZERO)

    @pl.when(j == pl.num_programs(ZERO) - ONE)
    def _():
        for k in range(4):
            db_ref[:, pl.ds(pl.multiple_of((me ^ k) * LANES, LANES), LANES)] = db_acc[:, k * LANES:(k + ONE) * LANES]
        db_ref[:, WIDTH:640] = dw_acc[ALL].T


def expert_dgrad(sc, layer, b_group, d_all, ranks, rank_cols, comb, w_gate, w_up, pieces, w_down, wd1):
    rows, width = b_group.shape
    return pl.pallas_call(
        expert_dgrad_kernel,
        grid_spec=pltpu.PrefetchScalarGridSpec(
            num_scalar_prefetch=ONE,
            grid=(4, ONE),
            in_specs=[
                pl.BlockSpec((rows, width), lambda j, t, sc: (ZERO, ZERO)),
                pl.BlockSpec((rows, width), lambda j, t, sc: (sc[TWO], ZERO)),
                pl.BlockSpec((ONE, 8, rows), lambda j, t, sc: (sc[TWO], ZERO, ZERO)),
                pl.BlockSpec((ONE, rows, 8), lambda j, t, sc: (sc[TWO], ZERO, ZERO)),
                pl.BlockSpec((8, rows), lambda j, t, sc: (ZERO, ZERO)),
            ] + expert_weight_specs(layer),
            out_specs=pl.BlockSpec((rows, 640), lambda j, t, sc: (ZERO, ZERO)),
            scratch_shapes=EXPERT_SCRATCH + [pltpu.VMEM((rows, TWO * width), BF16), pltpu.VMEM((rows, width), F32), pltpu.VMEM((LANES, rows), F32)],
        ),
        out_shape=jax.ShapeDtypeStruct((rows, 640), F32),
        compiler_params=params(TWO),
        cost_estimate=pl.CostEstimate(flops=15_000_000_000, bytes_accessed=25_000_000, transcendentals=2_000_000),
    )(sc, b_group, d_all, ranks, rank_cols, comb, w_gate, w_up, *pieces, w_down, wd1)


def expert_wgrad_kernel(sc, b_own, b_other, d_own, d_other, rank_ref, comb_own, comb_other,
                        wg_own, wu_own, gu1, rx2, ry2, rx3, ry3, wd_own, wd1,
                        own_ref, near_ref, far2_ref, far3_ref, down_own_ref, down_other_ref, wgu, wd, tokens_ref, comb_ref, down_acc):
    j, group = pl.program_id(ZERO), pl.program_id(ONE)
    core, rep, me = sc[ZERO], sc[TWO], sc[3]
    expert = TWO * j + core

    @pl.when((j == ZERO) & (group == ZERO))
    def _():
        load_tokens(tokens_ref.at[rep], b_own, d_own, me)
        load_tokens(tokens_ref.at[ONE - rep], b_other, d_other, me)
        comb_ref[rep] = comb_own[ALL]
        comb_ref[ONE - rep] = comb_other[ALL]

    @pl.when(group == ZERO)
    def _():
        fill_expert_weights(sc, wg_own, wu_own, gu1, rx2, ry2, rx3, ry3, wd_own, wd1, wgu, wd)
        for ref in (own_ref, near_ref, far2_ref, far3_ref, down_acc):
            ref[ALL] = jnp.zeros_like(ref)

    row = pl.ds(expert, ONE)

    def slots(m, carry):
        _, b_sel, d_sel, weight = select_slots(rank_ref[ZERO, row, :], comb_ref[group, row, :], m, tokens_ref.at[group])
        hidden, d_both, _ = slot_gradients(b_sel.astype(BF16), d_sel.astype(BF16), weight, wgu, wd)
        bt = b_sel.T.astype(BF16)
        dt = d_sel.T.astype(BF16)
        dw = dot_nn(bt[ZERO:256], d_both)
        for matrix in range(TWO):
            cols = slice(matrix * FF_HALF, matrix * FF_HALF + FF_HALF)
            own_ref[matrix, ZERO] += dw[ZERO:LANES, cols]
            near_ref[matrix, ZERO] += dw[LANES:256, cols]
        dw = dot_nn(bt[256:WIDTH], jnp.where(rep == ZERO, d_both[:, ZERO:FF_HALF], d_both[:, FF_HALF:1792]))
        far2_ref[ZERO] += dw[ZERO:LANES]
        far3_ref[ZERO] += dw[LANES:256]
        down_acc[ALL] += dot_nn(dt, hidden)
        return carry

    lax.fori_loop(ZERO, slot_tiles(sc, group, expert), slots, ZERO)

    @pl.when(group == ONE)
    def _():
        down_t = down_acc[ALL].T
        lower, upper = down_t[ZERO:448], down_t[448:FF_HALF]

        @pl.when(core == ZERO)
        def _():
            down_own_ref[ZERO] = lower
            down_other_ref[ZERO] = upper

        @pl.when(core != ZERO)
        def _():
            down_own_ref[ZERO] = upper
            down_other_ref[ZERO] = lower


def expert_wgrad(sc, layer, b_own, b_other, d_all, ranks, comb_own, comb_other, w_gate, w_up, pieces, w_down, wd1):
    rows, width = b_own.shape
    once = pl.BlockSpec((rows, width), lambda j, g, t, sc: (ZERO, ZERO))
    weights = [pl.BlockSpec(spec.block_shape, functools.partial(lambda index, j, g, t, sc: index(j, t, sc), spec.index_map)) for spec in expert_weight_specs(layer)]
    return pl.pallas_call(
        expert_wgrad_kernel,
        grid_spec=pltpu.PrefetchScalarGridSpec(
            num_scalar_prefetch=ONE,
            grid=(4, TWO, ONE),
            in_specs=[once] * TWO + [
                pl.BlockSpec((rows, width), lambda j, g, t, sc: (sc[TWO], ZERO)),
                pl.BlockSpec((rows, width), lambda j, g, t, sc: (ONE - sc[TWO], ZERO)),
                pl.BlockSpec((ONE, 8, rows), lambda j, g, t, sc: (g, ZERO, ZERO)),
                pl.BlockSpec((8, rows), lambda j, g, t, sc: (ZERO, ZERO)),
                pl.BlockSpec((8, rows), lambda j, g, t, sc: (ZERO, ZERO)),
            ] + weights,
            out_specs=[
                pl.BlockSpec((TWO, ONE, LANES, FF_HALF), lambda j, g, t, sc: (ZERO, j, ZERO, ZERO)),
                pl.BlockSpec((TWO, ONE, LANES, FF_HALF), lambda j, g, t, sc: (ZERO, j, ZERO, ZERO)),
                pl.BlockSpec((ONE, LANES, FF_HALF), lambda j, g, t, sc: (j, ZERO, ZERO)),
                pl.BlockSpec((ONE, LANES, FF_HALF), lambda j, g, t, sc: (j, ZERO, ZERO)),
                pl.BlockSpec((ONE, 448, WIDTH), lambda j, g, t, sc: (j, ZERO, ZERO)),
                pl.BlockSpec((ONE, 448, WIDTH), lambda j, g, t, sc: (j, ZERO, ZERO)),
            ],
            scratch_shapes=EXPERT_SCRATCH + [pltpu.VMEM((TWO, rows, TWO * width), BF16), pltpu.VMEM((TWO, 8, rows), F32), pltpu.VMEM((WIDTH, FF_HALF), F32)],
        ),
        out_shape=[
            jax.ShapeDtypeStruct((TWO, 4, LANES, FF_HALF), F32),
            jax.ShapeDtypeStruct((TWO, 4, LANES, FF_HALF), F32),
            jax.ShapeDtypeStruct((4, LANES, FF_HALF), F32),
            jax.ShapeDtypeStruct((4, LANES, FF_HALF), F32),
            jax.ShapeDtypeStruct((4, 448, WIDTH), F32),
            jax.ShapeDtypeStruct((4, 448, WIDTH), F32),
        ],
        compiler_params=params(3),
        cost_estimate=pl.CostEstimate(flops=30_000_000_000, bytes_accessed=50_000_000, transcendentals=4_000_000),
    )(sc, b_own, b_other, d_all, d_all, ranks, comb_own, comb_other, w_gate, w_up, *pieces, w_down, wd1)


HEAD_COLS = 8192
HEAD_BLOCK = 1024
HEAD_TILE = 1024
HEAD_HALF = 16000
HEAD_SHIFT = 7808
HEAD_OVERLAP = HEAD_COLS - HEAD_SHIFT


def head_start(x, core):
    return x * HEAD_HALF + core * HEAD_SHIFT


def fill_head_weights(sc, own, p1, rx2, ry2, rx3, ry3, w):
    rep = sc[TWO]
    w[ZERO:LANES, :] = own[ALL]
    w[LANES:256, :] = p1[ALL]
    for k, (rx, ry) in ((TWO, (rx2, ry2)), (3, (rx3, ry3))):
        w[pl.ds(pl.multiple_of(k * LANES + rep * 64, 64), 64), :] = rx[ALL]
        w[pl.ds(pl.multiple_of(k * LANES + (ONE - rep) * 64, 64), 64), :] = ry[ALL]


def head_weight_specs():
    return [pl.BlockSpec((LANES, HEAD_BLOCK), lambda i, sc: (ZERO, i))] * TWO + [pl.BlockSpec((64, HEAD_BLOCK), lambda i, sc: (ZERO, i))] * 4


def head_stats_kernel(sc, x_ref, own, p1, rx2, ry2, rx3, ry3, out_ref, w, xp, m_acc, s_acc):
    i = pl.program_id(ZERO)
    rows = x_ref.shape[ZERO]

    @pl.when(i == ZERO)
    def _():
        xp[ALL] = permuted_columns(x_ref, sc[3])
        m_acc[ALL] = jnp.full((rows, LANES), -1e30, F32)
        s_acc[ALL] = jnp.zeros((rows, LANES), F32)

    fill_head_weights(sc, own, p1, rx2, ry2, rx3, ry3, w)
    first_new = jnp.where((sc[ZERO] == ONE) & (i == ZERO), HEAD_OVERLAP, ZERO)
    tiles = [slice(t, t + HEAD_TILE) for t in range(ZERO, rows, HEAD_TILE)]

    def update(tile, logits):
        pieces = []
        for q in range(HEAD_BLOCK // LANES):
            piece = logits[:, q * LANES:(q + ONE) * LANES]
            if q * LANES < HEAD_OVERLAP:
                piece = piece + jnp.where(q * LANES >= first_new, 0.0, -1e30)
            pieces.append(piece)
        peak = m_acc[tile, :]
        top = functools.reduce(jnp.maximum, pieces, peak)
        total = s_acc[tile, :] * jnp.exp(peak - top)
        for piece in pieces:
            total = total + jnp.exp(piece - top)
        m_acc[tile, :] = top
        s_acc[tile, :] = total

    ahead = dot_nn(xp[tiles[ZERO], :], w[ALL])
    for n, tile in enumerate(tiles):
        logits = ahead
        if n + ONE < len(tiles):
            ahead = dot_nn(xp[tiles[n + ONE], :], w[ALL])
        update(tile, logits)

    @pl.when(i == pl.num_programs(ZERO) - ONE)
    def _():
        top = m_acc[ALL]
        highest = jnp.max(top, axis=ONE, keepdims=True)
        out_ref[:, ZERO:ONE] = highest
        out_ref[:, ONE:TWO] = jnp.sum(s_acc[ALL] * jnp.exp(top - highest), axis=ONE, keepdims=True)


def head_stats(sc, x_rows, pieces):
    rows, width = x_rows.shape
    return pl.pallas_call(
        head_stats_kernel,
        grid_spec=pltpu.PrefetchScalarGridSpec(
            num_scalar_prefetch=ONE,
            grid=(HEAD_COLS // HEAD_BLOCK,),
            in_specs=[pl.BlockSpec((rows, width), lambda i, sc: (ZERO, ZERO))] + head_weight_specs(),
            out_specs=pl.BlockSpec((rows, 8), lambda i, sc: (ZERO, ZERO)),
            scratch_shapes=[pltpu.VMEM((width, HEAD_BLOCK), BF16), pltpu.VMEM((rows, width), BF16)] + [pltpu.VMEM((rows, LANES), F32)] * TWO,
        ),
        out_shape=jax.ShapeDtypeStruct((rows, 8), F32),
        compiler_params=params(ONE),
        cost_estimate=pl.CostEstimate(flops=17_000_000_000, bytes_accessed=25_000_000, transcendentals=16_800_000),
    )(sc, x_rows, *pieces)


def head_dx_kernel(sc, x_ref, label_ref, lse_ref, own, p1, rx2, ry2, rx3, ry3, dl_ref, dx_ref, picked_ref, w, xp, dx_acc, picked_acc):
    i = pl.program_id(ZERO)
    core, x, rep, me = sc[ZERO], sc[ONE], sc[TWO], sc[3]
    rows = x_ref.shape[ZERO]
    half = rows // TWO

    @pl.when(i == ZERO)
    def _():
        xp[ALL] = permuted_columns(x_ref, me)
        dx_acc[ALL] = jnp.zeros_like(dx_acc)
        picked_acc[ALL] = jnp.zeros_like(picked_acc)

    fill_head_weights(sc, own, p1, rx2, ry2, rx3, ry3, w)
    start = head_start(x, core) + i * HEAD_BLOCK
    first_new = jnp.where((core == ONE) & (i == ZERO), HEAD_OVERLAP, ZERO)
    cols = lax.broadcasted_iota(jnp.int32, (HEAD_TILE, HEAD_BLOCK), ONE)
    count = half // HEAD_TILE
    tiles = []
    for side in (rep, ONE - rep):
        for t in range(count):
            tiles.append(pl.ds(pl.multiple_of(side * half + t * HEAD_TILE, HEAD_TILE), HEAD_TILE))

    def gradient(tile, logits):
        hit = cols == label_ref[tile, :] - start
        prob = jnp.exp(logits - lse_ref[tile, :])
        picked = jnp.where(hit, logits, 0.0)
        picked_acc[ALL] += sum(jnp.where(q * LANES >= first_new, 1.0, 0.0) * jnp.sum(picked[:, q * LANES:(q + ONE) * LANES].reshape(HEAD_TILE // 8, 8, LANES), axis=ZERO)
                               for q in range(HEAD_BLOCK // LANES))
        d_logits = (jnp.where(hit, prob - 1.0, prob) * (1.0 / rows)).astype(BF16)
        dl_ref[tile, :] = d_logits
        return d_logits

    def project(n, d_logits):
        overlap = d_logits[:, ZERO:HEAD_OVERLAP]
        overlap = jnp.where(first_new == ZERO, overlap.astype(F32), 0.0).astype(BF16)
        masked = jnp.concatenate([overlap, d_logits[:, HEAD_OVERLAP:]], axis=ONE)
        dx_acc[n * HEAD_TILE:(n + ONE) * HEAD_TILE, :] += dot_nt(masked, w[ALL])

    ahead = dot_nn(xp[tiles[ZERO], :], w[ALL])
    for n, tile in enumerate(tiles):
        logits = ahead
        if n + ONE < len(tiles):
            ahead = dot_nn(xp[tiles[n + ONE], :], w[ALL])
        d_logits = gradient(tile, logits)
        if n < count:
            project(n, d_logits)

    @pl.when(i == pl.num_programs(ZERO) - ONE)
    def _():
        for k in range(4):
            dx_ref[:, pl.ds(pl.multiple_of((me ^ k) * LANES, LANES), LANES)] = dx_acc[:, k * LANES:(k + ONE) * LANES]
        picked_ref[ALL] = picked_acc[ALL]


def head_dx(sc, x_rows, labels, lse, pieces):
    rows, width = x_rows.shape
    return pl.pallas_call(
        head_dx_kernel,
        grid_spec=pltpu.PrefetchScalarGridSpec(
            num_scalar_prefetch=ONE,
            grid=(HEAD_COLS // HEAD_BLOCK,),
            in_specs=[
                pl.BlockSpec((rows, width), lambda i, sc: (ZERO, ZERO)),
                pl.BlockSpec((rows, ONE), lambda i, sc: (ZERO, ZERO)),
                pl.BlockSpec((rows, ONE), lambda i, sc: (ZERO, ZERO)),
            ] + head_weight_specs(),
            out_specs=[pl.BlockSpec((rows, HEAD_BLOCK), lambda i, sc: (ZERO, i)), pl.BlockSpec((rows // TWO, width), lambda i, sc: (ZERO, ZERO)),
                       pl.BlockSpec((8, LANES), lambda i, sc: (ZERO, ZERO))],
            scratch_shapes=[pltpu.VMEM((width, HEAD_BLOCK), BF16), pltpu.VMEM((rows, width), BF16), pltpu.VMEM((rows // TWO, width), F32),
                            pltpu.VMEM((8, LANES), F32)],
        ),
        out_shape=[jax.ShapeDtypeStruct((rows, HEAD_COLS), BF16), jax.ShapeDtypeStruct((rows // TWO, width), F32), jax.ShapeDtypeStruct((8, LANES), F32)],
        compiler_params=params(ONE),
        cost_estimate=pl.CostEstimate(flops=26_000_000_000, bytes_accessed=60_000_000, transcendentals=16_800_000),
    )(sc, x_rows, labels, lse, *pieces)


def head_dw_kernel(sc, xt_ref, dl_ref, d0, d1, d2, d3, xt):
    @pl.when(pl.program_id(ZERO) == ZERO)
    def _():
        me, rep = sc[3], sc[TWO]
        for k in range(TWO):
            xt[k * LANES:(k + ONE) * LANES, :] = xt_ref[pl.ds(pl.multiple_of((me ^ k) * LANES, LANES), LANES), :]
        for k in range(TWO, 4):
            xt[LANES + k * 64:192 + k * 64, :] = xt_ref[pl.ds(pl.multiple_of((me ^ k) * LANES + rep * 64, 64), 64), :]

    dw = dot_nn(xt[ALL], dl_ref[ALL])
    d0[ALL] = dw[ZERO:LANES]
    d1[ALL] = dw[LANES:256]
    d2[ALL] = dw[256:320]
    d3[ALL] = dw[320:384]


def head_dw(sc, x_cols, dl):
    width, rows = x_cols.shape
    block = WIDTH
    return pl.pallas_call(
        head_dw_kernel,
        grid_spec=pltpu.PrefetchScalarGridSpec(
            num_scalar_prefetch=ONE,
            grid=(HEAD_COLS // block,),
            in_specs=[
                pl.BlockSpec((width, rows), lambda i, sc: (ZERO, ZERO)),
                pl.BlockSpec((rows, block), lambda i, sc: (ZERO, i)),
            ],
            out_specs=[pl.BlockSpec((LANES, block), lambda i, sc: (ZERO, i))] * TWO + [pl.BlockSpec((64, block), lambda i, sc: (ZERO, i))] * TWO,
            scratch_shapes=[pltpu.VMEM((384, rows), BF16)],
        ),
        out_shape=[jax.ShapeDtypeStruct((LANES, HEAD_COLS), F32)] * TWO + [jax.ShapeDtypeStruct((64, HEAD_COLS), F32)] * TWO,
        compiler_params=params(ONE),
        cost_estimate=pl.CostEstimate(flops=13_000_000_000, bytes_accessed=52_000_000, transcendentals=ZERO),
    )(sc, x_cols, dl)


def update_near_kernel(sc, rate, w_ref, own, p1, *rest):
    out_ref = rest[-ONE]

    @pl.when(pl.program_id(ZERO) == ZERO)
    def _():
        out_ref[ZERO, ZERO] = w_ref[ZERO, ZERO] - rate[ZERO] * own[ZERO, ZERO]

    @pl.when(pl.program_id(ZERO) == ONE)
    def _():
        out_ref[ZERO, ZERO] = w_ref[ZERO, ZERO] - rate[ZERO] * p1[ZERO, ZERO]


def update_far_kernel(sc, rate, w_ref, first2, first3, second2, second3, *rest):
    out_ref = rest[-ONE]

    @pl.when((pl.program_id(ZERO) == ZERO) & (sc[TWO] == sc[4]))
    def _():
        out_ref[ZERO, ZERO] = w_ref[ZERO, ZERO] - rate[ZERO] * first2[ZERO]

    @pl.when((pl.program_id(ZERO) == ZERO) & (sc[TWO] != sc[4]))
    def _():
        out_ref[ZERO, ZERO] = w_ref[ZERO, ZERO] - rate[ZERO] * second2[ZERO]

    @pl.when((pl.program_id(ZERO) == ONE) & (sc[TWO] == sc[4]))
    def _():
        out_ref[ZERO, ZERO] = w_ref[ZERO, ZERO] - rate[ZERO] * first3[ZERO]

    @pl.when((pl.program_id(ZERO) == ONE) & (sc[TWO] != sc[4]))
    def _():
        out_ref[ZERO, ZERO] = w_ref[ZERO, ZERO] - rate[ZERO] * second3[ZERO]


def update_blocks(kernel, sc, rate, layer, near, w, grads, grad_specs, previous):
    def whole(s, j, sc):
        return layer, TWO * j + jnp.where(s == ZERO, sc[ZERO], ONE - sc[ZERO]), ZERO, (sc[ONE] if near else ONE - sc[ONE])

    block = pl.BlockSpec((ONE, ONE, LANES, FF_HALF), whole)
    in_specs = [pl.BlockSpec(memory_space=pltpu.SMEM), block] + grad_specs
    args = [sc, rate, w] + grads
    aliases = {}
    if previous is not None:
        in_specs.append(pl.BlockSpec(memory_space=pl.ANY))
        aliases = {len(args): ZERO}
        args.append(previous)
    return pl.pallas_call(
        kernel,
        grid_spec=pltpu.PrefetchScalarGridSpec(num_scalar_prefetch=ONE, grid=(TWO, 4), in_specs=in_specs, out_specs=block),
        out_shape=jax.ShapeDtypeStruct(w.shape, F32),
        input_output_aliases=aliases,
        compiler_params=params(TWO),
        cost_estimate=pl.CostEstimate(flops=2_000_000, bytes_accessed=11_000_000, transcendentals=ZERO),
    )(*args)


def early(s, j):
    return jnp.where(s == ZERO, j, 3)


def late(s, j):
    return jnp.where(s == ZERO, ZERO, j)


def update_near(sc, rate, layer, matrix, w, own, p1, previous=None):
    specs = [
        pl.BlockSpec((ONE, ONE, LANES, FF_HALF), lambda s, j, sc: (matrix, early(s, j), ZERO, ZERO)),
        pl.BlockSpec((ONE, ONE, LANES, FF_HALF), lambda s, j, sc: (matrix, late(s, j), ZERO, ZERO)),
    ]
    return update_blocks(update_near_kernel, sc, rate, layer, True, w, [own, p1], specs, previous)


def update_far(sc, rate, layer, matrix, w, rx2, ry2, rx3, ry3, previous):
    sc = jnp.concatenate([sc, jnp.full((ONE,), matrix, jnp.int32)])

    def spec(place, by_x):
        def index(s, j, sc):
            return jnp.where((sc[TWO] == sc[4]) == by_x, place(s, j), ZERO), ZERO, ZERO

        return pl.BlockSpec((ONE, LANES, FF_HALF), index)

    specs = [spec(early, True), spec(late, True), spec(early, False), spec(late, False)]
    return update_blocks(update_far_kernel, sc, rate, layer, False, w, [rx2, rx3, ry2, ry3], specs, previous)


def update_down_kernel(sc, rate, w_ref, own, p1, *rest):
    out_ref = rest[-ONE]
    s = pl.program_id(ZERO)

    @pl.when(s == ZERO)
    def _():
        out_ref[ZERO, ZERO] = w_ref[ZERO, ZERO] - rate[ZERO] * own[ZERO]

    @pl.when(s == ONE)
    def _():
        out_ref[ZERO, ZERO] = w_ref[ZERO, ZERO] - rate[ZERO] * p1[ZERO]


def update_down(sc, rate, layer, w, own, p1, previous=None):
    whole = lambda s, j, sc: (layer, TWO * j + jnp.where(s == ZERO, sc[ZERO], ONE - sc[ZERO]), ZERO, ZERO)
    in_specs = [
        pl.BlockSpec(memory_space=pltpu.SMEM),
        pl.BlockSpec((ONE, ONE, 448, WIDTH), whole),
        pl.BlockSpec((ONE, 448, WIDTH), lambda s, j, sc: (jnp.where(s == ZERO, j, 3), ZERO, ZERO)),
        pl.BlockSpec((ONE, 448, WIDTH), lambda s, j, sc: (jnp.where(s == ZERO, ZERO, j), ZERO, ZERO)),
    ]
    args = [sc, rate, w, own, p1]
    aliases = {}
    if previous is not None:
        in_specs.append(pl.BlockSpec(memory_space=pl.ANY))
        aliases = {len(args): ZERO}
        args.append(previous)
    return pl.pallas_call(
        update_down_kernel,
        grid_spec=pltpu.PrefetchScalarGridSpec(
            num_scalar_prefetch=ONE, grid=(TWO, 4), in_specs=in_specs, out_specs=pl.BlockSpec((ONE, ONE, 448, WIDTH), whole),
        ),
        out_shape=jax.ShapeDtypeStruct(w.shape, F32),
        input_output_aliases=aliases,
        compiler_params=params(TWO),
        cost_estimate=pl.CostEstimate(flops=4_000_000, bytes_accessed=22_000_000, transcendentals=ZERO),
    )(*args)


def update_head_kernel(sc, rate, w_ref, own, p1, rx2, ry2, rx3, ry3, out_ref):
    half = pl.program_id(ZERO) // (pl.num_programs(ZERO) // TWO)
    core, x, rep = sc[ZERO], sc[ONE], sc[TWO]
    lr = rate[ZERO]
    blocks = (
        (x, core, own[ALL]),
        (x, ONE - core, p1[ALL]),
        (ONE - x, core, jnp.where(half == rep, rx2[ALL], ry2[ALL])),
        (ONE - x, ONE - core, jnp.where(half == rep, rx3[ALL], ry3[ALL])),
    )
    for bx, bc, grad in blocks:
        cols = pl.ds(pl.multiple_of(head_start(bx, bc), LANES), HEAD_COLS)
        out_ref[:, cols] = w_ref[:, cols] - lr * grad


def update_head(sc, rate, w, own, p1, rx2, ry2, rx3, ry3):
    rows, vocab = w.shape
    step = 16
    count = rows // step
    inner = count // TWO
    return pl.pallas_call(
        update_head_kernel,
        grid_spec=pltpu.PrefetchScalarGridSpec(
            num_scalar_prefetch=ONE,
            grid=(count,),
            in_specs=[
                pl.BlockSpec(memory_space=pltpu.SMEM),
                pl.BlockSpec((step, vocab), lambda i, sc: (i, ZERO)),
                pl.BlockSpec((step, HEAD_COLS), lambda i, sc: (i, ZERO)),
                pl.BlockSpec((step, HEAD_COLS), lambda i, sc: (i, ZERO)),
            ] + [pl.BlockSpec((step, HEAD_COLS), lambda i, sc: (i % inner, ZERO))] * 4,
            out_specs=pl.BlockSpec((step, vocab), lambda i, sc: (i, ZERO)),
        ),
        out_shape=jax.ShapeDtypeStruct(w.shape, F32),
        compiler_params=params(ONE),
        cost_estimate=pl.CostEstimate(flops=8_000_000, bytes_accessed=50_000_000, transcendentals=ZERO),
    )(sc, rate, w, own, p1, rx2, ry2, rx3, ry3)


def update_embedding_kernel(sc, rate, ids_ref, d_ref, w_ref, out_ref):
    rows = w_ref.shape[ZERO]
    first = sc[3] * (pl.num_programs(ZERO) * rows) + pl.program_id(ZERO) * rows
    index = lax.broadcasted_iota(jnp.int32, (rows, ids_ref.shape[ONE]), ZERO) + first
    onehot = jnp.where(index == ids_ref[ALL], 1.0, 0.0).astype(BF16)
    out_ref[ALL] = w_ref[ALL] - rate[ZERO] * dot_nn(onehot, d_ref[ALL])


def update_embedding(sc, rate, ids, d_rows, w):
    rows, width = w.shape
    step = 400
    tokens = d_rows.shape[ZERO]
    return pl.pallas_call(
        update_embedding_kernel,
        grid_spec=pltpu.PrefetchScalarGridSpec(
            num_scalar_prefetch=ONE,
            grid=(rows // step,),
            in_specs=[
                pl.BlockSpec(memory_space=pltpu.SMEM),
                pl.BlockSpec((ONE, tokens), lambda i, sc: (ZERO, ZERO)),
                pl.BlockSpec((tokens, width), lambda i, sc: (ZERO, ZERO)),
                pl.BlockSpec((step, width), lambda i, sc: (i, ZERO)),
            ],
            out_specs=pl.BlockSpec((step, width), lambda i, sc: (i, ZERO)),
        ),
        out_shape=jax.ShapeDtypeStruct(w.shape, F32),
        compiler_params=params(ONE),
        cost_estimate=pl.CostEstimate(flops=17_000_000_000, bytes_accessed=35_000_000, transcendentals=ZERO),
    )(sc, rate, ids, d_rows, w)


def peer_of(rep, me, other_rep, k):
    across = (me, me + ONE - TWO * (me % TWO), (me + TWO) % 4, 3 - me)[k]
    return (ONE - rep if other_rep else rep), across


def exchange_kernel(both, in_ref, out_ref, send_sem, recv_sem):
    rep, me = lax.axis_index(REP), lax.axis_index(FSDP)
    slot = rep * 4 + me if both else me
    peers = [(other, k) for other in ((False, True) if both else (False,)) for k in range(4) if other or k]
    barrier = pltpu.get_barrier_semaphore()
    for other, k in peers:
        pl.semaphore_signal(barrier, inc=ONE, device_id=peer_of(rep, me, other, k), device_id_type=pl.DeviceIdType.MESH)
    pl.semaphore_wait(barrier, len(peers))
    copies = []
    for n, (other, k) in enumerate(peers):
        copy = pltpu.make_async_remote_copy(
            src_ref=in_ref, dst_ref=out_ref.at[slot], send_sem=send_sem.at[n], recv_sem=recv_sem.at[n],
            device_id=peer_of(rep, me, other, k), device_id_type=pl.DeviceIdType.MESH)
        copy.start()
        copies.append(copy)
    out_ref[slot] = in_ref[ALL]
    for copy in copies:
        copy.wait()


def exchange(value, both, collective_id):
    count = 8 if both else 4
    return pl.pallas_call(
        functools.partial(exchange_kernel, both),
        in_specs=[pl.BlockSpec(memory_space=pltpu.VMEM)],
        out_specs=pl.BlockSpec(memory_space=pltpu.VMEM),
        out_shape=jax.ShapeDtypeStruct((count,) + value.shape, value.dtype),
        scratch_shapes=[pltpu.SemaphoreType.DMA((count - ONE,)), pltpu.SemaphoreType.DMA((count - ONE,))],
        compiler_params=pltpu.CompilerParams(collective_id=collective_id, has_side_effects=True),
        cost_estimate=pl.CostEstimate(flops=1_000_000_000, bytes_accessed=100_000, transcendentals=ZERO),
        name="exchange",
    )(value)


def row_major(value):
    return with_layout_constraint(value, Layout(major_to_minor=(ZERO, ONE)))


def to_peer(value, k):
    return lax.ppermute(value, FSDP, [(i, i ^ k) for i in range(4)])


def to_replica(value):
    return lax.ppermute(value, REP, [(ZERO, ONE), (ONE, ZERO)])


def solution(mesh):
    batch_spec = P((REP, FSDP))
    layer_spec = P(None, FSDP)
    expert_spec = P(None, None, FSDP)
    param_specs = (P(FSDP), layer_spec, layer_spec, layer_spec, layer_spec, layer_spec, layer_spec, layer_spec, expert_spec, expert_spec, expert_spec, P(FSDP), P(FSDP))
    in_specs = (batch_spec, batch_spec, batch_spec, P(None, (REP, FSDP)), P()) + param_specs
    out_specs = param_specs + (P(),)

    def train_step(tok_ids, tok_labels, tok_pos, expert_idx, learn_rate, embedding, w_query, w_key, w_value, w_attn_out, g_attn, g_mlp, w_router, w_gate, w_up, w_down, g_final, w_head):
        me = lax.axis_index(FSDP)
        rep = lax.axis_index(REP)
        core, x = me % TWO, me // TWO
        place = jnp.stack([core, x, rep, me]).astype(jnp.int32)
        rate = learn_rate.reshape(ONE)
        layers = w_query.shape[ZERO]
        length = tok_ids.shape[ONE]
        tokens = 8 * length
        cos_tab, sin_tab = rope_tables(tok_pos[ZERO])

        packed = jnp.concatenate([tok_ids, tok_labels, expert_idx[ZERO, ZERO].T, expert_idx[ONE, ZERO].T, tok_ids, tok_labels], axis=ZERO)
        packed = exchange(packed, True, ZERO)
        all_ids, all_labels = packed[:, ZERO].reshape(-ONE), packed[:, ONE].reshape(-ONE, ONE)
        group = tokens // TWO
        chosen_all = [packed[:, TWO + TWO * layer:4 + TWO * layer].transpose(ONE, ZERO, TWO).reshape(TWO, tokens) for layer in range(layers)]
        before = (lax.broadcasted_iota(jnp.int32, (group, group), ZERO) < lax.broadcasted_iota(jnp.int32, (group, group), ONE)).astype(BF16)
        routes = []
        for layer in range(layers):
            experts = lax.broadcasted_iota(jnp.int32, (8, tokens), ZERO)
            mask = ((experts == chosen_all[layer][:ONE]) | (experts == chosen_all[layer][ONE:])).reshape(8, TWO, group).transpose(ONE, ZERO, TWO)
            rank = lax.dot_general(mask.astype(BF16), before, (((TWO,), (ZERO,)), ((), ())), preferred_element_type=F32).astype(jnp.int32)
            rank = jnp.where(mask, rank, -ONE)
            counts = jnp.sum(mask.astype(jnp.int32), axis=TWO).reshape(-ONE)
            routes.append((jnp.concatenate([place, counts]), rank, rank.transpose(ZERO, TWO, ONE)))
        sc = routes[ZERO][ZERO]

        def own_group(values, axis=ZERO):
            return lax.dynamic_slice_in_dim(values, rep * group, group, axis)

        def relay(value, k):
            rx = to_peer(value, k)
            return rx, to_replica(rx)

        def near(value):
            return to_peer(value, ONE)

        def send_experts(layer):
            gu1, mine2, mine3, wd1 = pack_experts(place, layer, w_gate, w_up, w_down)
            pieces = (near(gu1), *relay(mine2, TWO), *relay(mine3, 3))
            return pieces, near(wd1)

        def send_head():
            own, p1, mine2, mine3 = pack_head(place, w_head)
            return [own, near(p1), *relay(mine2, TWO), *relay(mine3, 3)]

        final_col = jnp.stack([g_final, jnp.zeros_like(g_final)])[:, :, None]
        small = jnp.concatenate([w_query, w_key, w_value, w_attn_out, w_router, g_attn[:, :, None], g_mlp[:, :, None], final_col], axis=TWO)
        whole = []
        for layer in range(layers):
            whole.append(lax.all_gather(small[layer].astype(BF16), FSDP, axis=ZERO, tiled=True))
        cuts = (ZERO, WIDTH, 640, 768, 1280, 1288, 1289, 1290, 1291)

        def small_param(layer, slot):
            value = whole[layer][:, cuts[slot]:cuts[slot + ONE]]
            return value[:, ZERO] if slot >= 5 else value

        def attention_params(layer):
            return whole[layer][:, :cuts[3]], whole[layer][:, cuts[3]:cuts[4]], small_param(layer, 5)

        local = own_group(all_ids) - me * embedding.shape[ZERO]
        owned = (local >= ZERO) & (local < embedding.shape[ZERO])
        rows = jnp.take(embedding, jnp.clip(local, ZERO, embedding.shape[ZERO] - ONE), axis=ZERO)
        rows = jnp.where(owned[:, None], rows, 0.0).astype(BF16)
        residual = row_major(lax.psum_scatter(rows, FSDP, scatter_dimension=ZERO, tiled=True).astype(F32))

        sent = [send_experts(layer) for layer in range(layers)]
        head_pieces = send_head()
        saved = []
        for layer in range(layers):
            w_r, gain_m = small_param(layer, 4), small_param(layer, 6)
            residual, attn_vjp = jax.vjp(functools.partial(attention_part, cos_tab=cos_tab, sin_tab=sin_tab), residual, *attention_params(layer))

            def routed(*values, layer=layer):
                return router_part(*values, chosen=expert_idx[layer, ZERO].T)

            (b, _), router_vjp = jax.vjp(routed, residual, gain_m, w_r)
            b_group = lax.all_gather(row_major(b), FSDP, axis=ZERO, tiled=True)
            b_other = to_replica(b_group)
            comb = combine_weights(router_logits(b_group, w_r), own_group(chosen_all[layer], ONE))
            pieces, wd1 = sent[layer]
            partial = expert_forward(sc, layer, b_group, comb.T, w_gate, w_up, pieces, w_down, wd1)
            residual = row_major(residual + lax.psum_scatter(partial, FSDP, scatter_dimension=ZERO, tiled=True))
            saved.append((attn_vjp, router_vjp, b_group, b_other, comb, w_r))

        others, residual = lax.optimization_barrier(([entry[3] for entry in saved], residual))
        comb_others = []
        for layer in range(layers):
            other = lax.dynamic_slice_in_dim(chosen_all[layer], (ONE - rep) * group, group, ONE)
            comb_others.append(combine_weights(router_logits(others[layer], saved[layer][5]), other))
        final, final_vjp = jax.vjp(rms_norm, residual, small_param(ZERO, 7))
        x_all = lax.all_gather(row_major(final), (REP, FSDP), axis=ZERO, tiled=True)
        stats = head_stats(sc, x_all, head_pieces)
        stats = exchange(stats.T, False, ONE)
        peak = jnp.max(stats[:, ZERO], axis=ZERO)
        lse = peak + jnp.log(jnp.sum(stats[:, ONE] * jnp.exp(stats[:, ZERO] - peak), axis=ZERO))
        dl, dx, picked = head_dx(sc, x_all, all_labels, lse[:, None], head_pieces)
        dh0, dh1, dh2, dh3 = head_dw(sc, x_all.T, dl)
        d_final = row_major(lax.psum_scatter(dx, FSDP, scatter_dimension=ZERO, tiled=True))
        d_residual, d_gain_final = final_vjp(d_final.astype(BF16))
        head_returns = [near(dh1), *relay(dh2, TWO), *relay(dh3, 3)]
        new_head = update_head(sc, rate, w_head, dh0, *head_returns)

        small_grads = [None] * layers
        new_gate = new_up = new_down = None
        for layer in reversed(range(layers)):
            attn_vjp, router_vjp, b_group, _, comb, _ = saved[layer]
            d_all = lax.all_gather(row_major(d_residual), (REP, FSDP), axis=ZERO, tiled=True)
            pieces, wd1 = sent[layer]
            scalars, ranks, rank_cols = routes[layer]
            db = expert_dgrad(scalars, layer, b_group, d_all, ranks, rank_cols, comb, w_gate, w_up, pieces, w_down, wd1)
            own, near1, far2, far3, down_own, down_other = expert_wgrad(scalars, layer, b_group, others[layer], d_all, ranks, comb, comb_others[layer], w_gate, w_up, pieces, w_down, wd1)
            returned = (*relay(far2, TWO), *relay(far3, 3))
            gu1 = near(near1)
            down1 = near(down_other)
            new_gate = update_near(place, rate, layer, ZERO, w_gate, own, gu1, new_gate)
            new_up = update_near(place, rate, layer, ONE, w_up, own, gu1, new_up)
            new_gate = update_far(place, rate, layer, ZERO, w_gate, *returned, new_gate)
            new_up = update_far(place, rate, layer, ONE, w_up, *returned, new_up)
            new_down = update_down(sc, rate, layer, w_down, down_own, down1, previous=new_down)
            db = row_major(lax.psum_scatter(db, FSDP, scatter_dimension=ZERO, tiled=True))
            d_router_in, d_gain_m, d_wr = router_vjp((db[:, :WIDTH].astype(BF16), db[:, WIDTH:520].T))
            d_residual = d_residual + d_router_in
            d_residual, d_wqkv, d_wo, d_gain_a = attn_vjp(d_residual)
            extra = d_gain_final if layer == ZERO else jnp.full_like(d_gain_final, ZERO, F32) + jnp.sum(picked)
            grads = [d_wqkv, d_wo, d_wr, d_gain_a[:, None], d_gain_m[:, None], extra[:, None]]
            grads = jnp.concatenate([g.astype(F32) for g in grads], axis=ONE)
            if layer + ONE < layers:
                grads, small_grads[layer + ONE] = lax.optimization_barrier((grads, small_grads[layer + ONE]))
            grads = lax.psum_scatter(grads, FSDP, scatter_dimension=ZERO, tiled=True)
            small_grads[layer] = lax.psum(grads, REP)

        d_rows = lax.all_gather(row_major(d_residual.astype(BF16)), (REP, FSDP), axis=ZERO, tiled=True)
        new_embedding = update_embedding(sc, rate, all_ids[None, :], d_rows, embedding)

        small_grad = jnp.stack(small_grads)
        new_small = small - learn_rate * small_grad
        mean_loss = (jnp.sum(lse) - small_grad[ONE, ZERO, 1290] / TWO) / tokens

        def new_param(slot):
            value = new_small[:, :, cuts[slot]:cuts[slot + ONE]]
            return value[:, :, ZERO] if slot >= 5 else value

        return (new_embedding, new_param(ZERO), new_param(ONE), new_param(TWO), new_param(3), new_param(5), new_param(6), new_param(4),
                new_gate, new_up, new_down, new_param(7)[ZERO], new_head, mean_loss)


    return jax.shard_map(train_step, mesh=mesh, in_specs=in_specs, out_specs=out_specs, check_vma=False)
```

time: 1280 us -> 1280 us (level)
  Pallas kernels: 442 us -> 462 us
    ppermute x22, waiting for transfers between devices: 309 us -> 334 us  [to_peer(): return lax.ppermute(value, FSDP, [(i, i ^ k) for i in range(4)])]
    pallas_call x4 -> x8, Pallas kernels: 45 us -> 64.4 us  [update_blocks(): pl.pallas_call(kernel, grid_spec=pltpu.PrefetchScalarGridSpec(num_scalar_...]
    reduce_scatter x7 -> x8, waiting for transfers between devices: 137 us -> 118 us  [the longest x2 46.1 us: train_step(): lax.psum_scatter(partial, FSDP, scatter_dimension=ZERO, tiled=True)]
    all_gather x8, waiting for transfers between devices: 62 us -> 45.6 us  [the longest x2 45.6 us: train_step(): lax.all_gather(row_major(d_residual), (REP, FSDP), axis=ZERO, tiled=True)]
    dot_general x30 -> x18, matrix products: 35.6 us -> 24.6 us  [the longest x10 14.5 us: router_logits(): lax.dot_general(w_r, normed, (((ZERO,), (ONE,)), ((), ())), preferred_ele...]
  transfers between devices with their start and end apart: 52 -> 54, of which waited for: 27 -> 25; matrix products, arithmetic and copies ran while one was open for 5% -> 7% of each run, Pallas kernels for 22% -> 26%
where the time goes in v2:
time: 1280 us; the launch traced here: 1260 us
  waiting for transfers between devices  597 us (47%)
  Pallas kernels  462 us (36%)
  local copies, waits for them, and re-layouts  75.1 us (6%)
  matrix products  43.1 us (3%)
  other arithmetic  36.5 us (3%)
  starting transfers between devices  29.6 us (2%)
  between operations  20.2 us (2%)
    ppermute x22, waiting for transfers between devices, to_peer(): return lax.ppermute(value, FSDP, [(i, i ^ k) for i in range(4)])  334 us
    pallas_call x2, Pallas kernels, expert_wgrad(): pl.pallas_call(expert_wgrad_kernel, grid_spec=pltpu.PrefetchScalarGridSpe...  83.8 us
    ppermute x14, waiting for transfers between devices, to_replica(): return lax.ppermute(value, REP, [(ZERO, ONE), (ONE, ZERO)])  82.2 us
    pallas_call x8, Pallas kernels, update_blocks(): pl.pallas_call(kernel, grid_spec=pltpu.PrefetchScalarGridSpec(num_scalar_...  64.4 us
    pallas_call x2, Pallas kernels, expert_dgrad(): pl.pallas_call(expert_dgrad_kernel, grid_spec=pltpu.PrefetchScalarGridSpe...  57.7 us
    pallas_call x1, Pallas kernels, head_dx(): pl.pallas_call(head_dx_kernel, grid_spec=pltpu.PrefetchScalarGridSpec(num...  46.7 us
    reduce_scatter x2, waiting for transfers between devices, train_step(): lax.psum_scatter(partial, FSDP, scatter_dimension=ZERO, tiled=True)  46.1 us
    all_gather x2, waiting for transfers between devices, train_step(): lax.all_gather(row_major(d_residual), (REP, FSDP), axis=ZERO, tiled=True)  45.6 us
  transfers between devices with their start and end apart: 54, of which 25 were waited for; matrix products, arithmetic and copies ran while one was open for 7% of the time, Pallas kernels for 26%

profile of v2, /device:TPU:0, one launch (start us, length us, event | category | flops | bytes accessed | tf_op | source)
XLA Modules:
  0.0 1263.3 jit_solution(10261211751073658868)
XLA Ops:
  77.8 26.3 %collective-permute-done.2.rx2 = bf16[4,128,896]{2,1,0:T(8,128)(2,1)} collective-permute-done((bf16[4,128,896]{2,1,0:T(8,128)(2,1)}, bf16[4,128,896]{2,1,0:T(8,128)(2,1)}, u32[]{:S(2)}, u32[]{:S(2)}) %collective-permute-start.2) | collective-permute-done | bytes 917536 | tf_op jit(solution)/shard_map/ppermute | solution.py:883
  168.7 23.5 %reduce-scatter.11.cloned.1.call-done = f32[256,512]{1,0:T(8,128)} async-done(((f32[1024,512]{1,0:T(8,128)}), f32[256,512]{1,0:T(8,128)}) %reduce-scatter.11.cloned.1.call-update) | async-done | bytes 524304 | tf_op jit(solution)/shard_map/reduce_scatter | solution.py:980
  217.2 22.4 %collective-permute-done.9.rx2 = bf16[4,128,896]{2,1,0:T(8,128)(2,1)S(1)} collective-permute-done((bf16[4,128,896]{2,1,0:T(8,128)(2,1)}, bf16[4,128,896]{2,1,0:T(8,128)(2,1)S(1)}, u32[]{:S(2)}, u32[]{:S(2)}) %collective-permute-start.9) | collective-permute-done | bytes 917536 | tf_op jit(solution)/shard_map/ppermute | solution.py:883
  283.0 19.0 %shard_map.284 = f32[1024,512]{1,0:T(8,128)} custom-call(s32[20]{0:T(128)} %concatenate.62.sc, bf16[1024,512]{1,0:T(8,128)(2,1)} %all-gather.13.cloned.1.call-done.b_ref.b_own, f32[1024,8]{1,0:T(8,128)} %select_add_fusion.comb_ref, f32[2,8,128,1792]{3,2,1,0:T(8,128)} %w_ref.18, f32[2,8,128,1792]{3,2,1,0:T(8,128)} %w_ref.22, ...), custom_call_target="tpu_custom_call" | custom-call | flops 11299999744 | bytes 20000000 | tf_op jit(solution)/shard_map/pallas_call | solution.py:235
  305.3 22.6 %reduce-scatter.13.cloned.1.call-done = f32[256,512]{1,0:T(8,128)} async-done(((f32[1024,512]{1,0:T(8,128)}), f32[256,512]{1,0:T(8,128)}) %reduce-scatter.13.cloned.1.call-update) | async-done | bytes 524304 | tf_op jit(solution)/shard_map/reduce_scatter | solution.py:980
  329.4 21.1 %collective-permute-done.7.b_other = bf16[1024,512]{1,0:T(8,128)(2,1)} collective-permute-done((bf16[1024,512]{1,0:T(8,128)(2,1)S(1)}, bf16[1024,512]{1,0:T(8,128)(2,1)}, u32[]{:S(2)}, u32[]{:S(2)}) %collective-permute-start.7) | collective-permute-done | bytes 1048608 | tf_op jit(solution)/shard_map/ppermute | solution.py:887
  365.3 29.8 %collective-permute-done.15.rx2 = bf16[64,8192]{1,0:T(8,128)(2,1)} collective-permute-done((bf16[64,8192]{1,0:T(8,128)(2,1)}, bf16[64,8192]{1,0:T(8,128)(2,1)}, u32[]{:S(2)}, u32[]{:S(2)}) %collective-permute-start.15) | collective-permute-done | bytes 1048608 | tf_op jit(solution)/shard_map/ppermute | solution.py:883
  439.6 30.8 %shard_map.286 = f32[2048,8]{1,0:T(8,128)} custom-call(s32[20]{0:T(128)} %concatenate.62.sc, bf16[2048,512]{1,0:T(8,128)(2,1)} %copy.192.x_ref, bf16[128,8192]{1,0:T(8,128)(2,1)} %get-tuple-element.59.own, bf16[128,8192]{1,0:T(8,128)(2,1)} %copy-done.139, bf16[64,8192]{1,0:T(8,128)(2,1)} %collective-permute-done.15.rx2, ...), custom_call_target="tpu_custom_call" | custom-call | flops 16999999488 | bytes 25000000 | tf_op jit(solution)/shard_map/pallas_call | solution.py:518
  484.2 46.7 %shard_map.287 = (bf16[2048,8192]{1,0:T(8,128)(2,1)}, f32[1024,512]{1,0:T(8,128)}, f32[8,128]{1,0:T(8,128)}) custom-call(s32[20]{0:T(128)} %concatenate.62.sc, bf16[2048,512]{1,0:T(8,128)(2,1)} %copy.192.x_ref, s32[2048,1]{1,0:T(8,128)} %copy.193.label_ref, f32[2048,1]{1,0:T(8,128)} %copy.194.lse_ref, bf16[128,8192]{1,0:T(8,128)(2,1)} %get-tuple-element.59.own, ...), custom_call_target="tpu_custom_call" | custom-call | flops 25999998976 | bytes 60000000 | tf_op jit(solution)/shard_map/pallas_call | solution.py:589
  531.0 26.2 %reduce-scatter.15.cloned.1.call-done = f32[256,512]{1,0:T(8,128)} async-done(((f32[1024,512]{1,0:T(8,128)}), f32[256,512]{1,0:T(8,128)}) %reduce-scatter.15.cloned.1.call-update) | async-done | bytes 524304 | tf_op jit(solution)/shard_map/reduce_scatter | solution.py:996
  565.0 27.3 %all-gather.17.cloned.1.call-done.d_ref.d_own.d_other = f32[2048,512]{1,0:T(8,128)} async-done(((f32[256,512]{1,0:T(8,128)}), f32[2048,512]{1,0:T(8,128)}) %all-gather.17.cloned.1.call-update) | async-done | bytes 4194320 | tf_op jit(solution)/shard_map/all_gather | solution.py:1005
  592.2 27.2 %shard_map.288 = f32[1024,640]{1,0:T(8,128)} custom-call(s32[20]{0:T(128)} %concatenate.68.sc, bf16[1024,512]{1,0:T(8,128)(2,1)} %all-gather.13.cloned.1.call-done.b_ref.b_own, f32[2048,512]{1,0:T(8,128)} %all-gather.17.cloned.1.call-done.d_ref.d_own.d_other, s32[2,8,1024]{2,1,0:T(8,128)} %get-tuple-element.224.rank_ref, s32[2,1024,8]{2,1,0:T(8,128)} %copy.195.rank_col_ref, ...), custom_call_target="tpu_custom_call" | custom-call | flops 15000000512 | bytes 25000000 | tf_op jit(solution)/shard_map/pallas_call | solution.py:331
  620.9 27.8 %reduce-scatter.17.cloned.1.call-done = f32[256,640]{1,0:T(8,128)} async-done(((f32[1024,640]{1,0:T(8,128)}), f32[256,640]{1,0:T(8,128)}) %reduce-scatter.17.cloned.1.call-update) | async-done | bytes 655376 | tf_op jit(solution)/shard_map/reduce_scatter | solution.py:1018
  699.2 30.5 %shard_map.289 = f32[1024,640]{1,0:T(8,128)} custom-call(s32[20]{0:T(128)} %concatenate.62.sc, bf16[1024,512]{1,0:T(8,128)(2,1)} %all-gather.11.cloned.1.call-done.b_ref.b_own, f32[2048,512]{1,0:T(8,128)} %all-gather.19.cloned.1.call-done.d_ref.d_own.d_other, s32[2,8,1024]{2,1,0:T(8,128)} %get-tuple-element.222.rank_ref, s32[2,1024,8]{2,1,0:T(8,128)} %copy.205.rank_col_ref, ...), custom_call_target="tpu_custom_call" | custom-call | flops 15000000512 | bytes 25000000 | tf_op jit(solution)/shard_map/pallas_call | solution.py:331
  729.8 27.1 %shard_map.303 = (f32[128,8192]{1,0:T(8,128)}, f32[128,8192]{1,0:T(8,128)}, f32[64,8192]{1,0:T(8,128)}, f32[64,8192]{1,0:T(8,128)}) custom-call(s32[20]{0:T(128)} %concatenate.62.sc, bf16[512,2048]{1,0:T(8,128)(2,1)} %bitcast.308, bf16[2048,8192]{1,0:T(8,128)(2,1)} %get-tuple-element.81.dl_ref), custom_call_target="tpu_custom_call" | custom-call | flops 12999999488 | bytes 52000000 | tf_op jit(solution)/shard_map/pallas_call | solution.py:629
  761.6 49.3 %collective-permute-done.32.rx2 = f32[64,8192]{1,0:T(8,128)} collective-permute-done((f32[64,8192]{1,0:T(8,128)}, f32[64,8192]{1,0:T(8,128)}, u32[]{:S(2)}, u32[]{:S(2)}) %collective-permute-start.32) | collective-permute-done | bytes 2097184 | tf_op jit(solution)/shard_map/ppermute | solution.py:883
  855.8 40.8 %shard_map.292 = (f32[2,4,128,896]{3,2,1,0:T(8,128)}, f32[2,4,128,896]{3,2,1,0:T(8,128)}, f32[4,128,896]{2,1,0:T(8,128)}, f32[4,128,896]{2,1,0:T(8,128)}, f32[4,...) custom-call(s32[20]{0:T(128)} %concatenate.68.sc, bf16[1024,512]{1,0:T(8,128)(2,1)} %all-gather.13.cloned.1.call-done.b_ref.b_own, ...), custom_call_target="tpu_custom_call" | custom-call | flops 30000001024 | bytes 50000000 | tf_op jit(solution)/shard_map/pallas_call | solution.py:412
  901.6 38.2 %collective-permute-done.24.first2 = f32[4,128,896]{2,1,0:T(8,128)S(1)} collective-permute-done((f32[4,128,896]{2,1,0:T(8,128)}, f32[4,128,896]{2,1,0:T(8,128)S(1)}, u32[]{:S(2)}, u32[]{:S(2)}) %collective-permute-start.24) | collective-permute-done | bytes 1835040 | tf_op jit(solution)/shard_map/ppermute | solution.py:883
  939.9 36.9 %collective-permute-done.25.first3 = f32[4,128,896]{2,1,0:T(8,128)} collective-permute-done((f32[4,128,896]{2,1,0:T(8,128)}, f32[4,128,896]{2,1,0:T(8,128)}, u32[]{:S(2)}, u32[]{:S(2)}) %collective-permute-start.25) | collective-permute-done | bytes 1835040 | tf_op jit(solution)/shard_map/ppermute | solution.py:883
  977.3 43.0 %shard_map.291 = (f32[2,4,128,896]{3,2,1,0:T(8,128)}, f32[2,4,128,896]{3,2,1,0:T(8,128)}, f32[4,128,896]{2,1,0:T(8,128)}, f32[4,128,896]{2,1,0:T(8,128)}, f32[4,...) custom-call(s32[20]{0:T(128)} %concatenate.62.sc, bf16[1024,512]{1,0:T(8,128)(2,1)} %all-gather.11.cloned.1.call-done.b_ref.b_own, ...), custom_call_target="tpu_custom_call" | custom-call | flops 30000001024 | bytes 50000000 | tf_op jit(solution)/shard_map/pallas_call | solution.py:412
  1030.0 42.0 %collective-permute-done.19.first2 = f32[4,128,896]{2,1,0:T(8,128)} collective-permute-done((f32[4,128,896]{2,1,0:T(8,128)}, f32[4,128,896]{2,1,0:T(8,128)}, u32[]{:S(2)}, u32[]{:S(2)}) %collective-permute-start.19) | collective-permute-done | bytes 1835040 | tf_op jit(solution)/shard_map/ppermute | solution.py:883
  1073.6 36.7 %collective-permute-done.20.first3 = f32[4,128,896]{2,1,0:T(8,128)S(1)} collective-permute-done((f32[4,128,896]{2,1,0:T(8,128)}, f32[4,128,896]{2,1,0:T(8,128)S(1)}, u32[]{:S(2)}, u32[]{:S(2)}) %collective-permute-start.20) | collective-permute-done | bytes 1835040 | tf_op jit(solution)/shard_map/ppermute | solution.py:883
  1113.6 19.8 %shard_map.304 = f32[128,32000]{1,0:T(8,128)} custom-call(s32[20]{0:T(128)} %concatenate.62.sc, f32[1]{0:T(128)} %bitcast.283.rate, f32[128,32000]{1,0:T(8,128)} %w_ref.25, f32[128,8192]{1,0:T(8,128)} %get-tuple-element.82.own, f32[128,8192]{1,0:T(8,128)} %collective-permute-done.31.p1, f32[64,8192]{1,0:T(8,128)} %collective-permute-done.32.rx2, ...), custom_call_target="tpu_custom_call" | custom-call | flops 8000000 | bytes 50000000 | tf_op jit(solution)/shard_map/pallas_call | solution.py:789
  1221.0 28.5 %shard_map.290 = f32[8000,512]{1,0:T(8,128)} custom-call(s32[20]{0:T(128)} %concatenate.62.sc, f32[1]{0:T(128)} %bitcast.272.rate, s32[1,2048]{1,0:T(1,128)} %bitcast.377, bf16[2048,512]{1,0:T(8,128)(2,1)} %all-gather.21.cloned.1.call-done.d_ref, f32[8000,512]{1,0:T(8,128)} %w_ref.14), custom_call_target="tpu_custom_call" | custom-call | flops 16999999488 | bytes 35000000 | tf_op jit(solution)/shard_map/pallas_call | solution.py:820
  (608 shorter events, 499.5 us)
Async XLA Ops:
  35.0 89.5 %all-gather.11.cloned.1.call-start = ((), (), s32[]{:S(2)}) async-start(), calls=%async_computation.9 | async-start | bytes 1310720 | tf_op jit(solution)/shard_map/all_gather | solution.py:975
  63.7 103.1 %all-gather.25.cloned.1.call-start = ((), (), s32[]{:S(2)}) async-start(), calls=%async_computation.25 | async-start | bytes 1802240 | tf_op jit(solution)/shard_map/all_gather | solution.py:948
  74.6 117.6 %reduce-scatter.11.cloned.1.call-start = ((), (), s32[]{:S(2)}) async-start(), calls=%async_computation.10 | async-start | bytes 2621440 | tf_op jit(solution)/shard_map/reduce_scatter | solution.py:980
  166.5 93.7 %all-gather.13.cloned.1.call-start = ((), (), s32[]{:S(2)}) async-start(), calls=%async_computation.11 | async-start | bytes 1310720 | tf_op jit(solution)/shard_map/all_gather | solution.py:975
  207.1 120.8 %reduce-scatter.13.cloned.1.call-start = ((), (), s32[]{:S(2)}) async-start(), calls=%async_computation.12 | async-start | bytes 2621440 | tf_op jit(solution)/shard_map/reduce_scatter | solution.py:980
  302.1 114.0 %all-gather.15.cloned.1.call-start = ((), (), s32[]{:S(2)}) async-start(), calls=%async_computation.13 | async-start | bytes 2359296 | tf_op jit(solution)/shard_map/all_gather | solution.py:989
  351.7 205.5 %reduce-scatter.15.cloned.1.call-start = ((), (), s32[]{:S(2)}) async-start(), calls=%async_computation.14 | async-start | bytes 2621440 | tf_op jit(solution)/shard_map/reduce_scatter | solution.py:996
  561.0 87.6 %reduce-scatter.17.cloned.1.call-start = ((), (), s32[]{:S(2)}) async-start(), calls=%async_computation.16 | async-start | bytes 3276800 | tf_op jit(solution)/shard_map/reduce_scatter | solution.py:1018
  668.0 143.7 %reduce-scatter.21.cloned.1.call-start = ((), (), s32[]{:S(2)}) async-start(), calls=%async_computation.20 | async-start | bytes 3604480 | tf_op jit(solution)/shard_map/reduce_scatter | solution.py:1027
  678.2 133.6 %reduce-scatter.19.cloned.1.call-start = ((), (), s32[]{:S(2)}) async-start(), calls=%async_computation.18 | async-start | bytes 3276800 | tf_op jit(solution)/shard_map/reduce_scatter | solution.py:1018
  729.7 125.7 %all-reduce.20.cloned.1.call-start = ((), (), s32[]{:S(2)}) async-start(), calls=%async_computation.21 | async-start | bytes 1441792 | tf_op jit(solution)/shard_map/psum | solution.py:1028
  761.6 139.0 %collective-permute-start.34 = (f32[64,8192]{1,0:T(8,128)}, f32[64,8192]{1,0:T(8,128)}, u32[]{:S(2)}, u32[]{:S(2)}) collective-permute-start(f32[64,8192]{1,0:T(8,128)} %get-tuple-element.85), channel_id=1, source_target_pairs={{0,3},{1,2},{2,1},{3,0},{4,7},{5,6},{6,5},{7,4}} | collective-permute-start | bytes 6291464 | tf_op jit(solution)/shard_map/ppermute | solution.py:883
  810.9 90.4 %collective-permute-start.33 = (f32[64,8192]{1,0:T(8,128)}, f32[64,8192]{1,0:T(8,128)}, u32[]{:S(2)}, u32[]{:S(2)}) collective-permute-start(f32[64,8192]{1,0:T(8,128)} %collective-permute-done.32.rx2), channel_id=1, source_target_pairs={{0,4},{4,0},{1,5},{5,1},{2,6},{6,2},{3,7},{7,3}} | collective-permute-start | bytes 6291464 | tf_op jit(solution)/shard_map/ppermute | solution.py:887
  811.7 409.2 %reduce-scatter.23.cloned.1.call-start = ((), (), s32[]{:S(2)}) async-start(), calls=%async_computation.22 | async-start | bytes 3604480 | tf_op jit(solution)/shard_map/reduce_scatter | solution.py:1027
  855.5 365.5 %all-gather.21.cloned.1.call-start = ((), (), s32[]{:S(2)}) async-start(), calls=%async_computation.19 | async-start | bytes 2359296 | tf_op jit(solution)/shard_map/all_gather | solution.py:1030
  898.0 122.4 %collective-permute-start.31 = (f32[128,8192]{1,0:T(8,128)}, f32[128,8192]{1,0:T(8,128)}, u32[]{:S(2)}, u32[]{:S(2)}) collective-permute-start(f32[128,8192]{1,0:T(8,128)} %get-tuple-element.83), channel_id=1, source_target_pairs={{0,1},{1,0},{2,3},{3,2},{4,5},{5,4},{6,7},{7,6}} | collective-permute-start | bytes 12582920 | tf_op jit(solution)/shard_map/ppermute | solution.py:883
  900.6 127.7 %collective-permute-start.28 = (f32[2,4,128,896]{3,2,1,0:T(8,128)}, f32[2,4,128,896]{3,2,1,0:T(8,128)}, u32[]{:S(2)}, u32[]{:S(2)}) collective-permute-start(f32[2,4,128,896]{3,2,1,0:T(8,128)} %get-tuple-element.76), channel_id=1, source_target_pairs={{0,1},{1,0},{2,3},{3,2},{4,5},{5,4},{6,7},{7,6}} | collective-permute-start | bytes 11010056 | tf_op jit(solution)/shard_map/ppermute | solution.py:883
  901.3 119.1 %collective-permute-start.35 = (f32[64,8192]{1,0:T(8,128)}, f32[64,8192]{1,0:T(8,128)}, u32[]{:S(2)}, u32[]{:S(2)}) collective-permute-start(f32[64,8192]{1,0:T(8,128)} %collective-permute-done.34.rx3), channel_id=1, source_target_pairs={{0,4},{4,0},{1,5},{5,1},{2,6},{6,2},{3,7},{7,3}} | collective-permute-start | bytes 6291464 | tf_op jit(solution)/shard_map/ppermute | solution.py:887
  1020.4 145.2 %collective-permute-start.30 = (f32[4,448,512]{2,1,0:T(8,128)}, f32[4,448,512]{2,1,0:T(8,128)}, u32[]{:S(2)}, u32[]{:S(2)}) collective-permute-start(f32[4,448,512]{2,1,0:T(8,128)} %get-tuple-element.80), channel_id=1, source_target_pairs={{0,1},{1,0},{2,3},{3,2},{4,5},{5,4},{6,7},{7,6}} | collective-permute-start | bytes 11010056 | tf_op jit(solution)/shard_map/ppermute | solution.py:883
  1021.7 88.6 %collective-permute-start.20 = (f32[4,128,896]{2,1,0:T(8,128)}, f32[4,128,896]{2,1,0:T(8,128)S(1)}, u32[]{:S(2)}, u32[]{:S(2)}) collective-permute-start(f32[4,128,896]{2,1,0:T(8,128)} %get-tuple-element.69), channel_id=1, source_target_pairs={{0,3},{1,2},{2,1},{3,0},{4,7},{5,6},{6,5},{7,4}} | collective-permute-start | bytes 5505032 | tf_op jit(solution)/shard_map/ppermute | solution.py:883
  1028.3 147.9 %collective-permute-start.23 = (f32[2,4,128,896]{3,2,1,0:T(8,128)}, f32[2,4,128,896]{3,2,1,0:T(8,128)}, u32[]{:S(2)}, u32[]{:S(2)}) collective-permute-start(f32[2,4,128,896]{3,2,1,0:T(8,128)} %get-tuple-element.71), channel_id=1, source_target_pairs={{0,1},{1,0},{2,3},{3,2},{4,5},{5,4},{6,7},{7,6}} | collective-permute-start | bytes 11010056 | tf_op jit(solution)/shard_map/ppermute | solution.py:883
  1028.3 180.1 %collective-permute-start.29 = (f32[4,448,512]{2,1,0:T(8,128)}, f32[4,448,512]{2,1,0:T(8,128)}, u32[]{:S(2)}, u32[]{:S(2)}) collective-permute-start(f32[4,448,512]{2,1,0:T(8,128)} %get-tuple-element.78), channel_id=1, source_target_pairs={{0,1},{1,0},{2,3},{3,2},{4,5},{5,4},{6,7},{7,6}} | collective-permute-start | bytes 11010056 | tf_op jit(solution)/shard_map/ppermute | solution.py:883
  1029.7 219.9 %all-reduce.22.cloned.1.call-start = ((), (), s32[]{:S(2)}) async-start(), calls=%async_computation.23 | async-start | bytes 1441792 | tf_op jit(solution)/shard_map/psum | solution.py:1028
  1072.1 119.9 %collective-permute-start.21 = (f32[4,128,896]{2,1,0:T(8,128)}, f32[4,128,896]{2,1,0:T(8,128)}, u32[]{:S(2)}, u32[]{:S(2)}) collective-permute-start(f32[4,128,896]{2,1,0:T(8,128)} %collective-permute-done.19.first2), channel_id=1, source_target_pairs={{0,4},{4,0},{1,5},{5,1},{2,6},{6,2},{3,7},{7,3}} | collective-permute-start | bytes 5505032 | tf_op jit(solution)/shard_map/ppermute | solution.py:887
  (170 other events, 3972.1 us)
Sparse Core Ops, SparseCore 0:
  13.3 18.9 all-gather.22
  35.3 19.9 reduce-scatter.8
  63.8 15.1 all-gather.10
  80.9 23.9 all-gather.24
  166.6 25.5 reduce-scatter.10
  207.2 15.7 all-gather.12
  302.3 25.5 reduce-scatter.12
  351.8 27.9 all-gather.14
  531.0 26.1 reduce-scatter.14
  561.1 31.0 all-gather.16
  619.6 28.9 reduce-scatter.16
  668.1 31.0 all-gather.18
  702.3 30.6 reduce-scatter.20
  735.9 36.6 reduce-scatter.18
  811.9 43.5 all-reduce.19
  857.8 30.5 reduce-scatter.22
  1029.8 30.5 all-gather.20
  1221.1 27.3 all-reduce.21

commit v3 on v2

--- a/solution.py
+++ b/solution.py
@@ -71,9 +71,107 @@
     return lax.dot_general(w_r, normed, (((ZERO,), (ONE,)), ((), ())), preferred_element_type=F32)
 
 
-def router_part(residual, gain, w_r, chosen):
-    normed = rms_norm(residual, gain)
-    return normed, combine_weights(router_logits(normed, w_r), chosen)
+def dot_tn(a, b):
+    return dot_nn(a.T.astype(BF16), b)
+
+
+def norm_backward(value, gain, d_out):
+    width = value.shape[ONE]
+    inverse = lax.rsqrt(jnp.mean(value * value, axis=ONE, keepdims=True) + NORM_EPS)
+    unit = value * inverse
+    scaled = d_out * gain
+    along = jnp.sum(scaled * unit, axis=ONE, keepdims=True) / width
+    return inverse * (scaled - unit * along), jnp.sum(d_out * unit, axis=ZERO, keepdims=True)
+
+
+def normalize(value, gain):
+    return value * lax.rsqrt(jnp.mean(value * value, axis=ONE, keepdims=True) + NORM_EPS) * gain
+
+
+def round_trip(value):
+    return value.astype(BF16).astype(F32)
+
+
+def block_backward_kernel(r0_ref, r1_ref, dr_ref, db_ref, whole_ref, gain_ref, cos_ref, sin_ref, chosen_ref, extra_ref, d_ref, grad_ref):
+    tokens, width = r0_ref.shape
+    gain_a = gain_ref[ZERO:ONE, :].astype(F32)
+    gain_m = gain_ref[ONE:TWO, :].astype(F32)
+    r1 = r1_ref[ALL]
+    b = normalize(r1, gain_m)
+    w_r = whole_ref[:, 1280:1408]
+    logits = dot_nn(b.astype(BF16), w_r)
+    lanes = lax.broadcasted_iota(jnp.int32, (tokens, LANES), ONE)
+    first = lanes == chosen_ref[:, ZERO:ONE]
+    second = lanes == chosen_ref[:, ONE:TWO]
+
+    def pick(mask, value):
+        return jnp.sum(jnp.where(mask, value, 0.0), axis=ONE, keepdims=True)
+
+    l0, l1 = pick(first, logits), pick(second, logits)
+    top = jnp.maximum(l0, l1)
+    e0, e1 = jnp.exp(l0 - top), jnp.exp(l1 - top)
+    g0, g1 = e0 / (e0 + e1), e1 / (e0 + e1)
+    d_comb = db_ref[:, width:width + LANES]
+    d0, d1 = pick(first, d_comb), pick(second, d_comb)
+    shared = g0 * d0 + g1 * d1
+    d_logits = (jnp.where(first, g0 * (d0 - shared), 0.0) + jnp.where(second, g1 * (d1 - shared), 0.0)).astype(BF16)
+    d_b = round_trip(round_trip(db_ref[:, ZERO:width]) + round_trip(dot_nt(d_logits, w_r)))
+    d_wr = dot_tn(round_trip(b), d_logits)
+    d_value, d_gain_m = norm_backward(r1, gain_m, d_b)
+    dr = dr_ref[ALL] + d_value
+    r0 = r0_ref[ALL]
+    a = normalize(r0, gain_a)
+    w_qkv = whole_ref[:, ZERO:768]
+    projected = dot_nn(a.astype(BF16), w_qkv)
+    cos, sin = cos_ref[ALL], sin_ref[ALL]
+
+    def turn(value):
+        return value * cos + pltpu.roll(value, 64, ONE) * sin
+
+    def turn_back(value):
+        return value * cos + pltpu.roll(value * sin, 64, ONE)
+
+    keyed = turn(projected[:, WIDTH:640]).astype(BF16)
+    values = projected[:, 640:768].astype(BF16)
+    allowed = lax.broadcasted_iota(jnp.int32, (tokens, tokens), ZERO) >= lax.broadcasted_iota(jnp.int32, (tokens, tokens), ONE)
+    scale = HEAD_DIM ** -0.5
+    dr_low = dr.astype(BF16)
+    d_mixed = dot_nt(dr_low, whole_ref[:, 768:1280]).astype(BF16)
+    d_keyed = jnp.zeros((tokens, LANES), F32)
+    d_values = jnp.zeros((tokens, LANES), F32)
+    d_projected, mixed = [], []
+    for head in range(4):
+        cols = slice(head * LANES, head * LANES + LANES)
+        query = turn(projected[:, cols])
+        scores = jnp.where(allowed, dot_nt(query.astype(BF16), keyed) * scale, -1e30)
+        weight = jnp.exp(scores - jnp.max(scores, axis=ONE, keepdims=True))
+        weight = weight / jnp.sum(weight, axis=ONE, keepdims=True)
+        rounded = round_trip(weight)
+        mixed.append(round_trip(dot_nn(rounded.astype(BF16), values)))
+        d_out = d_mixed[:, cols]
+        d_weight = round_trip(dot_nt(d_out, values))
+        d_values += dot_tn(rounded, d_out)
+        d_scores = weight * (d_weight - jnp.sum(d_weight * weight, axis=ONE, keepdims=True)) * scale
+        d_projected.append(turn_back(round_trip(dot_nn(d_scores.astype(BF16), keyed))))
+        d_keyed += dot_tn(d_scores, query.astype(BF16))
+    d_projected = jnp.concatenate(d_projected + [turn_back(round_trip(d_keyed)), round_trip(d_values)], axis=ONE).astype(BF16)
+    grad_ref[:, ZERO:768] = dot_tn(round_trip(a), d_projected)
+    grad_ref[:, 768:1280] = dot_tn(jnp.concatenate(mixed, axis=ONE), dr_low)
+    d_value, d_gain_a = norm_backward(r0, gain_a, round_trip(dot_nt(d_projected, w_qkv)))
+    d_ref[ALL] = dr + d_value
+    row = lax.broadcasted_iota(jnp.int32, (LANES, width), ZERO)
+    gains = jnp.where(row == 8, d_gain_a, jnp.where(row == 9, d_gain_m, jnp.where(row == 10, extra_ref[ALL], 0.0)))
+    grad_ref[:, 1280:1408] = d_wr + gains.T
+
+
+def block_backward(r0, r1, d_residual, db, whole, gains, cos, sin, chosen, extra):
+    tokens, width = r0.shape
+    return pl.pallas_call(
+        block_backward_kernel,
+        out_shape=[jax.ShapeDtypeStruct((tokens, width), F32), jax.ShapeDtypeStruct((width, 1408), F32)],
+        compiler_params=pltpu.CompilerParams(vmem_limit_bytes=VMEM_LIMIT),
+        cost_estimate=pl.CostEstimate(flops=2_000_000_000, bytes_accessed=8_000_000, transcendentals=300_000),
+    )(r0, r1, d_residual, db, whole, gains, cos, sin, chosen, extra)
 
 
 def dot_nn(a, b):
@@ -649,11 +747,11 @@
 
     @pl.when(pl.program_id(ZERO) == ZERO)
     def _():
-        out_ref[ZERO, ZERO] = w_ref[ZERO, ZERO] - rate[ZERO] * own[ZERO, ZERO]
+        out_ref[ZERO, :, ZERO] = w_ref[ZERO, :, ZERO] - rate[ZERO] * own[ZERO]
 
     @pl.when(pl.program_id(ZERO) == ONE)
     def _():
-        out_ref[ZERO, ZERO] = w_ref[ZERO, ZERO] - rate[ZERO] * p1[ZERO, ZERO]
+        out_ref[ZERO, :, ZERO] = w_ref[ZERO, :, ZERO] - rate[ZERO] * p1[ZERO]
 
 
 def update_far_kernel(sc, rate, w_ref, first2, first3, second2, second3, *rest):
@@ -661,45 +759,48 @@
 
     @pl.when((pl.program_id(ZERO) == ZERO) & (sc[TWO] == sc[4]))
     def _():
-        out_ref[ZERO, ZERO] = w_ref[ZERO, ZERO] - rate[ZERO] * first2[ZERO]
+        out_ref[ZERO, :, ZERO] = w_ref[ZERO, :, ZERO] - rate[ZERO] * first2[ALL]
 
     @pl.when((pl.program_id(ZERO) == ZERO) & (sc[TWO] != sc[4]))
     def _():
-        out_ref[ZERO, ZERO] = w_ref[ZERO, ZERO] - rate[ZERO] * second2[ZERO]
+        out_ref[ZERO, :, ZERO] = w_ref[ZERO, :, ZERO] - rate[ZERO] * second2[ALL]
 
     @pl.when((pl.program_id(ZERO) == ONE) & (sc[TWO] == sc[4]))
     def _():
-        out_ref[ZERO, ZERO] = w_ref[ZERO, ZERO] - rate[ZERO] * first3[ZERO]
+        out_ref[ZERO, :, ZERO] = w_ref[ZERO, :, ZERO] - rate[ZERO] * first3[ALL]
 
     @pl.when((pl.program_id(ZERO) == ONE) & (sc[TWO] != sc[4]))
     def _():
-        out_ref[ZERO, ZERO] = w_ref[ZERO, ZERO] - rate[ZERO] * second3[ZERO]
+        out_ref[ZERO, :, ZERO] = w_ref[ZERO, :, ZERO] - rate[ZERO] * second3[ALL]
 
 
 def update_blocks(kernel, sc, rate, layer, near, w, grads, grad_specs, previous):
+    shape = w.shape
+    paired = (shape[ZERO], 4, TWO) + shape[TWO:]
+
     def whole(s, j, sc):
-        return layer, TWO * j + jnp.where(s == ZERO, sc[ZERO], ONE - sc[ZERO]), ZERO, (sc[ONE] if near else ONE - sc[ONE])
-
-    block = pl.BlockSpec((ONE, ONE, LANES, FF_HALF), whole)
+        return layer, j, jnp.where(s == ZERO, sc[ZERO], ONE - sc[ZERO]), ZERO, (sc[ONE] if near else ONE - sc[ONE])
+
+    block = pl.BlockSpec((ONE, TWO, ONE, LANES, FF_HALF), whole)
     in_specs = [pl.BlockSpec(memory_space=pltpu.SMEM), block] + grad_specs
-    args = [sc, rate, w] + grads
+    args = [sc, rate, w.reshape(paired)] + grads
     aliases = {}
     if previous is not None:
         in_specs.append(pl.BlockSpec(memory_space=pl.ANY))
         aliases = {len(args): ZERO}
-        args.append(previous)
+        args.append(previous.reshape(paired))
     return pl.pallas_call(
         kernel,
-        grid_spec=pltpu.PrefetchScalarGridSpec(num_scalar_prefetch=ONE, grid=(TWO, 4), in_specs=in_specs, out_specs=block),
-        out_shape=jax.ShapeDtypeStruct(w.shape, F32),
+        grid_spec=pltpu.PrefetchScalarGridSpec(num_scalar_prefetch=ONE, grid=(TWO, TWO), in_specs=in_specs, out_specs=block),
+        out_shape=jax.ShapeDtypeStruct(paired, F32),
         input_output_aliases=aliases,
         compiler_params=params(TWO),
         cost_estimate=pl.CostEstimate(flops=2_000_000, bytes_accessed=11_000_000, transcendentals=ZERO),
-    )(*args)
+    )(*args).reshape(shape)
 
 
 def early(s, j):
-    return jnp.where(s == ZERO, j, 3)
+    return jnp.where(s == ZERO, j, ONE)
 
 
 def late(s, j):
@@ -708,8 +809,8 @@
 
 def update_near(sc, rate, layer, matrix, w, own, p1, previous=None):
     specs = [
-        pl.BlockSpec((ONE, ONE, LANES, FF_HALF), lambda s, j, sc: (matrix, early(s, j), ZERO, ZERO)),
-        pl.BlockSpec((ONE, ONE, LANES, FF_HALF), lambda s, j, sc: (matrix, late(s, j), ZERO, ZERO)),
+        pl.BlockSpec((ONE, TWO, LANES, FF_HALF), lambda s, j, sc: (matrix, early(s, j), ZERO, ZERO)),
+        pl.BlockSpec((ONE, TWO, LANES, FF_HALF), lambda s, j, sc: (matrix, late(s, j), ZERO, ZERO)),
     ]
     return update_blocks(update_near_kernel, sc, rate, layer, True, w, [own, p1], specs, previous)
 
@@ -721,7 +822,7 @@
         def index(s, j, sc):
             return jnp.where((sc[TWO] == sc[4]) == by_x, place(s, j), ZERO), ZERO, ZERO
 
-        return pl.BlockSpec((ONE, LANES, FF_HALF), index)
+        return pl.BlockSpec((TWO, LANES, FF_HALF), index)
 
     specs = [spec(early, True), spec(late, True), spec(early, False), spec(late, False)]
     return update_blocks(update_far_kernel, sc, rate, layer, False, w, [rx2, rx3, ry2, ry3], specs, previous)
@@ -733,37 +834,39 @@
 
     @pl.when(s == ZERO)
     def _():
-        out_ref[ZERO, ZERO] = w_ref[ZERO, ZERO] - rate[ZERO] * own[ZERO]
+        out_ref[ZERO, :, ZERO] = w_ref[ZERO, :, ZERO] - rate[ZERO] * own[ALL]
 
     @pl.when(s == ONE)
     def _():
-        out_ref[ZERO, ZERO] = w_ref[ZERO, ZERO] - rate[ZERO] * p1[ZERO]
+        out_ref[ZERO, :, ZERO] = w_ref[ZERO, :, ZERO] - rate[ZERO] * p1[ALL]
 
 
 def update_down(sc, rate, layer, w, own, p1, previous=None):
-    whole = lambda s, j, sc: (layer, TWO * j + jnp.where(s == ZERO, sc[ZERO], ONE - sc[ZERO]), ZERO, ZERO)
+    shape = w.shape
+    paired = (shape[ZERO], 4, TWO) + shape[TWO:]
+    whole = lambda s, j, sc: (layer, j, jnp.where(s == ZERO, sc[ZERO], ONE - sc[ZERO]), ZERO, ZERO)
     in_specs = [
         pl.BlockSpec(memory_space=pltpu.SMEM),
-        pl.BlockSpec((ONE, ONE, 448, WIDTH), whole),
-        pl.BlockSpec((ONE, 448, WIDTH), lambda s, j, sc: (jnp.where(s == ZERO, j, 3), ZERO, ZERO)),
-        pl.BlockSpec((ONE, 448, WIDTH), lambda s, j, sc: (jnp.where(s == ZERO, ZERO, j), ZERO, ZERO)),
+        pl.BlockSpec((ONE, TWO, ONE, 448, WIDTH), whole),
+        pl.BlockSpec((TWO, 448, WIDTH), lambda s, j, sc: (early(s, j), ZERO, ZERO)),
+        pl.BlockSpec((TWO, 448, WIDTH), lambda s, j, sc: (late(s, j), ZERO, ZERO)),
     ]
-    args = [sc, rate, w, own, p1]
+    args = [sc, rate, w.reshape(paired), own, p1]
     aliases = {}
     if previous is not None:
         in_specs.append(pl.BlockSpec(memory_space=pl.ANY))
         aliases = {len(args): ZERO}
-        args.append(previous)
+        args.append(previous.reshape(paired))
     return pl.pallas_call(
         update_down_kernel,
         grid_spec=pltpu.PrefetchScalarGridSpec(
-            num_scalar_prefetch=ONE, grid=(TWO, 4), in_specs=in_specs, out_specs=pl.BlockSpec((ONE, ONE, 448, WIDTH), whole),
+            num_scalar_prefetch=ONE, grid=(TWO, TWO), in_specs=in_specs, out_specs=pl.BlockSpec((ONE, TWO, ONE, 448, WIDTH), whole),
         ),
-        out_shape=jax.ShapeDtypeStruct(w.shape, F32),
+        out_shape=jax.ShapeDtypeStruct(paired, F32),
         input_output_aliases=aliases,
         compiler_params=params(TWO),
         cost_estimate=pl.CostEstimate(flops=4_000_000, bytes_accessed=22_000_000, transcendentals=ZERO),
-    )(*args)
+    )(*args).reshape(shape)
 
 
 def update_head_kernel(sc, rate, w_ref, own, p1, rx2, ry2, rx3, ry3, out_ref):
@@ -815,7 +918,7 @@
 
 def update_embedding(sc, rate, ids, d_rows, w):
     rows, width = w.shape
-    step = 400
+    step = 800
     tokens = d_rows.shape[ZERO]
     return pl.pallas_call(
         update_embedding_kernel,
@@ -906,6 +1009,9 @@
         tokens = 8 * length
         cos_tab, sin_tab = rope_tables(tok_pos[ZERO])
 
+        cos_wide = jnp.concatenate([cos_tab[:, ZERO]] * TWO, axis=ONE)
+        sin_wide = jnp.concatenate([-sin_tab[:, ZERO], sin_tab[:, ZERO]], axis=ONE)
+
         packed = jnp.concatenate([tok_ids, tok_labels, expert_idx[ZERO, ZERO].T, expert_idx[ONE, ZERO].T, tok_ids, tok_labels], axis=ZERO)
         packed = exchange(packed, True, ZERO)
         all_ids, all_labels = packed[:, ZERO].reshape(-ONE), packed[:, ONE].reshape(-ONE, ONE)
@@ -942,7 +1048,8 @@
             return [own, near(p1), *relay(mine2, TWO), *relay(mine3, 3)]
 
         final_col = jnp.stack([g_final, jnp.zeros_like(g_final)])[:, :, None]
-        small = jnp.concatenate([w_query, w_key, w_value, w_attn_out, w_router, g_attn[:, :, None], g_mlp[:, :, None], final_col], axis=TWO)
+        unused = jnp.zeros(g_attn.shape + (1408 - 1291,), F32)
+        small = jnp.concatenate([w_query, w_key, w_value, w_attn_out, w_router, g_attn[:, :, None], g_mlp[:, :, None], final_col, unused], axis=TWO)
         whole = []
         for layer in range(layers):
             whole.append(lax.all_gather(small[layer].astype(BF16), FSDP, axis=ZERO, tiled=True))
@@ -966,19 +1073,17 @@
         saved = []
         for layer in range(layers):
             w_r, gain_m = small_param(layer, 4), small_param(layer, 6)
-            residual, attn_vjp = jax.vjp(functools.partial(attention_part, cos_tab=cos_tab, sin_tab=sin_tab), residual, *attention_params(layer))
-
-            def routed(*values, layer=layer):
-                return router_part(*values, chosen=expert_idx[layer, ZERO].T)
-
-            (b, _), router_vjp = jax.vjp(routed, residual, gain_m, w_r)
+            before_attention = residual
+            residual = row_major(attention_part(residual, *attention_params(layer), cos_tab=cos_tab, sin_tab=sin_tab))
+            after_attention = residual
+            b = rms_norm(residual, gain_m)
             b_group = lax.all_gather(row_major(b), FSDP, axis=ZERO, tiled=True)
             b_other = to_replica(b_group)
             comb = combine_weights(router_logits(b_group, w_r), own_group(chosen_all[layer], ONE))
             pieces, wd1 = sent[layer]
             partial = expert_forward(sc, layer, b_group, comb.T, w_gate, w_up, pieces, w_down, wd1)
             residual = row_major(residual + lax.psum_scatter(partial, FSDP, scatter_dimension=ZERO, tiled=True))
-            saved.append((attn_vjp, router_vjp, b_group, b_other, comb, w_r))
+            saved.append((before_attention, after_attention, b_group, b_other, comb, w_r))
 
         others, residual = lax.optimization_barrier(([entry[3] for entry in saved], residual))
         comb_others = []
@@ -1001,7 +1106,7 @@
         small_grads = [None] * layers
         new_gate = new_up = new_down = None
         for layer in reversed(range(layers)):
-            attn_vjp, router_vjp, b_group, _, comb, _ = saved[layer]
+            before_attention, after_attention, b_group, _, comb, _ = saved[layer]
             d_all = lax.all_gather(row_major(d_residual), (REP, FSDP), axis=ZERO, tiled=True)
             pieces, wd1 = sent[layer]
             scalars, ranks, rank_cols = routes[layer]
@@ -1016,21 +1121,15 @@
             new_up = update_far(place, rate, layer, ONE, w_up, *returned, new_up)
             new_down = update_down(sc, rate, layer, w_down, down_own, down1, previous=new_down)
             db = row_major(lax.psum_scatter(db, FSDP, scatter_dimension=ZERO, tiled=True))
-            d_router_in, d_gain_m, d_wr = router_vjp((db[:, :WIDTH].astype(BF16), db[:, WIDTH:520].T))
-            d_residual = d_residual + d_router_in
-            d_residual, d_wqkv, d_wo, d_gain_a = attn_vjp(d_residual)
-            extra = d_gain_final if layer == ZERO else jnp.full_like(d_gain_final, ZERO, F32) + jnp.sum(picked)
-            grads = [d_wqkv, d_wo, d_wr, d_gain_a[:, None], d_gain_m[:, None], extra[:, None]]
-            grads = jnp.concatenate([g.astype(F32) for g in grads], axis=ONE)
-            if layer + ONE < layers:
-                grads, small_grads[layer + ONE] = lax.optimization_barrier((grads, small_grads[layer + ONE]))
-            grads = lax.psum_scatter(grads, FSDP, scatter_dimension=ZERO, tiled=True)
-            small_grads[layer] = lax.psum(grads, REP)
+            extra = d_gain_final.astype(F32)[None, :] if layer == ZERO else jnp.full((ONE, d_gain_final.shape[ZERO]), jnp.sum(picked), F32)
+            gains = whole[layer][:, cuts[5]:cuts[7]].T
+            d_residual, grads = block_backward(before_attention, after_attention, d_residual, db, whole[layer], gains, cos_wide, sin_wide, expert_idx[layer, ZERO], extra)
+            small_grads[layer] = lax.psum_scatter(grads, FSDP, scatter_dimension=ZERO, tiled=True)
 
         d_rows = lax.all_gather(row_major(d_residual.astype(BF16)), (REP, FSDP), axis=ZERO, tiled=True)
         new_embedding = update_embedding(sc, rate, all_ids[None, :], d_rows, embedding)
 
-        small_grad = jnp.stack(small_grads)
+        small_grad = lax.psum(jnp.stack(small_grads), REP)
         new_small = small - learn_rate * small_grad
         mean_loss = (jnp.sum(lse) - small_grad[ONE, ZERO, 1290] / TWO) / tokens
 

time: 1280 us -> 1260 us (0.984)
  waiting for transfers between devices: 597 us -> 622 us
  matrix products: 43.1 us -> 19.2 us
    all_gather x2, waiting for transfers between devices: 0.04 us -> 17.3 us  [train_step(): lax.all_gather(small[layer].astype(BF16), FSDP, axis=ZERO, tiled=True)]
    pallas_call x0 -> x2, Pallas kernels: none -> 16.9 us  [block_backward(): pl.pallas_call(block_backward_kernel, out_shape=[jax.ShapeDtypeStruct((to...]
    pallas_call x8, Pallas kernels: 64.4 us -> 50.6 us  [update_blocks(): pl.pallas_call(kernel, grid_spec=pltpu.PrefetchScalarGridSpec(num_scalar_...]
  transfers between devices with their start and end apart: 54 -> 53, of which waited for: 25 -> 25; matrix products, arithmetic and copies ran while one was open for 7% -> 5% of each run, Pallas kernels for 26% -> 22%
where the time goes in v3:
time: 1260 us; the launch traced here: 1250 us
  waiting for transfers between devices  622 us (49%)
  Pallas kernels  458 us (36%)
  local copies, waits for them, and re-layouts  67.9 us (5%)
  starting transfers between devices  37.3 us (3%)
  other arithmetic  30.5 us (2%)
  matrix products  19.2 us (2%)
  between operations  18.7 us (1%)
    ppermute x22, waiting for transfers between devices, to_peer(): return lax.ppermute(value, FSDP, [(i, i ^ k) for i in range(4)])  339 us
    pallas_call x2, Pallas kernels, expert_wgrad(): pl.pallas_call(expert_wgrad_kernel, grid_spec=pltpu.PrefetchScalarGridSpe...  84.9 us
    ppermute x14, waiting for transfers between devices, to_replica(): return lax.ppermute(value, REP, [(ZERO, ONE), (ONE, ZERO)])  76.3 us
    pallas_call x2, Pallas kernels, expert_dgrad(): pl.pallas_call(expert_dgrad_kernel, grid_spec=pltpu.PrefetchScalarGridSpe...  57.7 us
    all_gather x2, waiting for transfers between devices, train_step(): lax.all_gather(row_major(d_residual), (REP, FSDP), axis=ZERO, tiled=True)  56.2 us
    pallas_call x8, Pallas kernels, update_blocks(): pl.pallas_call(kernel, grid_spec=pltpu.PrefetchScalarGridSpec(num_scalar_...  50.6 us
    pallas_call x1, Pallas kernels, head_dx(): pl.pallas_call(head_dx_kernel, grid_spec=pltpu.PrefetchScalarGridSpec(num...  46.7 us
    reduce_scatter x2, waiting for transfers between devices, train_step(): lax.psum_scatter(partial, FSDP, scatter_dimension=ZERO, tiled=True)  46.7 us
  transfers between devices with their start and end apart: 53, of which 25 were waited for; matrix products, arithmetic and copies ran while one was open for 5% of the time, Pallas kernels for 22%

profile of v3, /device:TPU:0, one launch (start us, length us, event | category | flops | bytes accessed | tf_op | source)
XLA Modules:
  0.0 1253.2 jit_solution(10227082721291419230)
XLA Ops:
  98.4 20.7 %collective-permute-done.1.rx2 = bf16[4,128,896]{2,1,0:T(8,128)(2,1)S(1)} collective-permute-done((bf16[4,128,896]{2,1,0:T(8,128)(2,1)}, bf16[4,128,896]{2,1,0:T(8,128)(2,1)S(1)}, u32[]{:S(2)}, u32[]{:S(2)}) %collective-permute-start.1) | collective-permute-done | bytes 917536 | tf_op jit(solution)/shard_map/ppermute | solution.py:986
  183.4 24.1 %reduce-scatter.11.cloned.1.call-done = f32[256,512]{1,0:T(8,128)} async-done(((f32[1024,512]{1,0:T(8,128)}), f32[256,512]{1,0:T(8,128)}) %reduce-scatter.11.cloned.1.call-update) | async-done | bytes 524304 | tf_op jit(solution)/shard_map/reduce_scatter | solution.py:1085
  228.0 22.6 %collective-permute-done.9.rx2 = bf16[4,128,896]{2,1,0:T(8,128)(2,1)} collective-permute-done((bf16[4,128,896]{2,1,0:T(8,128)(2,1)}, bf16[4,128,896]{2,1,0:T(8,128)(2,1)}, u32[]{:S(2)}, u32[]{:S(2)}) %collective-permute-start.9) | collective-permute-done | bytes 917536 | tf_op jit(solution)/shard_map/ppermute | solution.py:986
  316.1 22.6 %reduce-scatter.13.cloned.1.call-done = f32[256,512]{1,0:T(8,128)} async-done(((f32[1024,512]{1,0:T(8,128)}), f32[256,512]{1,0:T(8,128)}) %reduce-scatter.13.cloned.1.call-update) | async-done | bytes 524304 | tf_op jit(solution)/shard_map/reduce_scatter | solution.py:1085
  340.2 21.1 %collective-permute-done.7.b_other = bf16[1024,512]{1,0:T(8,128)(2,1)} collective-permute-done((bf16[1024,512]{1,0:T(8,128)(2,1)S(1)}, bf16[1024,512]{1,0:T(8,128)(2,1)}, u32[]{:S(2)}, u32[]{:S(2)}) %collective-permute-start.7) | collective-permute-done | bytes 1048608 | tf_op jit(solution)/shard_map/ppermute | solution.py:990
  376.0 29.8 %collective-permute-done.15.rx2 = bf16[64,8192]{1,0:T(8,128)(2,1)} collective-permute-done((bf16[64,8192]{1,0:T(8,128)(2,1)}, bf16[64,8192]{1,0:T(8,128)(2,1)}, u32[]{:S(2)}, u32[]{:S(2)}) %collective-permute-start.15) | collective-permute-done | bytes 1048608 | tf_op jit(solution)/shard_map/ppermute | solution.py:986
  450.5 30.8 %shard_map.286 = f32[2048,8]{1,0:T(8,128)} custom-call(s32[20]{0:T(128)} %concatenate.53.sc, bf16[2048,512]{1,0:T(8,128)(2,1)} %copy.166.x_ref, bf16[128,8192]{1,0:T(8,128)(2,1)} %get-tuple-element.61.own, bf16[128,8192]{1,0:T(8,128)(2,1)} %copy-done.51, bf16[64,8192]{1,0:T(8,128)(2,1)} %collective-permute-done.15.rx2, ...), custom_call_target="tpu_custom_call" | custom-call | flops 16999999488 | bytes 25000000 | tf_op jit(solution)/shard_map/pallas_call | solution.py:616
  494.9 46.7 %shard_map.287 = (bf16[2048,8192]{1,0:T(8,128)(2,1)}, f32[1024,512]{1,0:T(8,128)}, f32[8,128]{1,0:T(8,128)}) custom-call(s32[20]{0:T(128)} %concatenate.53.sc, bf16[2048,512]{1,0:T(8,128)(2,1)} %copy.166.x_ref, s32[2048,1]{1,0:T(8,128)} %copy.167.label_ref, f32[2048,1]{1,0:T(8,128)} %copy.168.lse_ref, bf16[128,8192]{1,0:T(8,128)(2,1)} %get-tuple-element.61.own, ...), custom_call_target="tpu_custom_call" | custom-call | flops 25999998976 | bytes 60000000 | tf_op jit(solution)/shard_map/pallas_call | solution.py:687
  541.7 26.2 %reduce-scatter.15.cloned.1.call-done = f32[256,512]{1,0:T(8,128)} async-done(((f32[1024,512]{1,0:T(8,128)}), f32[256,512]{1,0:T(8,128)}) %reduce-scatter.15.cloned.1.call-update) | async-done | bytes 524304 | tf_op jit(solution)/shard_map/reduce_scatter | solution.py:1101
  575.1 27.2 %all-gather.17.cloned.1.call-done.d_ref.d_own.d_other = f32[2048,512]{1,0:T(8,128)} async-done(((f32[256,512]{1,0:T(8,128)}), f32[2048,512]{1,0:T(8,128)}) %all-gather.17.cloned.1.call-update) | async-done | bytes 4194320 | tf_op jit(solution)/shard_map/all_gather | solution.py:1110
  602.3 27.2 %shard_map.288 = f32[1024,640]{1,0:T(8,128)} custom-call(s32[20]{0:T(128)} %concatenate.59.sc, bf16[1024,512]{1,0:T(8,128)(2,1)} %all-gather.13.cloned.1.call-done.b_ref.b_own, f32[2048,512]{1,0:T(8,128)} %all-gather.17.cloned.1.call-done.d_ref.d_own.d_other, s32[2,8,1024]{2,1,0:T(8,128)} %get-tuple-element.204.rank_ref, s32[2,1024,8]{2,1,0:T(8,128)} %copy.169.rank_col_ref, ...), custom_call_target="tpu_custom_call" | custom-call | flops 15000000512 | bytes 25000000 | tf_op jit(solution)/shard_map/pallas_call | solution.py:429
  634.0 24.7 %reduce-scatter.17.cloned.1.call-done.db_ref = f32[256,640]{1,0:T(8,128)} async-done(((f32[1024,640]{1,0:T(8,128)}), f32[256,640]{1,0:T(8,128)}) %reduce-scatter.17.cloned.1.call-update) | async-done | bytes 655376 | tf_op jit(solution)/shard_map/reduce_scatter | solution.py:1123
  670.6 28.9 %all-gather.19.cloned.1.call-done.d_ref.d_own.d_other = f32[2048,512]{1,0:T(8,128)} async-done(((f32[256,512]{1,0:T(8,128)}), f32[2048,512]{1,0:T(8,128)}) %all-gather.19.cloned.1.call-update) | async-done | bytes 4194320 | tf_op jit(solution)/shard_map/all_gather | solution.py:1110
  699.6 30.5 %shard_map.290 = f32[1024,640]{1,0:T(8,128)} custom-call(s32[20]{0:T(128)} %concatenate.53.sc, bf16[1024,512]{1,0:T(8,128)(2,1)} %all-gather.11.cloned.1.call-done.b_ref.b_own, f32[2048,512]{1,0:T(8,128)} %all-gather.19.cloned.1.call-done.d_ref.d_own.d_other, s32[2,8,1024]{2,1,0:T(8,128)} %get-tuple-element.202.rank_ref, s32[2,1024,8]{2,1,0:T(8,128)} %copy.171.rank_col_ref, ...), custom_call_target="tpu_custom_call" | custom-call | flops 15000000512 | bytes 25000000 | tf_op jit(solution)/shard_map/pallas_call | solution.py:429
  733.7 27.0 %shard_map.305 = (f32[128,8192]{1,0:T(8,128)}, f32[128,8192]{1,0:T(8,128)}, f32[64,8192]{1,0:T(8,128)}, f32[64,8192]{1,0:T(8,128)}) custom-call(s32[20]{0:T(128)} %concatenate.53.sc, bf16[512,2048]{1,0:T(8,128)(2,1)} %bitcast.202, bf16[2048,8192]{1,0:T(8,128)(2,1)} %get-tuple-element.85.dl_ref), custom_call_target="tpu_custom_call" | custom-call | flops 12999999488 | bytes 52000000 | tf_op jit(solution)/shard_map/pallas_call | solution.py:727
  768.3 56.7 %collective-permute-done.32.rx2 = f32[64,8192]{1,0:T(8,128)} collective-permute-done((f32[64,8192]{1,0:T(8,128)}, f32[64,8192]{1,0:T(8,128)}, u32[]{:S(2)}, u32[]{:S(2)}) %collective-permute-start.32) | collective-permute-done | bytes 2097184 | tf_op jit(solution)/shard_map/ppermute | solution.py:986
  825.0 36.6 %collective-permute-done.34.rx3 = f32[64,8192]{1,0:T(8,128)} collective-permute-done((f32[64,8192]{1,0:T(8,128)}, f32[64,8192]{1,0:T(8,128)}, u32[]{:S(2)}, u32[]{:S(2)}) %collective-permute-start.34) | collective-permute-done | bytes 2097184 | tf_op jit(solution)/shard_map/ppermute | solution.py:986
  879.5 41.9 %shard_map.294 = (f32[2,4,128,896]{3,2,1,0:T(8,128)}, f32[2,4,128,896]{3,2,1,0:T(8,128)}, f32[4,128,896]{2,1,0:T(8,128)}, f32[4,128,896]{2,1,0:T(8,128)}, f32[4,...) custom-call(s32[20]{0:T(128)} %concatenate.59.sc, bf16[1024,512]{1,0:T(8,128)(2,1)} %all-gather.13.cloned.1.call-done.b_ref.b_own, ...), custom_call_target="tpu_custom_call" | custom-call | flops 30000001024 | bytes 50000000 | tf_op jit(solution)/shard_map/pallas_call | solution.py:510
  926.5 38.1 %collective-permute-done.24.first2 = f32[4,128,896]{2,1,0:T(8,128)S(1)} collective-permute-done((f32[4,128,896]{2,1,0:T(8,128)}, f32[4,128,896]{2,1,0:T(8,128)S(1)}, u32[]{:S(2)}, u32[]{:S(2)}) %collective-permute-start.24) | collective-permute-done | bytes 1835040 | tf_op jit(solution)/shard_map/ppermute | solution.py:986
  964.6 43.0 %shard_map.293 = (f32[2,4,128,896]{3,2,1,0:T(8,128)}, f32[2,4,128,896]{3,2,1,0:T(8,128)}, f32[4,128,896]{2,1,0:T(8,128)}, f32[4,128,896]{2,1,0:T(8,128)}, f32[4,...) custom-call(s32[20]{0:T(128)} %concatenate.53.sc, bf16[1024,512]{1,0:T(8,128)(2,1)} %all-gather.11.cloned.1.call-done.b_ref.b_own, ...), custom_call_target="tpu_custom_call" | custom-call | flops 30000001024 | bytes 50000000 | tf_op jit(solution)/shard_map/pallas_call | solution.py:510
  1012.7 47.1 %collective-permute-done.19.first2 = f32[4,128,896]{2,1,0:T(8,128)} collective-permute-done((f32[4,128,896]{2,1,0:T(8,128)}, f32[4,128,896]{2,1,0:T(8,128)}, u32[]{:S(2)}, u32[]{:S(2)}) %collective-permute-start.19) | collective-permute-done | bytes 1835040 | tf_op jit(solution)/shard_map/ppermute | solution.py:986
  1061.8 35.4 %collective-permute-done.20.first3 = f32[4,128,896]{2,1,0:T(8,128)} collective-permute-done((f32[4,128,896]{2,1,0:T(8,128)}, f32[4,128,896]{2,1,0:T(8,128)}, u32[]{:S(2)}, u32[]{:S(2)}) %collective-permute-start.20) | collective-permute-done | bytes 1835040 | tf_op jit(solution)/shard_map/ppermute | solution.py:986
  1101.1 19.8 %shard_map.306 = f32[128,32000]{1,0:T(8,128)} custom-call(s32[20]{0:T(128)} %concatenate.53.sc, f32[1]{0:T(128)} %bitcast.172.rate, f32[128,32000]{1,0:T(8,128)} %w_ref.5, f32[128,8192]{1,0:T(8,128)} %get-tuple-element.86.own, f32[128,8192]{1,0:T(8,128)} %collective-permute-done.31.p1, f32[64,8192]{1,0:T(8,128)} %collective-permute-done.32.rx2, ...), custom_call_target="tpu_custom_call" | custom-call | flops 8000000 | bytes 50000000 | tf_op jit(solution)/shard_map/pallas_call | solution.py:892
  1193.5 23.9 %shard_map.292 = f32[8000,512]{1,0:T(8,128)} custom-call(s32[20]{0:T(128)} %concatenate.53.sc, f32[1]{0:T(128)} %bitcast.161.rate, s32[1,2048]{1,0:T(1,128)} %bitcast.265, bf16[2048,512]{1,0:T(8,128)(2,1)} %all-gather.21.cloned.1.call-done.d_ref, f32[8000,512]{1,0:T(8,128)} %w_ref.4), custom_call_target="tpu_custom_call" | custom-call | flops 16999999488 | bytes 35000000 | tf_op jit(solution)/shard_map/pallas_call | solution.py:923
  (372 shorter events, 481.8 us)
Async XLA Ops:
  34.4 105.6 %all-gather.11.cloned.1.call-start = ((), (), s32[]{:S(2)}) async-start(), calls=%async_computation.9 | async-start | bytes 1310720 | tf_op jit(solution)/shard_map/all_gather | solution.py:1080
  79.0 103.0 %all-gather.25.cloned.1.call-start = ((), (), s32[]{:S(2)}) async-start(), calls=%async_computation.24 | async-start | bytes 1802240 | tf_op jit(solution)/shard_map/all_gather | solution.py:1055
  89.8 117.7 %reduce-scatter.11.cloned.1.call-start = ((), (), s32[]{:S(2)}) async-start(), calls=%async_computation.10 | async-start | bytes 2621440 | tf_op jit(solution)/shard_map/reduce_scatter | solution.py:1085
  181.8 89.2 %all-gather.13.cloned.1.call-start = ((), (), s32[]{:S(2)}) async-start(), calls=%async_computation.11 | async-start | bytes 1310720 | tf_op jit(solution)/shard_map/all_gather | solution.py:1080
  217.9 120.8 %reduce-scatter.13.cloned.1.call-start = ((), (), s32[]{:S(2)}) async-start(), calls=%async_computation.12 | async-start | bytes 2621440 | tf_op jit(solution)/shard_map/reduce_scatter | solution.py:1085
  312.9 114.1 %all-gather.15.cloned.1.call-start = ((), (), s32[]{:S(2)}) async-start(), calls=%async_computation.13 | async-start | bytes 2359296 | tf_op jit(solution)/shard_map/all_gather | solution.py:1094
  362.5 205.4 %reduce-scatter.15.cloned.1.call-start = ((), (), s32[]{:S(2)}) async-start(), calls=%async_computation.14 | async-start | bytes 2621440 | tf_op jit(solution)/shard_map/reduce_scatter | solution.py:1101
  571.1 87.5 %reduce-scatter.17.cloned.1.call-start = ((), (), s32[]{:S(2)}) async-start(), calls=%async_computation.16 | async-start | bytes 3276800 | tf_op jit(solution)/shard_map/reduce_scatter | solution.py:1123
  668.4 198.9 %reduce-scatter.19.cloned.1.call-start = ((), (), s32[]{:S(2)}) async-start(), calls=%async_computation.18 | async-start | bytes 3276800 | tf_op jit(solution)/shard_map/reduce_scatter | solution.py:1123
  730.1 460.8 %reduce-scatter.23.cloned.1.call-start = ((), (), s32[]{:S(2)}) async-start(), calls=%async_computation.21 | async-start | bytes 3604480 | tf_op jit(solution)/shard_map/reduce_scatter | solution.py:1127
  733.6 457.3 %reduce-scatter.21.cloned.1.call-start = ((), (), s32[]{:S(2)}) async-start(), calls=%async_computation.20 | async-start | bytes 3604480 | tf_op jit(solution)/shard_map/reduce_scatter | solution.py:1127
  762.8 98.9 %collective-permute-start.34 = (f32[64,8192]{1,0:T(8,128)}, f32[64,8192]{1,0:T(8,128)}, u32[]{:S(2)}, u32[]{:S(2)}) collective-permute-start(f32[64,8192]{1,0:T(8,128)} %get-tuple-element.89), channel_id=1, source_target_pairs={{0,3},{1,2},{2,1},{3,0},{4,7},{5,6},{6,5},{7,4}} | collective-permute-start | bytes 6291464 | tf_op jit(solution)/shard_map/ppermute | solution.py:986
  825.0 97.2 %collective-permute-start.33 = (f32[64,8192]{1,0:T(8,128)}, f32[64,8192]{1,0:T(8,128)}, u32[]{:S(2)}, u32[]{:S(2)}) collective-permute-start(f32[64,8192]{1,0:T(8,128)} %collective-permute-done.32.rx2), channel_id=1, source_target_pairs={{0,4},{4,0},{1,5},{5,1},{2,6},{6,2},{3,7},{7,3}} | collective-permute-start | bytes 6291464 | tf_op jit(solution)/shard_map/ppermute | solution.py:990
  879.2 314.2 %all-gather.21.cloned.1.call-start = ((), (), s32[]{:S(2)}) async-start(), calls=%async_computation.19 | async-start | bytes 2359296 | tf_op jit(solution)/shard_map/all_gather | solution.py:1129
  921.7 85.9 %collective-permute-start.31 = (f32[128,8192]{1,0:T(8,128)}, f32[128,8192]{1,0:T(8,128)}, u32[]{:S(2)}, u32[]{:S(2)}) collective-permute-start(f32[128,8192]{1,0:T(8,128)} %get-tuple-element.87), channel_id=1, source_target_pairs={{0,1},{1,0},{2,3},{3,2},{4,5},{5,4},{6,7},{7,6}} | collective-permute-start | bytes 12582920 | tf_op jit(solution)/shard_map/ppermute | solution.py:986
  922.0 86.2 %collective-permute-start.28 = (f32[2,4,128,896]{3,2,1,0:T(8,128)}, f32[2,4,128,896]{3,2,1,0:T(8,128)}, u32[]{:S(2)}, u32[]{:S(2)}) collective-permute-start(f32[2,4,128,896]{3,2,1,0:T(8,128)} %get-tuple-element.80), channel_id=1, source_target_pairs={{0,1},{1,0},{2,3},{3,2},{4,5},{5,4},{6,7},{7,6}} | collective-permute-start | bytes 11010056 | tf_op jit(solution)/shard_map/ppermute | solution.py:986
  922.2 86.1 %collective-permute-start.30 = (f32[4,448,512]{2,1,0:T(8,128)}, f32[4,448,512]{2,1,0:T(8,128)}, u32[]{:S(2)}, u32[]{:S(2)}) collective-permute-start(f32[4,448,512]{2,1,0:T(8,128)} %get-tuple-element.84), channel_id=1, source_target_pairs={{0,1},{1,0},{2,3},{3,2},{4,5},{5,4},{6,7},{7,6}} | collective-permute-start | bytes 11010056 | tf_op jit(solution)/shard_map/ppermute | solution.py:986
  924.8 82.8 %collective-permute-start.25 = (f32[4,128,896]{2,1,0:T(8,128)}, f32[4,128,896]{2,1,0:T(8,128)}, u32[]{:S(2)}, u32[]{:S(2)}) collective-permute-start(f32[4,128,896]{2,1,0:T(8,128)} %get-tuple-element.78), channel_id=1, source_target_pairs={{0,3},{1,2},{2,1},{3,0},{4,7},{5,6},{6,5},{7,4}} | collective-permute-start | bytes 5505032 | tf_op jit(solution)/shard_map/ppermute | solution.py:986
  1007.6 147.8 %collective-permute-start.23 = (f32[2,4,128,896]{3,2,1,0:T(8,128)}, f32[2,4,128,896]{3,2,1,0:T(8,128)}, u32[]{:S(2)}, u32[]{:S(2)}) collective-permute-start(f32[2,4,128,896]{3,2,1,0:T(8,128)} %get-tuple-element.75), channel_id=1, source_target_pairs={{0,1},{1,0},{2,3},{3,2},{4,5},{5,4},{6,7},{7,6}} | collective-permute-start | bytes 11010056 | tf_op jit(solution)/shard_map/ppermute | solution.py:986
  1007.6 159.8 %collective-permute-start.29 = (f32[4,448,512]{2,1,0:T(8,128)}, f32[4,448,512]{2,1,0:T(8,128)}, u32[]{:S(2)}, u32[]{:S(2)}) collective-permute-start(f32[4,448,512]{2,1,0:T(8,128)} %get-tuple-element.82), channel_id=1, source_target_pairs={{0,1},{1,0},{2,3},{3,2},{4,5},{5,4},{6,7},{7,6}} | collective-permute-start | bytes 11010056 | tf_op jit(solution)/shard_map/ppermute | solution.py:986
  1008.3 88.9 %collective-permute-start.20 = (f32[4,128,896]{2,1,0:T(8,128)}, f32[4,128,896]{2,1,0:T(8,128)}, u32[]{:S(2)}, u32[]{:S(2)}) collective-permute-start(f32[4,128,896]{2,1,0:T(8,128)} %get-tuple-element.73), channel_id=1, source_target_pairs={{0,3},{1,2},{2,1},{3,0},{4,7},{5,6},{6,5},{7,4}} | collective-permute-start | bytes 5505032 | tf_op jit(solution)/shard_map/ppermute | solution.py:986
  1010.3 225.5 %all-reduce.3.cloned.1.call-start = ((), (), s32[]{:S(2)}) async-start(), calls=%async_computation.22 | async-start | bytes 2883584 | tf_op jit(solution)/shard_map/psum | solution.py:1132
  1010.6 131.5 %collective-permute-start.27 = (f32[4,128,896]{2,1,0:T(8,128)}, f32[4,128,896]{2,1,0:T(8,128)}, u32[]{:S(2)}, u32[]{:S(2)}) collective-permute-start(f32[4,128,896]{2,1,0:T(8,128)} %collective-permute-done.25.first3), channel_id=1, source_target_pairs={{0,4},{4,0},{1,5},{5,1},{2,6},{6,2},{3,7},{7,3}} | collective-permute-start | bytes 5505032 | tf_op jit(solution)/shard_map/ppermute | solution.py:990
  1059.7 116.7 %collective-permute-start.21 = (f32[4,128,896]{2,1,0:T(8,128)}, f32[4,128,896]{2,1,0:T(8,128)S(1)}, u32[]{:S(2)}, u32[]{:S(2)}) collective-permute-start(f32[4,128,896]{2,1,0:T(8,128)} %collective-permute-done.19.first2), channel_id=1, source_target_pairs={{0,4},{4,0},{1,5},{5,1},{2,6},{6,2},{3,7},{7,3}} | collective-permute-start | bytes 5505032 | tf_op jit(solution)/shard_map/ppermute | solution.py:990
  (81 other events, 2337.7 us)
Sparse Core Ops, SparseCore 0:
  32.0 20.1 reduce-scatter.8
  54.3 16.2 all-gather.22
  79.1 14.8 all-gather.10
  96.0 24.1 all-gather.24
  181.9 25.5 reduce-scatter.10
  218.0 15.8 all-gather.12
  313.0 25.5 reduce-scatter.12
  362.6 27.9 all-gather.14
  541.7 26.0 reduce-scatter.14
  571.2 31.0 all-gather.16
  629.7 28.9 reduce-scatter.16
  668.5 31.0 all-gather.18
  730.2 29.4 reduce-scatter.18
  762.1 45.5 reduce-scatter.22
  879.3 29.9 reduce-scatter.20
  1010.4 31.7 all-gather.20
  1193.6 42.1 all-reduce.2
